TPU v7x, 128 devices: a whole 4x4x4 slice. The times are simulated.
128 devices in a mesh: gx: 8 (over z, y_hi), gy: 16 (over x, y_lo, core).
Axes of the slice: x: 4, y: 4 (y_hi: 2, y_lo: 2; y = y_hi * 2 + y_lo), z: 4, core: 2. Of those that a mesh axis runs over, the one named last changes fastest.
Arguments:
- node_coords: float32 [49152, 3, 128], P(('gx', 'gy')), may hold values from -6 to 6
- node_disp: float32 [49152, 3, 128], P(('gx', 'gy')), may hold values from -6 to 6
- qpoints: float32 [32768, 3, 256], P(('gx', 'gy')), may hold values from -6 to 6
- qweights: float32 [32768, 256], P(('gx', 'gy')), may hold values from 0.1 to 2
- qcount: int32 [32768], P(('gx', 'gy')), may hold values from 64 to 256
- sec_block: int32 [32768], P(('gx', 'gy')), may hold values from 0 to 49151, as said below
- pri_block: int32 [32768], P(('gx', 'gy')), may hold values from 0 to 49151, as said below
Outputs:
- gap: float32 [49152, 3, 128], P(('gx', 'gy'))
Inputs may be any that keep to these rules, and one draw needn't show every extreme that they name: `sec_block`: patch b is owned by device b // 384. Among the segments of one device, at most 4 have their secondary patch owned by any one device; in every draw some device owns the secondary patches of exactly 4 segments of every device. `pri_block`: as for sec_block, with primary patches: at most 4 segments of one device name patches of any one owner, and some owner gets exactly 4 from every device.
All inputs are finite; a program needn't handle non-finite values.
Results may differ from a plain program's by a relative error of at most 0.000098.
Values sent between devices are 32-bit elements; how exact they have to be, the bound alone decides.
No kernel may reach another device: no remote copies, remote signals or barrier semaphores. Data moves between devices by JAX's collectives and lax.ppermute only.
A program may use at most 64 MiB of HBM per device.

v0:
```python
import jax
import jax.numpy as jnp
from jax import lax
from jax.sharding import PartitionSpec as P


def shape_values(points, coords):
    diff0 = points[:, 0, :, None] - coords[:, 0, None, :]
    diff1 = points[:, 1, :, None] - coords[:, 1, None, :]
    diff2 = points[:, 2, :, None] - coords[:, 2, None, :]
    radius = diff0 * diff0 + diff1 * diff1 + diff2 * diff2
    kernel = 1.0 / (1.0 + 2.0 * radius)
    return kernel / jnp.sum(kernel, axis=-1, keepdims=True)


def routing(block_ids, blocks_dev, capacity, slot_count):
    owners = block_ids // blocks_dev
    local_ids = block_ids % blocks_dev
    positions = jnp.arange(block_ids.shape[0], dtype=jnp.int32)
    same_owner = (owners[:, None] == owners[None, :]) & (positions[:, None] > positions[None, :])
    ranks = jnp.sum(same_owner.astype(jnp.int32), axis=1)
    slot_ids = owners * capacity + ranks
    matches = slot_ids[:, None] == jnp.arange(slot_count, dtype=jnp.int32)[None, :]
    request = jnp.sum(jnp.where(matches, local_ids[:, None], 0), axis=0)
    return (slot_ids, matches, request)


def body(node_coords, node_disp, qpoints, qweights, qcount, sec_block, pri_block):
    grid_x = lax.axis_size("gx")
    grid_y = lax.axis_size("gy")
    devices = grid_x * grid_y
    blocks_dev = node_coords.shape[0]
    node_count = node_coords.shape[2]
    seg_count = qpoints.shape[0]
    quad_points = qpoints.shape[2]
    slot_count = 2 * seg_count
    capacity = slot_count // devices
    hp = lax.Precision.HIGHEST
    sec_slots, sec_matches, sec_request = routing(sec_block, blocks_dev, capacity, slot_count)
    pri_slots, pri_matches, pri_request = routing(pri_block, blocks_dev, capacity, slot_count)
    requests = jnp.stack([sec_request, pri_request], axis=-1)
    received = lax.all_to_all(
        requests.reshape(devices, capacity, 2),
        ("gx", "gy"),
        split_axis=0,
        concat_axis=0,
        tiled=True,
    )
    received = received.reshape(slot_count, 2)
    node_data = jnp.concatenate([node_coords, node_disp], axis=1)
    outgoing = jnp.stack(
        [jnp.take(node_data, received[:, 0], axis=0), jnp.take(node_data, received[:, 1], axis=0)],
        axis=1,
    )
    fetched = lax.all_to_all(
        outgoing.reshape(devices, capacity, 2, 6, node_count),
        ("gx", "gy"),
        split_axis=0,
        concat_axis=0,
        tiled=True,
    )
    fetched = fetched.reshape(slot_count, 2, 6, node_count)
    sec_nodes = jnp.take(fetched[:, 0], sec_slots, axis=0)
    pri_nodes = jnp.take(fetched[:, 1], pri_slots, axis=0)
    live = jnp.arange(quad_points, dtype=jnp.int32)[None, :] < qcount[:, None]
    weights = jnp.where(live, qweights, jnp.zeros_like(qweights))
    seg_group = 16
    groups = seg_count // seg_group

    def one_group(inputs):
        points, quad_weights, sec_here, pri_here = inputs
        sec_shape = shape_values(points, sec_here[:, :3])
        pri_shape = shape_values(points, pri_here[:, :3])
        weighted = quad_weights[:, :, None] * sec_shape
        dense_sec = jnp.einsum("gqk,gqj->gkj", weighted, sec_shape, precision=hp)
        dense_mix = jnp.einsum("gqk,gqj->gkj", weighted, pri_shape, precision=hp)
        return jnp.einsum("gkj,gcj->gck", dense_sec, sec_here[:, 3:], precision=hp) - jnp.einsum(
            "gkj,gcj->gck", dense_mix, pri_here[:, 3:], precision=hp
        )

    contrib = lax.map(
        one_group,
        (
            qpoints.reshape(groups, seg_group, 3, quad_points),
            weights.reshape(groups, seg_group, quad_points),
            sec_nodes.reshape(groups, seg_group, 6, node_count),
            pri_nodes.reshape(groups, seg_group, 6, node_count),
        ),
    )
    contrib = contrib.reshape(seg_count, 3, node_count)
    placing = sec_matches.astype(jnp.float32)
    parcels = jnp.einsum("sp,scn->pcn", placing, contrib, precision=hp)
    incoming = lax.all_to_all(
        parcels.reshape(devices, capacity, 3, node_count),
        ("gx", "gy"),
        split_axis=0,
        concat_axis=0,
        tiled=True,
    )
    incoming = incoming.reshape(slot_count, 3, node_count)
    select = (jnp.arange(blocks_dev, dtype=jnp.int32)[:, None] == received[None, :, 0]).astype(
        jnp.float32
    )
    return jnp.einsum("bp,pcn->bcn", select, incoming, precision=hp)


def solution(mesh):
    placed = (
        P(("gx", "gy"), None, None),
        P(("gx", "gy"), None, None),
        P(("gx", "gy"), None, None),
        P(("gx", "gy"), None),
        P(("gx", "gy")),
        P(("gx", "gy")),
        P(("gx", "gy")),
    )
    return jax.shard_map(
        body, mesh=mesh, in_specs=placed, out_specs=P(("gx", "gy"), None, None), check_vma=False
    )
```

profile of v0, /device:TPU:1, one launch (start us, length us, event | category | flops | bytes accessed | tf_op | source)
XLA Modules:
  0.0 412.0 jit_solution(80999348846144236)
XLA Ops:
  3.2 11.5 %all-to-all-start = ((s32[128,4,2]{1,2,0:T(2,128)}), s32[128,4,2]{1,2,0:T(2,128)S(1)}, u32[]{:S(2)}, u32[]{:S(2)}) async-start(s32[128,4,2]{1,2,0:T(2,128)} %copy.60), calls=%async_computation | async-start | bytes 262144 | tf_op jit(solution)/shard_map/all_to_all | solution.py:42
  16.9 8.0 %all-to-all-done = s32[128,4,2]{1,2,0:T(2,128)S(1)} async-done(((s32[128,4,2]{1,2,0:T(2,128)}), s32[128,4,2]{1,2,0:T(2,128)S(1)}, u32[]{:S(2)}, u32[]{:S(2)}) %all-to-all-start) | async-done | bytes 4128 | tf_op jit(solution)/shard_map/all_to_all | solution.py:42
  45.7 40.3 %all-to-all-done.1 = f32[128,4,2,6,128]{4,1,3,2,0:T(4,128)S(1)} async-done(((f32[128,4,2,6,128]{4,1,3,2,0:T(4,128)}), f32[128,4,2,6,128]{4,1,3,2,0:T(4,128)S(1)}, u32[]{:S(2)}, u32[]{:S(2)}) %all-to-all-start.1) | async-done | bytes 3145760 | tf_op jit(solution)/shard_map/all_to_all | solution.py:55
  94.0 293.9 %while.10 = (s32[]{:T(128)}, f32[16,16,3,128]{3,2,1,0:T(4,128)S(1)}, f32[16,16,6,128]{3,2,1,0:T(8,128)}, f32[16,16,256]{2,1,0:T(8,128)S(1)}, f32[16,16,3,256]{3,...) while((s32[]{:T(128)}, f32[16,16,3,128]{3,2,1,0:T(4,128)S(1)}, f32[16,16,6,128]{3,2,1,0:T(8,128)}, ...), condition=%wide.region_7.10_spmd, body=%wide.region_4.9_spmd.sunk | while | flops 1668282368 | bytes 5259357 | solution.py:81
  97.9 5.5 %fusion.70 = f32[16,128,128]{2,1,0:T(8,128)S(1)} fusion(f32[16,256]{1,0:T(8,128)S(1)} %get-tuple-element.163, f32[16,128]{1,0:T(8,128)S(1)} %bitcast.101, f32[16,128]{1,0:T(8,128)S(1)} %bitcast.103, f32[16,128]{1,0:T(8,128)S(1)} %bitcast.99, f32[16,256]{1,0:T(8,128)S(1)} %get-tuple-element.155, f32[16,256]{1,0:T(8,128)S(1)} %get-tuple-element.156, ...), kind=kOutput, calls=%fused_computation.4.clone.1 | convolution fusion | flops 818413568 | bytes 1196032 | tf_op jit(solution)/shard_map/while/body/eval_jaxpr/gqk,gqj->gkj/dot_general | solution.py:76
  103.4 5.5 %fusion.68 = f32[16,128,128]{2,1,0:T(8,128)S(1)} fusion(f32[16,256]{1,0:T(8,128)S(1)} %get-tuple-element.162, f32[16,128]{1,0:T(8,128)S(1)} %bitcast.94, f32[16,256]{1,0:T(8,128)S(1)} %get-tuple-element.155, f32[16,128]{1,0:T(8,128)S(1)} %bitcast.97, f32[16,256]{1,0:T(8,128)S(1)} %get-tuple-element.156, f32[16,128]{1,0:T(8,128)S(1)} %bitcast.91, ...), kind=kOutput, calls=%fused_computation.6.clone.1 | convolution fusion | flops 818413568 | bytes 1155072 | tf_op jit(solution)/shard_map/while/body/eval_jaxpr/gqk,gqj->gkj/dot_general | solution.py:75
  116.3 5.5 %fusion.70 = f32[16,128,128]{2,1,0:T(8,128)S(1)} fusion(f32[16,256]{1,0:T(8,128)S(1)} %get-tuple-element.163, f32[16,128]{1,0:T(8,128)S(1)} %bitcast.101, f32[16,128]{1,0:T(8,128)S(1)} %bitcast.103, f32[16,128]{1,0:T(8,128)S(1)} %bitcast.99, f32[16,256]{1,0:T(8,128)S(1)} %get-tuple-element.155, f32[16,256]{1,0:T(8,128)S(1)} %get-tuple-element.156, ...), kind=kOutput, calls=%fused_computation.4.clone.1 | convolution fusion | flops 818413568 | bytes 1196032 | tf_op jit(solution)/shard_map/while/body/eval_jaxpr/gqk,gqj->gkj/dot_general | solution.py:76
  121.8 5.5 %fusion.68 = f32[16,128,128]{2,1,0:T(8,128)S(1)} fusion(f32[16,256]{1,0:T(8,128)S(1)} %get-tuple-element.162, f32[16,128]{1,0:T(8,128)S(1)} %bitcast.94, f32[16,256]{1,0:T(8,128)S(1)} %get-tuple-element.155, f32[16,128]{1,0:T(8,128)S(1)} %bitcast.97, f32[16,256]{1,0:T(8,128)S(1)} %get-tuple-element.156, f32[16,128]{1,0:T(8,128)S(1)} %bitcast.91, ...), kind=kOutput, calls=%fused_computation.6.clone.1 | convolution fusion | flops 818413568 | bytes 1155072 | tf_op jit(solution)/shard_map/while/body/eval_jaxpr/gqk,gqj->gkj/dot_general | solution.py:75
  134.6 5.5 %fusion.70 = f32[16,128,128]{2,1,0:T(8,128)S(1)} fusion(f32[16,256]{1,0:T(8,128)S(1)} %get-tuple-element.163, f32[16,128]{1,0:T(8,128)S(1)} %bitcast.101, f32[16,128]{1,0:T(8,128)S(1)} %bitcast.103, f32[16,128]{1,0:T(8,128)S(1)} %bitcast.99, f32[16,256]{1,0:T(8,128)S(1)} %get-tuple-element.155, f32[16,256]{1,0:T(8,128)S(1)} %get-tuple-element.156, ...), kind=kOutput, calls=%fused_computation.4.clone.1 | convolution fusion | flops 818413568 | bytes 1196032 | tf_op jit(solution)/shard_map/while/body/eval_jaxpr/gqk,gqj->gkj/dot_general | solution.py:76
  140.1 5.5 %fusion.68 = f32[16,128,128]{2,1,0:T(8,128)S(1)} fusion(f32[16,256]{1,0:T(8,128)S(1)} %get-tuple-element.162, f32[16,128]{1,0:T(8,128)S(1)} %bitcast.94, f32[16,256]{1,0:T(8,128)S(1)} %get-tuple-element.155, f32[16,128]{1,0:T(8,128)S(1)} %bitcast.97, f32[16,256]{1,0:T(8,128)S(1)} %get-tuple-element.156, f32[16,128]{1,0:T(8,128)S(1)} %bitcast.91, ...), kind=kOutput, calls=%fused_computation.6.clone.1 | convolution fusion | flops 818413568 | bytes 1155072 | tf_op jit(solution)/shard_map/while/body/eval_jaxpr/gqk,gqj->gkj/dot_general | solution.py:75
  153.0 5.5 %fusion.70 = f32[16,128,128]{2,1,0:T(8,128)S(1)} fusion(f32[16,256]{1,0:T(8,128)S(1)} %get-tuple-element.163, f32[16,128]{1,0:T(8,128)S(1)} %bitcast.101, f32[16,128]{1,0:T(8,128)S(1)} %bitcast.103, f32[16,128]{1,0:T(8,128)S(1)} %bitcast.99, f32[16,256]{1,0:T(8,128)S(1)} %get-tuple-element.155, f32[16,256]{1,0:T(8,128)S(1)} %get-tuple-element.156, ...), kind=kOutput, calls=%fused_computation.4.clone.1 | convolution fusion | flops 818413568 | bytes 1196032 | tf_op jit(solution)/shard_map/while/body/eval_jaxpr/gqk,gqj->gkj/dot_general | solution.py:76
  171.4 5.5 %fusion.70 = f32[16,128,128]{2,1,0:T(8,128)S(1)} fusion(f32[16,256]{1,0:T(8,128)S(1)} %get-tuple-element.163, f32[16,128]{1,0:T(8,128)S(1)} %bitcast.101, f32[16,128]{1,0:T(8,128)S(1)} %bitcast.103, f32[16,128]{1,0:T(8,128)S(1)} %bitcast.99, f32[16,256]{1,0:T(8,128)S(1)} %get-tuple-element.155, f32[16,256]{1,0:T(8,128)S(1)} %get-tuple-element.156, ...), kind=kOutput, calls=%fused_computation.4.clone.1 | convolution fusion | flops 818413568 | bytes 1196032 | tf_op jit(solution)/shard_map/while/body/eval_jaxpr/gqk,gqj->gkj/dot_general | solution.py:76
  189.7 5.5 %fusion.70 = f32[16,128,128]{2,1,0:T(8,128)S(1)} fusion(f32[16,256]{1,0:T(8,128)S(1)} %get-tuple-element.163, f32[16,128]{1,0:T(8,128)S(1)} %bitcast.101, f32[16,128]{1,0:T(8,128)S(1)} %bitcast.103, f32[16,128]{1,0:T(8,128)S(1)} %bitcast.99, f32[16,256]{1,0:T(8,128)S(1)} %get-tuple-element.155, f32[16,256]{1,0:T(8,128)S(1)} %get-tuple-element.156, ...), kind=kOutput, calls=%fused_computation.4.clone.1 | convolution fusion | flops 818413568 | bytes 1196032 | tf_op jit(solution)/shard_map/while/body/eval_jaxpr/gqk,gqj->gkj/dot_general | solution.py:76
  208.1 5.5 %fusion.70 = f32[16,128,128]{2,1,0:T(8,128)S(1)} fusion(f32[16,256]{1,0:T(8,128)S(1)} %get-tuple-element.163, f32[16,128]{1,0:T(8,128)S(1)} %bitcast.101, f32[16,128]{1,0:T(8,128)S(1)} %bitcast.103, f32[16,128]{1,0:T(8,128)S(1)} %bitcast.99, f32[16,256]{1,0:T(8,128)S(1)} %get-tuple-element.155, f32[16,256]{1,0:T(8,128)S(1)} %get-tuple-element.156, ...), kind=kOutput, calls=%fused_computation.4.clone.1 | convolution fusion | flops 818413568 | bytes 1196032 | tf_op jit(solution)/shard_map/while/body/eval_jaxpr/gqk,gqj->gkj/dot_general | solution.py:76
  226.5 5.5 %fusion.70 = f32[16,128,128]{2,1,0:T(8,128)S(1)} fusion(f32[16,256]{1,0:T(8,128)S(1)} %get-tuple-element.163, f32[16,128]{1,0:T(8,128)S(1)} %bitcast.101, f32[16,128]{1,0:T(8,128)S(1)} %bitcast.103, f32[16,128]{1,0:T(8,128)S(1)} %bitcast.99, f32[16,256]{1,0:T(8,128)S(1)} %get-tuple-element.155, f32[16,256]{1,0:T(8,128)S(1)} %get-tuple-element.156, ...), kind=kOutput, calls=%fused_computation.4.clone.1 | convolution fusion | flops 818413568 | bytes 1196032 | tf_op jit(solution)/shard_map/while/body/eval_jaxpr/gqk,gqj->gkj/dot_general | solution.py:76
  244.8 5.5 %fusion.70 = f32[16,128,128]{2,1,0:T(8,128)S(1)} fusion(f32[16,256]{1,0:T(8,128)S(1)} %get-tuple-element.163, f32[16,128]{1,0:T(8,128)S(1)} %bitcast.101, f32[16,128]{1,0:T(8,128)S(1)} %bitcast.103, f32[16,128]{1,0:T(8,128)S(1)} %bitcast.99, f32[16,256]{1,0:T(8,128)S(1)} %get-tuple-element.155, f32[16,256]{1,0:T(8,128)S(1)} %get-tuple-element.156, ...), kind=kOutput, calls=%fused_computation.4.clone.1 | convolution fusion | flops 818413568 | bytes 1196032 | tf_op jit(solution)/shard_map/while/body/eval_jaxpr/gqk,gqj->gkj/dot_general | solution.py:76
  263.2 5.5 %fusion.70 = f32[16,128,128]{2,1,0:T(8,128)S(1)} fusion(f32[16,256]{1,0:T(8,128)S(1)} %get-tuple-element.163, f32[16,128]{1,0:T(8,128)S(1)} %bitcast.101, f32[16,128]{1,0:T(8,128)S(1)} %bitcast.103, f32[16,128]{1,0:T(8,128)S(1)} %bitcast.99, f32[16,256]{1,0:T(8,128)S(1)} %get-tuple-element.155, f32[16,256]{1,0:T(8,128)S(1)} %get-tuple-element.156, ...), kind=kOutput, calls=%fused_computation.4.clone.1 | convolution fusion | flops 818413568 | bytes 1196032 | tf_op jit(solution)/shard_map/while/body/eval_jaxpr/gqk,gqj->gkj/dot_general | solution.py:76
  281.6 5.5 %fusion.70 = f32[16,128,128]{2,1,0:T(8,128)S(1)} fusion(f32[16,256]{1,0:T(8,128)S(1)} %get-tuple-element.163, f32[16,128]{1,0:T(8,128)S(1)} %bitcast.101, f32[16,128]{1,0:T(8,128)S(1)} %bitcast.103, f32[16,128]{1,0:T(8,128)S(1)} %bitcast.99, f32[16,256]{1,0:T(8,128)S(1)} %get-tuple-element.155, f32[16,256]{1,0:T(8,128)S(1)} %get-tuple-element.156, ...), kind=kOutput, calls=%fused_computation.4.clone.1 | convolution fusion | flops 818413568 | bytes 1196032 | tf_op jit(solution)/shard_map/while/body/eval_jaxpr/gqk,gqj->gkj/dot_general | solution.py:76
  299.9 5.5 %fusion.70 = f32[16,128,128]{2,1,0:T(8,128)S(1)} fusion(f32[16,256]{1,0:T(8,128)S(1)} %get-tuple-element.163, f32[16,128]{1,0:T(8,128)S(1)} %bitcast.101, f32[16,128]{1,0:T(8,128)S(1)} %bitcast.103, f32[16,128]{1,0:T(8,128)S(1)} %bitcast.99, f32[16,256]{1,0:T(8,128)S(1)} %get-tuple-element.155, f32[16,256]{1,0:T(8,128)S(1)} %get-tuple-element.156, ...), kind=kOutput, calls=%fused_computation.4.clone.1 | convolution fusion | flops 818413568 | bytes 1196032 | tf_op jit(solution)/shard_map/while/body/eval_jaxpr/gqk,gqj->gkj/dot_general | solution.py:76
  318.3 5.5 %fusion.70 = f32[16,128,128]{2,1,0:T(8,128)S(1)} fusion(f32[16,256]{1,0:T(8,128)S(1)} %get-tuple-element.163, f32[16,128]{1,0:T(8,128)S(1)} %bitcast.101, f32[16,128]{1,0:T(8,128)S(1)} %bitcast.103, f32[16,128]{1,0:T(8,128)S(1)} %bitcast.99, f32[16,256]{1,0:T(8,128)S(1)} %get-tuple-element.155, f32[16,256]{1,0:T(8,128)S(1)} %get-tuple-element.156, ...), kind=kOutput, calls=%fused_computation.4.clone.1 | convolution fusion | flops 818413568 | bytes 1196032 | tf_op jit(solution)/shard_map/while/body/eval_jaxpr/gqk,gqj->gkj/dot_general | solution.py:76
  336.7 5.5 %fusion.70 = f32[16,128,128]{2,1,0:T(8,128)S(1)} fusion(f32[16,256]{1,0:T(8,128)S(1)} %get-tuple-element.163, f32[16,128]{1,0:T(8,128)S(1)} %bitcast.101, f32[16,128]{1,0:T(8,128)S(1)} %bitcast.103, f32[16,128]{1,0:T(8,128)S(1)} %bitcast.99, f32[16,256]{1,0:T(8,128)S(1)} %get-tuple-element.155, f32[16,256]{1,0:T(8,128)S(1)} %get-tuple-element.156, ...), kind=kOutput, calls=%fused_computation.4.clone.1 | convolution fusion | flops 818413568 | bytes 1196032 | tf_op jit(solution)/shard_map/while/body/eval_jaxpr/gqk,gqj->gkj/dot_general | solution.py:76
  355.0 5.5 %fusion.70 = f32[16,128,128]{2,1,0:T(8,128)S(1)} fusion(f32[16,256]{1,0:T(8,128)S(1)} %get-tuple-element.163, f32[16,128]{1,0:T(8,128)S(1)} %bitcast.101, f32[16,128]{1,0:T(8,128)S(1)} %bitcast.103, f32[16,128]{1,0:T(8,128)S(1)} %bitcast.99, f32[16,256]{1,0:T(8,128)S(1)} %get-tuple-element.155, f32[16,256]{1,0:T(8,128)S(1)} %get-tuple-element.156, ...), kind=kOutput, calls=%fused_computation.4.clone.1 | convolution fusion | flops 818413568 | bytes 1196032 | tf_op jit(solution)/shard_map/while/body/eval_jaxpr/gqk,gqj->gkj/dot_general | solution.py:76
  373.4 5.5 %fusion.70 = f32[16,128,128]{2,1,0:T(8,128)S(1)} fusion(f32[16,256]{1,0:T(8,128)S(1)} %get-tuple-element.163, f32[16,128]{1,0:T(8,128)S(1)} %bitcast.101, f32[16,128]{1,0:T(8,128)S(1)} %bitcast.103, f32[16,128]{1,0:T(8,128)S(1)} %bitcast.99, f32[16,256]{1,0:T(8,128)S(1)} %get-tuple-element.155, f32[16,256]{1,0:T(8,128)S(1)} %get-tuple-element.156, ...), kind=kOutput, calls=%fused_computation.4.clone.1 | convolution fusion | flops 818413568 | bytes 1196032 | tf_op jit(solution)/shard_map/while/body/eval_jaxpr/gqk,gqj->gkj/dot_general | solution.py:76
  389.0 21.1 %all_to_all.15 = f32[128,4,3,128]{3,1,2,0:T(4,128)S(1)} all-to-all(f32[128,4,3,128]{3,1,2,0:T(4,128)S(1)} %copy.69), channel_id=1, replica_groups=mesh['gx'=8,'gy'=16] {'gx','gy'}, dimensions={0} | all-to-all | bytes 1572864 | tf_op jit(solution)/shard_map/all_to_all | solution.py:93
  (212 shorter events, 225.5 us)
Async XLA Ops:
  0.0 16.1 %copy-start = (f32[384,3,128]{2,0,1:T(8,128)S(1)}, f32[384,3,128]{2,0,1:T(8,128)}, u32[]{:S(2)}) copy-start(f32[384,3,128]{2,0,1:T(8,128)} %param.14) | copy-start | bytes 1769476
  3.2 21.7 %all-to-all-start = ((s32[128,4,2]{1,2,0:T(2,128)}), s32[128,4,2]{1,2,0:T(2,128)S(1)}, u32[]{:S(2)}, u32[]{:S(2)}) async-start(s32[128,4,2]{1,2,0:T(2,128)} %copy.60), calls=%async_computation | async-start | bytes 262144 | tf_op jit(solution)/shard_map/all_to_all | solution.py:42
  40.5 4.1 copy-start.2
  40.5 45.4 %all-to-all-start.1 = ((f32[128,4,2,6,128]{4,1,3,2,0:T(4,128)}), f32[128,4,2,6,128]{4,1,3,2,0:T(4,128)S(1)}, u32[]{:S(2)}, u32[]{:S(2)}) async-start(f32[128,4,2,6,128]{4,1,3,2,0:T(4,128)} %pad_maximum_fusion), calls=%async_computation.1 | async-start | bytes 6291456 | tf_op jit(solution)/shard_map/all_to_all | solution.py:55
  93.0 1.0 copy-start.1
where the time goes:
time: 414 us; the launch traced here: 412 us
  matrix products  234 us (57%)
  other arithmetic  48.4 us (12%)
  waiting for transfers between devices  48.3 us (12%)
  local copies, waits for them, and re-layouts  44 us (11%)
  blocking collectives  21.1 us (5%)
  starting transfers between devices  15.5 us (4%)
    dot_general x16, matrix products, one_group(): dense_mix = jnp.einsum('gqk,gqj->gkj', weighted, pri_shape, precision=hp)  88.1 us
    dot_general x16, matrix products, one_group(): dense_sec = jnp.einsum('gqk,gqj->gkj', weighted, sec_shape, precision=hp)  87.4 us
    all_to_all x1, waiting for transfers between devices, body(): lax.all_to_all(outgoing.reshape(devices, capacity, 2, 6, node_count), ('g...  40.3 us
    reduce_sum x16, other arithmetic, shape_values(): return kernel / jnp.sum(kernel, axis=-1, keepdims=True)  34 us
    dot_general x16, matrix products, one_group(): jnp.einsum('gkj,gcj->gck', dense_mix, pri_here[:, 3:], precision=hp)  28.2 us
    dot_general x16, matrix products, one_group(): jnp.einsum('gkj,gcj->gck', dense_sec, sec_here[:, 3:], precision=hp)  27.7 us
    squeeze x32, local copies, waits for them, and re-layouts, body(): lax.map(one_group, (qpoints.reshape(groups, seg_group, 3, quad_points), w...  26.8 us
    all_to_all x1, blocking collectives, body(): lax.all_to_all(parcels.reshape(devices, capacity, 3, node_count), ('gx',...  21.1 us
  transfers between devices with their start and end apart: 2, of which 2 were waited for; matrix products, arithmetic and copies ran while one was open for 1% of the time, Pallas kernels for 0%

commit v1 on v0

v1 whole, which is shorter than its diff:
```python
import functools
import jax
import jax.numpy as jnp
from jax import lax
from jax.experimental import pallas as pl
from jax.experimental.pallas import tpu as pltpu
from jax.sharding import PartitionSpec as P

AXES = ("gx", "gy")
GROUP = 8


def routing(block_ids, blocks_dev, capacity, slot_count):
    owners = block_ids // blocks_dev
    local_ids = block_ids % blocks_dev
    positions = jnp.arange(block_ids.shape[0], dtype=jnp.int32)
    same_owner = (owners[:, None] == owners[None, :]) & (positions[:, None] > positions[None, :])
    ranks = jnp.sum(same_owner.astype(jnp.int32), axis=1)
    slot_ids = owners * capacity + ranks
    matches = slot_ids[:, None] == jnp.arange(slot_count, dtype=jnp.int32)[None, :]
    request = jnp.sum(jnp.where(matches, local_ids[:, None], 0), axis=0)
    return (slot_ids, request)


def gather_kernel(devices, capacity, blocks, ids_ref, xc_ref, xu_ref, sec_ref, pri_ref):
    rows = 6 * capacity

    def one_device(dev, carry):
        for side, out in ((0, sec_ref), (1, pri_ref)):
            for rank in range(capacity):
                local = ids_ref[side * devices * capacity + dev * capacity + rank]
                base = dev * rows + rank
                out[pl.ds(base, 3, stride=capacity), :] = xc_ref[pl.ds(local, 3, stride=blocks), :]
                out[pl.ds(base + 3 * capacity, 3, stride=capacity), :] = xu_ref[
                    pl.ds(local, 3, stride=blocks), :
                ]
        return carry

    lax.fori_loop(0, devices, one_device, 0)


def pieces(value):
    first = value.astype(jnp.bfloat16).astype(jnp.float32)
    rest = value - first
    second = rest.astype(jnp.bfloat16).astype(jnp.float32)
    return (first, second, rest - second)


def node_side(fetched_ref, slot, capacity):
    dev = slot // capacity
    rank = slot % capacity
    raw = fetched_ref[pl.ds(dev * (6 * capacity) + rank, 6, stride=capacity), :]
    raw = jnp.concatenate([raw, jnp.zeros((2, raw.shape[1]), jnp.float32)], axis=0)
    row = lax.broadcasted_iota(jnp.int32, raw.shape, 0)
    coord = jnp.where(row < 3, raw, 0.0)
    square = 2.0 * jnp.sum(coord * coord, axis=0, keepdims=True)
    extended = jnp.where(row == 3, square, jnp.where(row == 4, 1.0, -4.0 * coord))
    a, b, c = pieces(extended)
    stacked = jnp.concatenate([a, a, b, b, a, c], axis=0)
    disp = jnp.where(row < 3, 0.0, jnp.where(row == 6, 1.0, raw))
    high = disp.astype(jnp.bfloat16).astype(jnp.float32)
    lhs = jnp.concatenate([high, disp - high], axis=0)
    lhs = jnp.concatenate([lhs, lhs], axis=1).astype(jnp.bfloat16)
    return stacked.T.astype(jnp.bfloat16), lhs


def point_side(points):
    a, b, c = pieces(points)
    return jnp.concatenate([a, b, a, b, c, a], axis=0).astype(jnp.bfloat16)


def kernel_values(node_op, point_op):
    dist = jnp.dot(node_op, point_op, preferred_element_type=jnp.float32)
    value = 1.0 / dist
    high = value.astype(jnp.bfloat16)
    low = (value - high.astype(jnp.float32)).astype(jnp.bfloat16)
    return jnp.concatenate([high, low], axis=0)


def pri_kernel(capacity, slots_ref, fetched_ref, points_ref, out_ref):
    def one_group(g, carry):
        for i in range(GROUP):
            s = g * GROUP + i
            node_op, lhs = node_side(fetched_ref, slots_ref[s], capacity)
            both = kernel_values(node_op, point_side(points_ref[s]))
            sums = jnp.dot(lhs, both, preferred_element_type=jnp.float32)
            sums = sums[:8] + sums[8:]
            out_ref[s] = sums * (1.0 / sums[6:7])
        return carry

    lax.fori_loop(0, points_ref.shape[0] // GROUP, one_group, 0)


def sec_kernel(capacity, slots_ref, fetched_ref, points_ref, other_ref, out_ref):
    out_ref[...] = jnp.zeros_like(out_ref)

    def one_group(g, carry):
        for i in range(GROUP):
            s = g * GROUP + i
            slot = slots_ref[s]
            points = points_ref[s]
            node_op, lhs = node_side(fetched_ref, slot, capacity)
            both = kernel_values(node_op, point_side(points))
            sums = jnp.dot(lhs, both, preferred_element_type=jnp.float32)
            sums = sums[:8] + sums[8:]
            inverse = 1.0 / sums[6:7]
            gap = (points[5:6] * inverse) * (sums * inverse - other_ref[s])
            high = gap.astype(jnp.bfloat16).astype(jnp.float32)
            left = jnp.concatenate([high, gap - high], axis=0).astype(jnp.bfloat16)
            result = lax.dot_general(
                left, both, (((1,), (1,)), ((), ())), preferred_element_type=jnp.float32
            )
            half = result.shape[1] // 2
            result = result[:8] + result[8:]
            result = result[:, :half] + result[:, half:]
            dev = slot // capacity
            base = dev * (3 * capacity) + slot % capacity
            out_ref[pl.ds(base, 3, stride=capacity), :] = result[3:6]
        return carry

    lax.fori_loop(0, points_ref.shape[0] // GROUP, one_group, 0)


def body(node_coords, node_disp, qpoints, qweights, qcount, sec_block, pri_block):
    devices = lax.axis_size("gx") * lax.axis_size("gy")
    blocks = node_coords.shape[0]
    nodes = node_coords.shape[2]
    segs = qpoints.shape[0]
    quad = qpoints.shape[2]
    slots = 2 * segs
    cap = slots // devices
    f32 = jnp.float32
    smem = pl.BlockSpec(memory_space=pltpu.SMEM)
    vmem = pl.BlockSpec(memory_space=pltpu.VMEM)

    def exchange(value):
        return lax.all_to_all(value, AXES, split_axis=0, concat_axis=0, tiled=True)

    sec_slots, sec_request = routing(sec_block, blocks, cap, slots)
    pri_slots, pri_request = routing(pri_block, blocks, cap, slots)
    requests = jnp.concatenate(
        [sec_request.reshape(devices, cap), pri_request.reshape(devices, cap)], axis=1
    )
    received = exchange(requests)
    sec_ids = received[:, :cap].reshape(slots)
    ids = jnp.concatenate([sec_ids, received[:, cap:].reshape(slots)])

    xc = jnp.transpose(node_coords, (1, 0, 2)).reshape(3 * blocks, nodes)
    xu = jnp.transpose(node_disp, (1, 0, 2)).reshape(3 * blocks, nodes)
    sendable = jax.ShapeDtypeStruct((devices * 6 * cap, nodes), f32)
    sec_out, pri_out = pl.pallas_call(
        functools.partial(gather_kernel, devices, cap, blocks),
        out_shape=(sendable, sendable),
        in_specs=[smem, vmem, vmem],
        out_specs=(vmem, vmem),
    )(ids, xc, xu)
    pri_in = exchange(pri_out.reshape(devices, 6 * cap, nodes)).reshape(-1, nodes)
    sec_in = exchange(sec_out.reshape(devices, 6 * cap, nodes)).reshape(-1, nodes)

    live = jnp.arange(quad, dtype=jnp.int32)[None, :] < qcount[:, None]
    weights = jnp.where(live, qweights, jnp.zeros_like(qweights))
    qx, qy, qz = qpoints[:, 0], qpoints[:, 1], qpoints[:, 2]
    ones = jnp.ones_like(qx)
    zeros = jnp.zeros_like(qx)
    square = 1.0 + 2.0 * (qx * qx + qy * qy + qz * qz)
    points = jnp.stack([qx, qy, qz, ones, square, weights, zeros, zeros], axis=1)

    other = pl.pallas_call(
        functools.partial(pri_kernel, cap),
        out_shape=jax.ShapeDtypeStruct((segs, 8, quad), f32),
        in_specs=[smem, vmem, vmem],
        out_specs=vmem,
    )(pri_slots, pri_in, points)
    parcels = pl.pallas_call(
        functools.partial(sec_kernel, cap),
        out_shape=jax.ShapeDtypeStruct((devices * 3 * cap, nodes), f32),
        in_specs=[smem, vmem, vmem, vmem],
        out_specs=vmem,
    )(sec_slots, sec_in, points, other)
    incoming = exchange(parcels.reshape(devices, 3 * cap, nodes))
    incoming = incoming.reshape(devices, 3, cap, nodes)
    select = (jnp.arange(blocks, dtype=jnp.int32)[:, None] == sec_ids[None, :]).astype(f32)
    incoming = jnp.transpose(incoming, (0, 2, 1, 3)).reshape(slots, 3, nodes)
    return jnp.einsum("bp,pcn->bcn", select, incoming, precision=lax.Precision.HIGHEST)


def solution(mesh):
    split3 = P(AXES, None, None)
    placed = (split3, split3, split3, P(AXES, None), P(AXES), P(AXES), P(AXES))
    return jax.shard_map(body, mesh=mesh, in_specs=placed, out_specs=split3, check_vma=False)
```

time: 414 us -> 191 us (0.46)
  matrix products: 234 us -> 1.67 us
  Pallas kernels: 0 us -> 87.5 us
  blocking collectives: 21.1 us -> 79.9 us
  waiting for transfers between devices: 48.3 us -> 0.01 us
  other arithmetic: 48.4 us -> 4.24 us
  local copies, waits for them, and re-layouts: 44 us -> 11.8 us
  starting transfers between devices: 15.5 us -> 4.46 us
    dot_general x66 -> x1, matrix products: 234 us -> 1.67 us  [body(): jnp.einsum('bp,pcn->bcn', select, incoming, precision=lax.Precision.HIGHEST)]
    pallas_call x0 -> x3, Pallas kernels: none -> 87.5 us  [the longest x1 56.7 us: body(): pl.pallas_call(functools.partial(sec_kernel, cap), out_shape=jax.ShapeDty...]
    all_to_all x1 -> x3, blocking collectives: 21.1 us -> 79.9 us  [exchange(): return lax.all_to_all(value, AXES, split_axis=0, concat_axis=0, tiled=True)]
    all_to_all x2 -> x1, waiting for transfers between devices: 48.3 us -> 0.01 us  [exchange(): return lax.all_to_all(value, AXES, split_axis=0, concat_axis=0, tiled=True)]
    reduce_sum x16 -> x0, other arithmetic: 34 us -> none  [shape_values(): return kernel / jnp.sum(kernel, axis=-1, keepdims=True)]
    squeeze x33 -> x0, local copies, waits for them, and re-layouts: 28.4 us -> none  [the longest x32 26.8 us: body(): lax.map(one_group, (qpoints.reshape(groups, seg_group, 3, quad_points), w...]
    all_to_all x2 -> x1, starting transfers between devices: 15.5 us -> 4.46 us  [exchange(): return lax.all_to_all(value, AXES, split_axis=0, concat_axis=0, tiled=True)]
    gather x4 -> x0, local copies, waits for them, and re-layouts: 8.84 us -> none  [the longest x1 2.74 us: body(): jnp.take(node_data, received[:, 0], axis=0)]
  transfers between devices with their start and end apart: 2 -> 1, of which waited for: 2 -> 0; matrix products, arithmetic and copies ran while one was open for 1% -> 5% of each run, Pallas kernels for 0% -> 13%
where the time goes in v1:
time: 191 us; the launch traced here: 190 us
  Pallas kernels  87.5 us (46%)
  blocking collectives  79.9 us (42%)
  local copies, waits for them, and re-layouts  11.8 us (6%)
  starting transfers between devices  4.46 us (2%)
  other arithmetic  4.24 us (2%)
    all_to_all x3, blocking collectives, exchange(): return lax.all_to_all(value, AXES, split_axis=0, concat_axis=0, tiled=True)  79.9 us
    pallas_call x1, Pallas kernels, body(): pl.pallas_call(functools.partial(sec_kernel, cap), out_shape=jax.ShapeDty...  56.7 us
    pallas_call x1, Pallas kernels, body(): pl.pallas_call(functools.partial(pri_kernel, cap), out_shape=jax.ShapeDty...  23.7 us
    another operation x4, local copies, waits for them, and re-layouts, body(): jnp.stack([qx, qy, qz, ones, square, weights, zeros, zeros], axis=1)  7.46 us
    pallas_call x1, Pallas kernels, body(): pl.pallas_call(functools.partial(gather_kernel, devices, cap, blocks), ou...  7 us
    all_to_all x1, starting transfers between devices, exchange(): return lax.all_to_all(value, AXES, split_axis=0, concat_axis=0, tiled=True)  4.46 us
  transfers between devices with their start and end apart: 1, of which 0 were waited for; matrix products, arithmetic and copies ran while one was open for 5% of the time, Pallas kernels for 13%

profile of v1, /device:TPU:1, one launch (start us, length us, event | category | flops | bytes accessed | tf_op | source)
XLA Modules:
  0.0 189.7 jit_solution(17456754352318436098)
XLA Ops:
  0.0 0.7 and_select_fusion.2
  0.7 0.2 convert_reduce_fusion.1
  0.9 0.7 and_select_fusion.1
  1.6 0.2 convert_reduce_fusion
  1.8 0.1 select_reduce_fusion
  2.1 0.1 select_reduce_fusion.1
  2.4 21.2 %all_to_all.27 = s32[128,1,8]{2,1,0:T(1,128)S(1)} all-to-all(s32[128,1,8]{2,1,0:T(1,128)S(1)} %bitcast.31), channel_id=1, replica_groups=mesh['gx'=8,'gy'=16] {'gx','gy'}, dimensions={0} | all-to-all | bytes 8192 | tf_op jit(solution)/shard_map/all_to_all | solution.py:137
  23.9 0.6 pad_add_fusion.1.ids_ref
  24.5 7.0 %shard_map.73 = (f32[3072,128]{1,0:T(8,128)}, f32[3072,128]{1,0:T(8,128)}) custom-call(s32[1024]{0:T(1024)} %pad_add_fusion.1.ids_ref, f32[1152,128]{1,0:T(8,128)} %bitcast.28, f32[1152,128]{1,0:T(8,128)} %bitcast.29), custom_call_target="tpu_custom_call" | custom-call | tf_op jit(solution)/shard_map/pallas_call | solution.py:151
  31.5 29.7 %all_to_all.28 = f32[128,24,128]{2,1,0:T(8,128)} all-to-all(f32[128,24,128]{2,1,0:T(8,128)} %bitcast.27), channel_id=1, replica_groups=mesh['gx'=8,'gy'=16] {'gx','gy'}, dimensions={0} | all-to-all | bytes 3145728 | tf_op jit(solution)/shard_map/all_to_all | solution.py:137
  61.2 4.5 %all-to-all-start.1 = ((f32[128,24,128]{2,1,0:T(8,128)}), f32[128,24,128]{2,1,0:T(8,128)S(1)}, u32[]{:S(2)}, u32[]{:S(2)}) async-start(f32[128,24,128]{2,1,0:T(8,128)} %bitcast.26), calls=%async_computation.1 | async-start | bytes 3145728 | tf_op jit(solution)/shard_map/all_to_all | solution.py:137
  65.8 0.9 stack.10
  66.7 0.5 copy.55
  67.3 1.4 multiply_add_fusion
  68.7 0.8 stack_broadcast_in_dim.3.clone
  69.7 5.6 %stack.12.points_ref = f32[256,8,256]{2,1,0:T(8,128)} concatenate(f32[256,3,256]{2,1,0:T(4,128)S(1)} %copy.55, f32[256,1,256]{2,1,0:T(1,128)} %stack_broadcast_in_dim.3.clone, f32[256,1,256]{2,1,0:T(1,128)} %multiply_add_fusion, f32[256,1,256]{2,1,0:T(1,128)S(1)} %copy-done.2, f32[256,2,256]{2,1,0:T(2,128)S(1)} %stack.11), dimensions={1} | concatenate | bytes 4194304 | tf_op jit(solution)/shard_map/stack | solution.py:166
  75.3 23.7 %shard_map.74.other_ref = f32[256,8,256]{2,1,0:T(8,128)} custom-call(s32[256]{0:T(256)} %copy-done.4, f32[3072,128]{1,0:T(8,128)} %bitcast.23, f32[256,8,256]{2,1,0:T(8,128)} %stack.12.points_ref), custom_call_target="tpu_custom_call" | custom-call | tf_op jit(solution)/shard_map/pallas_call | solution.py:168
  99.1 1.2 copy-done
  100.3 56.7 %shard_map.75 = f32[1536,128]{1,0:T(8,128)} custom-call(s32[256]{0:T(256)} %copy-done.5, f32[3072,128]{1,0:T(8,128)} %bitcast.22, f32[256,8,256]{2,1,0:T(8,128)} %stack.12.points_ref, f32[256,8,256]{2,1,0:T(8,128)} %shard_map.74.other_ref), custom_call_target="tpu_custom_call" | custom-call | tf_op jit(solution)/shard_map/pallas_call | solution.py:174
  157.0 1.2 reshape.58
  158.2 29.0 %all_to_all.29 = f32[128,12,128]{2,1,0:T(8,128)S(1)} all-to-all(f32[128,12,128]{2,1,0:T(8,128)S(1)} %reshape.58), channel_id=1, replica_groups=mesh['gx'=8,'gy'=16] {'gx','gy'}, dimensions={0} | all-to-all | bytes 1572864 | tf_op jit(solution)/shard_map/all_to_all | solution.py:137
  187.2 0.3 copy.57
  187.5 0.5 copy.58
  188.0 1.7 fusion.1
  (25 shorter events, 0.9 us)
Async XLA Ops:
  0.9 60.3 %copy-start.5 = (s32[256]{0:T(256)}, s32[256]{0:T(256)S(1)}, u32[]{:S(2)}) copy-start(s32[256]{0:T(256)S(1)} %multiply_add_fusion.2.slots_ref) | copy-start | bytes 3076
  1.8 59.4 %copy-start.4 = (s32[256]{0:T(256)}, s32[256]{0:T(256)S(1)}, u32[]{:S(2)}) copy-start(s32[256]{0:T(256)S(1)} %multiply_add_fusion.1.slots_ref) | copy-start | bytes 3076
  61.2 4.5 %copy-start.3 = (f32[256,256]{1,0:T(8,128)S(1)}, f32[256,256]{1,0:T(8,128)}, u32[]{:S(2)}) copy-start(f32[256,256]{1,0:T(8,128)} %param.10) | copy-start | bytes 786436
  61.2 4.5 %copy-start.6 = (s32[256]{0:T(256)S(1)}, s32[256]{0:T(256)}, u32[]{:S(2)}) copy-start(s32[256]{0:T(256)} %param.11) | copy-start | bytes 3076
  61.2 5.5 %copy-start.1 = (f32[256,3,256]{2,0,1:T(8,128)S(1)}, f32[256,3,256]{2,0,1:T(8,128)}, u32[]{:S(2)}) copy-start(f32[256,3,256]{2,0,1:T(8,128)} %param.9) | copy-start | bytes 2359300
  61.2 37.8 %all-to-all-start.1 = ((f32[128,24,128]{2,1,0:T(8,128)}), f32[128,24,128]{2,1,0:T(8,128)S(1)}, u32[]{:S(2)}, u32[]{:S(2)}) async-start(f32[128,24,128]{2,1,0:T(8,128)} %bitcast.26), calls=%async_computation.1 | async-start | bytes 3145728 | tf_op jit(solution)/shard_map/all_to_all | solution.py:137
  67.3 2.4 %copy-start.2 = (f32[256,1,256]{2,1,0:T(1,128)S(1)}, f32[256,1,256]{2,1,0:T(1,128)}, u32[]{:S(2)}) copy-start(f32[256,1,256]{2,1,0:T(1,128)} %stack.10) | copy-start | bytes 786436
  99.1 1.2 copy-start

commit v2 on v1

v2 whole, which is shorter than its diff:
```python
import functools
import jax
import jax.numpy as jnp
from jax import lax
from jax.experimental import pallas as pl
from jax.experimental.pallas import tpu as pltpu
from jax.sharding import PartitionSpec as P

AXES = ("gx", "gy")
HALF = 8


def routing(block_ids, blocks_dev, capacity, slot_count):
    owners = block_ids // blocks_dev
    local_ids = block_ids % blocks_dev
    positions = jnp.arange(block_ids.shape[0], dtype=jnp.int32)
    same_owner = (owners[:, None] == owners[None, :]) & (positions[:, None] > positions[None, :])
    ranks = jnp.sum(same_owner.astype(jnp.int32), axis=1)
    slot_ids = owners * capacity + ranks
    matches = slot_ids[:, None] == jnp.arange(slot_count, dtype=jnp.int32)[None, :]
    request = jnp.sum(jnp.where(matches, local_ids[:, None], 0), axis=0)
    return (slot_ids, request)


def gather_kernel(devices, capacity, blocks, ids_ref, xc_ref, xu_ref, out_ref):
    rows = 6 * capacity

    def one_device(dev, carry):
        for rank in range(capacity):
            local = ids_ref[dev * capacity + rank]
            base = dev * rows + rank
            out_ref[pl.ds(base, 3, stride=capacity), :] = xc_ref[pl.ds(local, 3, stride=blocks), :]
            out_ref[pl.ds(base + 3 * capacity, 3, stride=capacity), :] = xu_ref[
                pl.ds(local, 3, stride=blocks), :
            ]
        return carry

    lax.fori_loop(0, devices, one_device, 0, unroll=4)


def pieces(value):
    first = value.astype(jnp.bfloat16).astype(jnp.float32)
    rest = value - first
    second = rest.astype(jnp.bfloat16).astype(jnp.float32)
    return (first, second, rest - second)


def node_side(fetched_ref, slot, capacity):
    dev = slot // capacity
    rank = slot % capacity
    raw = fetched_ref[pl.ds(dev * (6 * capacity) + rank, 6, stride=capacity), :]
    raw = jnp.concatenate([raw, jnp.zeros((2, raw.shape[1]), jnp.float32)], axis=0)
    row = lax.broadcasted_iota(jnp.int32, raw.shape, 0)
    coord = jnp.where(row < 3, raw, 0.0)
    square = 2.0 * jnp.sum(coord * coord, axis=0, keepdims=True)
    extended = jnp.where(row == 3, square, jnp.where(row == 4, 1.0, -4.0 * coord))
    a, b, c = pieces(extended)
    stacked = jnp.concatenate([a, a, b, b, a, c], axis=0)
    disp = jnp.where(row < 3, 0.0, jnp.where(row == 6, 1.0, raw))
    high = disp.astype(jnp.bfloat16).astype(jnp.float32)
    lhs = jnp.concatenate([high, disp - high], axis=0)
    lhs = jnp.concatenate([lhs, lhs], axis=1).astype(jnp.bfloat16)
    return stacked.T.astype(jnp.bfloat16), lhs


def point_side(points):
    a, b, c = pieces(points)
    return jnp.concatenate([a, b, a, b, c, a], axis=0).astype(jnp.bfloat16)


def kernel_values(node_op, point_op):
    dist = jnp.dot(node_op, point_op, preferred_element_type=jnp.float32)
    value = 1.0 / dist
    high = value.astype(jnp.bfloat16)
    low = (value - high.astype(jnp.float32)).astype(jnp.bfloat16)
    return jnp.concatenate([high, low], axis=0)


def stage_a(capacity, s, slot, fetched_ref, points_ref, both_ref, lhs_ref, i):
    node_op, lhs = node_side(fetched_ref, slot, capacity)
    lhs_ref[i] = lhs
    both_ref[i] = kernel_values(node_op, point_side(points_ref[s]))


def sums_of(both_ref, lhs_ref, i):
    sums = jnp.dot(lhs_ref[i], both_ref[i], preferred_element_type=jnp.float32)
    return sums[:8] + sums[8:]


def pri_kernel(capacity, slots_ref, fetched_ref, points_ref, out_ref, both_ref, lhs_ref):
    segs = points_ref.shape[0]

    def first(s, i):
        stage_a(capacity, s, slots_ref[s], fetched_ref, points_ref, both_ref, lhs_ref, i)

    def second(s, i):
        sums = sums_of(both_ref, lhs_ref, i)
        out_ref[s] = sums * (1.0 / sums[6:7])

    for i in range(HALF):
        first(i, i)

    def one_group(g, carry):
        base = g * (2 * HALF)
        after = jnp.minimum(base + 2 * HALF, segs - HALF)
        for i in range(HALF):
            second(base + i, i)
            first(base + HALF + i, HALF + i)
        for i in range(HALF):
            second(base + HALF + i, HALF + i)
            first(after + i, i)
        return carry

    lax.fori_loop(0, segs // (2 * HALF), one_group, 0)


def sec_kernel(
    capacity, slots_ref, fetched_ref, points_ref, other_ref, out_ref, both_ref, lhs_ref, left_ref
):
    segs = points_ref.shape[0]
    out_ref[...] = jnp.zeros_like(out_ref)

    def first(s, i):
        stage_a(capacity, s, slots_ref[s], fetched_ref, points_ref, both_ref, lhs_ref, i)

    def second(s, i):
        sums = sums_of(both_ref, lhs_ref, i)
        inverse = 1.0 / sums[6:7]
        gap = (points_ref[s, 5:6] * inverse) * (sums * inverse - other_ref[s])
        high = gap.astype(jnp.bfloat16).astype(jnp.float32)
        left_ref[i] = jnp.concatenate([high, gap - high], axis=0).astype(jnp.bfloat16)

    def third(s, i):
        slot = slots_ref[s]
        result = lax.dot_general(
            left_ref[i], both_ref[i], (((1,), (1,)), ((), ())), preferred_element_type=jnp.float32
        )
        half = result.shape[1] // 2
        result = result[:8] + result[8:]
        result = result[:, :half] + result[:, half:]
        base = (slot // capacity) * (3 * capacity) + slot % capacity
        out_ref[pl.ds(base, 3, stride=capacity), :] = result[3:6]

    for i in range(HALF):
        first(i, i)

    def one_group(g, carry):
        base = g * (2 * HALF)
        after = jnp.minimum(base + 2 * HALF, segs - HALF)
        for i in range(HALF):
            second(base + i, i)
            first(base + HALF + i, HALF + i)
        for i in range(HALF):
            third(base + i, i)
            second(base + HALF + i, HALF + i)
        for i in range(HALF):
            third(base + HALF + i, HALF + i)
            first(after + i, i)
        return carry

    lax.fori_loop(0, segs // (2 * HALF), one_group, 0)


def body(node_coords, node_disp, qpoints, qweights, qcount, sec_block, pri_block):
    devices = lax.axis_size("gx") * lax.axis_size("gy")
    blocks = node_coords.shape[0]
    nodes = node_coords.shape[2]
    segs = qpoints.shape[0]
    quad = qpoints.shape[2]
    slots = 2 * segs
    cap = slots // devices
    f32 = jnp.float32
    smem = pl.BlockSpec(memory_space=pltpu.SMEM)
    vmem = pl.BlockSpec(memory_space=pltpu.VMEM)

    def exchange(value):
        return lax.all_to_all(value, AXES, split_axis=0, concat_axis=0, tiled=True)

    sec_slots, sec_request = routing(sec_block, blocks, cap, slots)
    pri_slots, pri_request = routing(pri_block, blocks, cap, slots)
    requests = jnp.concatenate(
        [sec_request.reshape(devices, cap), pri_request.reshape(devices, cap)], axis=1
    )
    received = exchange(requests)
    sec_ids = received[:, :cap].reshape(slots)
    pri_ids = received[:, cap:].reshape(slots)

    xc = jnp.transpose(node_coords, (1, 0, 2)).reshape(3 * blocks, nodes)
    xu = jnp.transpose(node_disp, (1, 0, 2)).reshape(3 * blocks, nodes)
    gather = pl.pallas_call(
        functools.partial(gather_kernel, devices, cap, blocks),
        out_shape=jax.ShapeDtypeStruct((devices * 6 * cap, nodes), f32),
        in_specs=[smem, vmem, vmem],
        out_specs=vmem,
    )
    pri_in = exchange(gather(pri_ids, xc, xu).reshape(devices, 6 * cap, nodes)).reshape(-1, nodes)
    sec_in = exchange(gather(sec_ids, xc, xu).reshape(devices, 6 * cap, nodes)).reshape(-1, nodes)

    live = jnp.arange(quad, dtype=jnp.int32)[None, :] < qcount[:, None]
    weights = jnp.where(live, qweights, jnp.zeros_like(qweights))
    qx, qy, qz = qpoints[:, 0], qpoints[:, 1], qpoints[:, 2]
    ones = jnp.ones_like(qx)
    zeros = jnp.zeros_like(qx)
    square = 1.0 + 2.0 * (qx * qx + qy * qy + qz * qz)
    points = jnp.stack([qx, qy, qz, ones, square, weights, zeros, zeros], axis=1)

    scratch = [
        pltpu.VMEM((2 * HALF, 2 * nodes, quad), jnp.bfloat16),
        pltpu.VMEM((2 * HALF, 16, 2 * nodes), jnp.bfloat16),
    ]
    other = pl.pallas_call(
        functools.partial(pri_kernel, cap),
        out_shape=jax.ShapeDtypeStruct((segs, 8, quad), f32),
        in_specs=[smem, vmem, vmem],
        out_specs=vmem,
        scratch_shapes=scratch,
    )(pri_slots, pri_in, points)
    parcels = pl.pallas_call(
        functools.partial(sec_kernel, cap),
        out_shape=jax.ShapeDtypeStruct((devices * 3 * cap, nodes), f32),
        in_specs=[smem, vmem, vmem, vmem],
        out_specs=vmem,
        scratch_shapes=scratch + [pltpu.VMEM((2 * HALF, 16, quad), jnp.bfloat16)],
    )(sec_slots, sec_in, points, other)
    incoming = exchange(parcels.reshape(devices, 3, cap, nodes))
    select = (jnp.arange(blocks, dtype=jnp.int32)[:, None] == sec_ids[None, :]).astype(f32)
    incoming = jnp.transpose(incoming, (0, 2, 1, 3)).reshape(slots, 3, nodes)
    return jnp.einsum("bp,pcn->bcn", select, incoming, precision=lax.Precision.HIGHEST)


def solution(mesh):
    split3 = P(AXES, None, None)
    placed = (split3, split3, split3, P(AXES, None), P(AXES), P(AXES), P(AXES))
    return jax.shard_map(body, mesh=mesh, in_specs=placed, out_specs=split3, check_vma=False)
```

time: 191 us -> 141 us (0.74)
  Pallas kernels: 87.5 us -> 46 us
  blocking collectives: 79.9 us -> 47.7 us
  waiting for transfers between devices: 0.01 us -> 19.7 us
  starting transfers between devices: 4.46 us -> 8.45 us
    pallas_call x1, Pallas kernels: 56.7 us -> 22.2 us  [body(): pl.pallas_call(functools.partial(sec_kernel, cap), out_shape=jax.ShapeDty...]
    all_to_all x3 -> x2, blocking collectives: 79.9 us -> 47.7 us  [exchange(): return lax.all_to_all(value, AXES, split_axis=0, concat_axis=0, tiled=True)]
    all_to_all x1 -> x2, waiting for transfers between devices: 0.01 us -> 19.7 us  [exchange(): return lax.all_to_all(value, AXES, split_axis=0, concat_axis=0, tiled=True)]
    pallas_call x1, Pallas kernels: 23.7 us -> 15.2 us  [body(): pl.pallas_call(functools.partial(pri_kernel, cap), out_shape=jax.ShapeDty...]
    all_to_all x1 -> x2, starting transfers between devices: 4.46 us -> 8.45 us  [exchange(): return lax.all_to_all(value, AXES, split_axis=0, concat_axis=0, tiled=True)]
    unnamed x15 -> x17, local copies, waits for them, and re-layouts: 1.76 us -> 4.16 us
    pallas_call x1 -> x2, Pallas kernels: 7 us -> 8.52 us  [the longest x1 4.27 us: body(): gather(sec_ids, xc, xu).reshape(devices, 6 * cap, nodes)]
  transfers between devices with their start and end apart: 1 -> 2, of which waited for: 0 -> 1; matrix products, arithmetic and copies ran while one was open for 5% -> 8% of each run, Pallas kernels for 13% -> 14%
where the time goes in v2:
time: 141 us; the launch traced here: 140 us
  blocking collectives  47.7 us (34%)
  Pallas kernels  46 us (33%)
  waiting for transfers between devices  19.7 us (14%)
  local copies, waits for them, and re-layouts  12.8 us (9%)
  starting transfers between devices  8.45 us (6%)
  other arithmetic  3.62 us (3%)
  matrix products  1.67 us (1%)
    all_to_all x2, blocking collectives, exchange(): return lax.all_to_all(value, AXES, split_axis=0, concat_axis=0, tiled=True)  47.7 us
    pallas_call x1, Pallas kernels, body(): pl.pallas_call(functools.partial(sec_kernel, cap), out_shape=jax.ShapeDty...  22.2 us
    all_to_all x2, waiting for transfers between devices, exchange(): return lax.all_to_all(value, AXES, split_axis=0, concat_axis=0, tiled=True)  19.7 us
    pallas_call x1, Pallas kernels, body(): pl.pallas_call(functools.partial(pri_kernel, cap), out_shape=jax.ShapeDty...  15.2 us
    all_to_all x2, starting transfers between devices, exchange(): return lax.all_to_all(value, AXES, split_axis=0, concat_axis=0, tiled=True)  8.45 us
    another operation x4, local copies, waits for them, and re-layouts, body(): jnp.stack([qx, qy, qz, ones, square, weights, zeros, zeros], axis=1)  6.77 us
    pallas_call x1, Pallas kernels, body(): gather(sec_ids, xc, xu).reshape(devices, 6 * cap, nodes)  4.27 us
    pallas_call x1, Pallas kernels, body(): gather(pri_ids, xc, xu).reshape(devices, 6 * cap, nodes)  4.25 us
  transfers between devices with their start and end apart: 2, of which 1 were waited for; matrix products, arithmetic and copies ran while one was open for 8% of the time, Pallas kernels for 14%

profile of v2, /device:TPU:1, one launch (start us, length us, event | category | flops | bytes accessed | tf_op | source)
XLA Modules:
  0.0 140.0 jit_solution(3718769795872570577)
XLA Ops:
  0.0 0.7 and_select_fusion.2
  0.7 0.2 convert_reduce_fusion.1
  0.9 0.7 and_select_fusion.1
  1.6 0.2 convert_reduce_fusion
  1.8 0.1 select_reduce_fusion
  2.4 21.2 %all_to_all.27 = s32[128,1,8]{2,1,0:T(1,128)S(1)} all-to-all(s32[128,1,8]{2,1,0:T(1,128)S(1)} %bitcast.33), channel_id=1, replica_groups=mesh['gx'=8,'gy'=16] {'gx','gy'}, dimensions={0} | all-to-all | bytes 8192 | tf_op jit(solution)/shard_map/all_to_all | solution.py:177
  23.6 0.7 reshape.52.ids_ref
  24.3 4.3 %shard_map.74 = f32[3072,128]{1,0:T(8,128)} custom-call(s32[512]{0:T(512)} %reshape.52.ids_ref, f32[1152,128]{1,0:T(8,128)} %bitcast.28, f32[1152,128]{1,0:T(8,128)} %bitcast.30), custom_call_target="tpu_custom_call" | custom-call | tf_op jit(solution)/shard_map/pallas_call | solution.py:196
  28.6 4.1 %all-to-all-start.2 = ((f32[128,24,128]{2,1,0:T(8,128)}), f32[128,24,128]{2,1,0:T(8,128)S(1)}, u32[]{:S(2)}, u32[]{:S(2)}) async-start(f32[128,24,128]{2,1,0:T(8,128)} %bitcast.22), calls=%async_computation.2 | async-start | bytes 3145728 | tf_op jit(solution)/shard_map/all_to_all | solution.py:177
  32.8 0.7 eq.83.ids_ref
  33.4 4.3 %shard_map.73 = f32[3072,128]{1,0:T(8,128)} custom-call(s32[512]{0:T(512)} %eq.83.ids_ref, f32[1152,128]{1,0:T(8,128)} %bitcast.29, f32[1152,128]{1,0:T(8,128)} %bitcast.31), custom_call_target="tpu_custom_call" | custom-call | tf_op jit(solution)/shard_map/pallas_call | solution.py:197
  37.7 19.7 %all-to-all-done.2 = f32[128,24,128]{2,1,0:T(8,128)S(1)} async-done(((f32[128,24,128]{2,1,0:T(8,128)}), f32[128,24,128]{2,1,0:T(8,128)S(1)}, u32[]{:S(2)}, u32[]{:S(2)}) %all-to-all-start.2) | async-done | bytes 1572896 | tf_op jit(solution)/shard_map/all_to_all | solution.py:177
  57.4 1.2 copy-done
  58.6 4.3 %all-to-all-start.1 = ((f32[128,24,128]{2,1,0:T(8,128)}), f32[128,24,128]{2,1,0:T(8,128)S(1)}, u32[]{:S(2)}, u32[]{:S(2)}) async-start(f32[128,24,128]{2,1,0:T(8,128)} %bitcast.21), calls=%async_computation.1 | async-start | bytes 3145728 | tf_op jit(solution)/shard_map/all_to_all | solution.py:177
  63.0 1.8 %copy.52 = f32[256,3,256]{2,1,0:T(4,128)S(1)} copy(f32[256,3,256]{2,0,1:T(8,128)} %param.9) | data formatting | bytes 1572864 | tf_op args[2]
  64.8 0.2 stack.10
  65.1 1.4 multiply_add_fusion
  66.5 0.8 stack_broadcast_in_dim.3.clone
  67.5 5.6 %stack.12.points_ref = f32[256,8,256]{2,1,0:T(8,128)} concatenate(f32[256,3,256]{2,1,0:T(4,128)S(1)} %copy.52, f32[256,1,256]{2,1,0:T(1,128)} %stack_broadcast_in_dim.3.clone, f32[256,1,256]{2,1,0:T(1,128)} %multiply_add_fusion, f32[256,1,256]{2,1,0:T(1,128)S(1)} %stack.10, f32[256,2,256]{2,1,0:T(2,128)S(1)} %stack.11), dimensions={1} | concatenate | bytes 4194304 | tf_op jit(solution)/shard_map/stack | solution.py:205
  73.1 15.2 %shard_map.75.other_ref = f32[256,8,256]{2,1,0:T(8,128)} custom-call(s32[256]{0:T(256)} %copy-done.5, f32[3072,128]{1,0:T(8,128)} %bitcast.23, f32[256,8,256]{2,1,0:T(8,128)} %stack.12.points_ref), custom_call_target="tpu_custom_call" | custom-call | tf_op jit(solution)/shard_map/pallas_call | solution.py:211
  88.3 1.2 copy-done.1
  89.5 22.2 %shard_map.76 = f32[1536,128]{1,0:T(8,128)} custom-call(s32[256]{0:T(256)} %copy-done.6, f32[3072,128]{1,0:T(8,128)} %bitcast.24, f32[256,8,256]{2,1,0:T(8,128)} %stack.12.points_ref, f32[256,8,256]{2,1,0:T(8,128)} %shard_map.75.other_ref), custom_call_target="tpu_custom_call" | custom-call | tf_op jit(solution)/shard_map/pallas_call | solution.py:218
  111.7 26.5 %all_to_all.28 = f32[128,3,4,128]{3,2,1,0:T(4,128)S(1)} all-to-all(f32[128,3,4,128]{3,2,1,0:T(4,128)} %bitcast.27), channel_id=1, replica_groups=mesh['gx'=8,'gy'=16] {'gx','gy'}, dimensions={0} | all-to-all | bytes 1572864 | tf_op jit(solution)/shard_map/all_to_all | solution.py:177
  138.4 1.7 %fusion.1 = f32[384,3,128]{2,0,1:T(8,128)} fusion(f32[512,3,128]{2,0,1:T(8,128)S(1)} %bitcast.26, s32[512]{0:T(512)S(1)} %copy-done.4), kind=kOutput, calls=%fused_computation.2 | convolution fusion | flops 906166272 | bytes 1378304 | tf_op jit(solution)/shard_map/bp,pcn->bcn/dot_general | solution.py:228
  (26 shorter events, 1.0 us)
Async XLA Ops:
  0.9 27.7 %copy-start.6 = (s32[256]{0:T(256)}, s32[256]{0:T(256)S(1)}, u32[]{:S(2)}) copy-start(s32[256]{0:T(256)S(1)} %multiply_add_fusion.2.slots_ref) | copy-start | bytes 3076
  1.8 26.8 %copy-start.5 = (s32[256]{0:T(256)}, s32[256]{0:T(256)S(1)}, u32[]{:S(2)}) copy-start(s32[256]{0:T(256)S(1)} %multiply_add_fusion.1.slots_ref) | copy-start | bytes 3076
  28.6 28.8 %all-to-all-start.2 = ((f32[128,24,128]{2,1,0:T(8,128)}), f32[128,24,128]{2,1,0:T(8,128)S(1)}, u32[]{:S(2)}, u32[]{:S(2)}) async-start(f32[128,24,128]{2,1,0:T(8,128)} %bitcast.22), calls=%async_computation.2 | async-start | bytes 3145728 | tf_op jit(solution)/shard_map/all_to_all | solution.py:177
  57.4 1.2 copy-start
  58.6 29.7 %all-to-all-start.1 = ((f32[128,24,128]{2,1,0:T(8,128)}), f32[128,24,128]{2,1,0:T(8,128)S(1)}, u32[]{:S(2)}, u32[]{:S(2)}) async-start(f32[128,24,128]{2,1,0:T(8,128)} %bitcast.21), calls=%async_computation.1 | async-start | bytes 3145728 | tf_op jit(solution)/shard_map/all_to_all | solution.py:177
  62.9 1.8 %copy-start.3 = (f32[256,256]{1,0:T(8,128)S(1)}, f32[256,256]{1,0:T(8,128)}, u32[]{:S(2)}) copy-start(f32[256,256]{1,0:T(8,128)} %param.10) | copy-start | bytes 786436
  62.9 1.8 %copy-start.7 = (s32[256]{0:T(256)S(1)}, s32[256]{0:T(256)}, u32[]{:S(2)}) copy-start(s32[256]{0:T(256)} %param.11) | copy-start | bytes 3076
  62.9 2.1 %copy-start.2 = (f32[256,3,256]{2,0,1:T(8,128)S(1)}, f32[256,3,256]{2,0,1:T(8,128)}, u32[]{:S(2)}) copy-start(f32[256,3,256]{2,0,1:T(8,128)} %param.9) | copy-start | bytes 2359300
  88.3 1.2 copy-start.1
  111.7 26.7 %copy-start.4 = (s32[512]{0:T(512)S(1)}, s32[512]{0:T(512)}, u32[]{:S(2)}) copy-start(s32[512]{0:T(512)} %eq.83.ids_ref) | copy-start | bytes 6148

commit v3 on v2

--- a/solution.py
+++ b/solution.py
@@ -22,20 +22,43 @@
     return (slot_ids, request)
 
 
-def gather_kernel(devices, capacity, blocks, ids_ref, xc_ref, xu_ref, out_ref):
-    rows = 6 * capacity
+def gather_kernel(devices, capacity, blocks, first, ids_ref, xc_ref, xu_ref, out_ref):
+    if first:
+        parts = [(1, rank, rank, capacity) for rank in range(capacity)]
+        parts.append((0, 0, 6 * capacity, 1))
+    else:
+        parts = [(0, rank, rank - 1, capacity - 1) for rank in range(1, capacity)]
+    rows = 6 * len(parts)
 
     def one_device(dev, carry):
-        for rank in range(capacity):
-            local = ids_ref[dev * capacity + rank]
-            base = dev * rows + rank
-            out_ref[pl.ds(base, 3, stride=capacity), :] = xc_ref[pl.ds(local, 3, stride=blocks), :]
-            out_ref[pl.ds(base + 3 * capacity, 3, stride=capacity), :] = xu_ref[
+        for side, rank, start, step in parts:
+            local = ids_ref[dev * (2 * capacity) + side * capacity + rank]
+            base = dev * rows + start
+            out_ref[pl.ds(base, 3, stride=step), :] = xc_ref[pl.ds(local, 3, stride=blocks), :]
+            out_ref[pl.ds(base + 3 * step, 3, stride=step), :] = xu_ref[
                 pl.ds(local, 3, stride=blocks), :
             ]
         return carry
 
     lax.fori_loop(0, devices, one_device, 0, unroll=4)
+
+
+def pack_kernel(points_ref, out_ref):
+    rows = 8
+    segs = points_ref.shape[1]
+    out_ref[...] = jnp.zeros_like(out_ref)
+
+    def one_block(b, carry):
+        here = pl.ds(pl.multiple_of(b * rows, rows), rows)
+        x, y, z = points_ref[0, here], points_ref[1, here], points_ref[2, here]
+        square = 1.0 + 2.0 * (x * x + y * y + z * z)
+        for row, value in enumerate((x, y, z, jnp.ones_like(x), square)):
+            for half in range(x.shape[1] // 128):
+                lanes = slice(half * 128, half * 128 + 128)
+                out_ref[half, pl.ds(b * rows * rows + row, rows, stride=rows), :] = value[:, lanes]
+        return carry
+
+    lax.fori_loop(0, segs // rows, one_block, 0, unroll=2)
 
 
 def pieces(value):
@@ -45,10 +68,8 @@
     return (first, second, rest - second)
 
 
-def node_side(fetched_ref, slot, capacity):
-    dev = slot // capacity
-    rank = slot % capacity
-    raw = fetched_ref[pl.ds(dev * (6 * capacity) + rank, 6, stride=capacity), :]
+def node_side(fetched_ref, start, step):
+    raw = fetched_ref[pl.ds(start, 6, stride=step), :]
     raw = jnp.concatenate([raw, jnp.zeros((2, raw.shape[1]), jnp.float32)], axis=0)
     row = lax.broadcasted_iota(jnp.int32, raw.shape, 0)
     coord = jnp.where(row < 3, raw, 0.0)
@@ -63,6 +84,11 @@
     return stacked.T.astype(jnp.bfloat16), lhs
 
 
+def points_of(points_ref, s):
+    here = pl.ds(pl.multiple_of(s * 8, 8), 8)
+    return jnp.concatenate([points_ref[h, here] for h in range(points_ref.shape[0])], axis=1)
+
+
 def point_side(points):
     a, b, c = pieces(points)
     return jnp.concatenate([a, b, a, b, c, a], axis=0).astype(jnp.bfloat16)
@@ -76,10 +102,10 @@
     return jnp.concatenate([high, low], axis=0)
 
 
-def stage_a(capacity, s, slot, fetched_ref, points_ref, both_ref, lhs_ref, i):
-    node_op, lhs = node_side(fetched_ref, slot, capacity)
+def stage_a(s, start, step, fetched_ref, points_ref, both_ref, lhs_ref, i):
+    node_op, lhs = node_side(fetched_ref, start, step)
     lhs_ref[i] = lhs
-    both_ref[i] = kernel_values(node_op, point_side(points_ref[s]))
+    both_ref[i] = kernel_values(node_op, point_side(points_of(points_ref, s)))
 
 
 def sums_of(both_ref, lhs_ref, i):
@@ -88,10 +114,12 @@
 
 
 def pri_kernel(capacity, slots_ref, fetched_ref, points_ref, out_ref, both_ref, lhs_ref):
-    segs = points_ref.shape[0]
+    segs = slots_ref.shape[0]
 
     def first(s, i):
-        stage_a(capacity, s, slots_ref[s], fetched_ref, points_ref, both_ref, lhs_ref, i)
+        slot = slots_ref[s]
+        start = (slot // capacity) * (6 * capacity + 6) + slot % capacity
+        stage_a(s, start, capacity, fetched_ref, points_ref, both_ref, lhs_ref, i)
 
     def second(s, i):
         sums = sums_of(both_ref, lhs_ref, i)
@@ -114,24 +142,43 @@
     lax.fori_loop(0, segs // (2 * HALF), one_group, 0)
 
 
-def sec_kernel(
-    capacity, slots_ref, fetched_ref, points_ref, other_ref, out_ref, both_ref, lhs_ref, left_ref
-):
-    segs = points_ref.shape[0]
-    out_ref[...] = jnp.zeros_like(out_ref)
-
-    def first(s, i):
-        stage_a(capacity, s, slots_ref[s], fetched_ref, points_ref, both_ref, lhs_ref, i)
-
-    def second(s, i):
+def sec_kernel(early, capacity, *refs):
+    slots_ref, count_ref, order_ref, early_ref, fetched_ref, points_ref, weights_ref, other_ref = refs[:8]
+    if early:
+        out_ref, both_ref, lhs_ref, left_ref = refs[8:]
+        out_ref[...] = jnp.zeros_like(out_ref)
+        low, high_end = 0, early_ref[0]
+    else:
+        before_ref, out_ref, both_ref, lhs_ref, left_ref = refs[8:]
+        out_ref[...] = before_ref[...]
+        low, high_end = early_ref[0], slots_ref.shape[0]
+
+    def segment(place):
+        return order_ref[jnp.minimum(low + place, high_end - 1)]
+
+    def first(place, i):
+        s = segment(place)
+        slot = slots_ref[s]
+        dev, rank = slot // capacity, slot % capacity
+        if early:
+            start, step = dev * (6 * capacity + 6) + 6 * capacity, 1
+        else:
+            start, step = dev * (6 * capacity - 6) + (rank - 1), capacity - 1
+        stage_a(s, start, step, fetched_ref, points_ref, both_ref, lhs_ref, i)
+
+    def second(place, i):
+        s = segment(place)
         sums = sums_of(both_ref, lhs_ref, i)
         inverse = 1.0 / sums[6:7]
-        gap = (points_ref[s, 5:6] * inverse) * (sums * inverse - other_ref[s])
+        weights = weights_ref[pl.ds(s, 1), :]
+        position = lax.broadcasted_iota(jnp.int32, weights.shape, 1)
+        weights = jnp.where(position < count_ref[s], weights, 0.0)
+        gap = (weights * inverse) * (sums * inverse - other_ref[s])
         high = gap.astype(jnp.bfloat16).astype(jnp.float32)
         left_ref[i] = jnp.concatenate([high, gap - high], axis=0).astype(jnp.bfloat16)
 
-    def third(s, i):
-        slot = slots_ref[s]
+    def third(place, i):
+        slot = slots_ref[segment(place)]
         result = lax.dot_general(
             left_ref[i], both_ref[i], (((1,), (1,)), ((), ())), preferred_element_type=jnp.float32
         )
@@ -146,7 +193,6 @@
 
     def one_group(g, carry):
         base = g * (2 * HALF)
-        after = jnp.minimum(base + 2 * HALF, segs - HALF)
         for i in range(HALF):
             second(base + i, i)
             first(base + HALF + i, HALF + i)
@@ -155,10 +201,10 @@
             second(base + HALF + i, HALF + i)
         for i in range(HALF):
             third(base + HALF + i, HALF + i)
-            first(after + i, i)
+            first(base + 2 * HALF + i, i)
         return carry
 
-    lax.fori_loop(0, segs // (2 * HALF), one_group, 0)
+    lax.fori_loop(0, (high_end - low + 2 * HALF - 1) // (2 * HALF), one_group, 0)
 
 
 def body(node_coords, node_disp, qpoints, qweights, qcount, sec_block, pri_block):
@@ -183,45 +229,73 @@
     )
     received = exchange(requests)
     sec_ids = received[:, :cap].reshape(slots)
-    pri_ids = received[:, cap:].reshape(slots)
+    ids = received.reshape(2 * slots)
+
+    is_early = sec_slots % cap == 0
+    early = jnp.sum(is_early.astype(jnp.int32))
+    here = jnp.arange(segs, dtype=jnp.int32)
+    same = (is_early[:, None] == is_early[None, :]) & (here[:, None] > here[None, :])
+    place = jnp.sum(same.astype(jnp.int32), axis=1) + jnp.where(is_early, 0, early)
+    order = jnp.sum(jnp.where(place[:, None] == here[None, :], here[:, None], 0), axis=0)
+    early = early.reshape(1)
 
     xc = jnp.transpose(node_coords, (1, 0, 2)).reshape(3 * blocks, nodes)
     xu = jnp.transpose(node_disp, (1, 0, 2)).reshape(3 * blocks, nodes)
-    gather = pl.pallas_call(
-        functools.partial(gather_kernel, devices, cap, blocks),
-        out_shape=jax.ShapeDtypeStruct((devices * 6 * cap, nodes), f32),
-        in_specs=[smem, vmem, vmem],
-        out_specs=vmem,
-    )
-    pri_in = exchange(gather(pri_ids, xc, xu).reshape(devices, 6 * cap, nodes)).reshape(-1, nodes)
-    sec_in = exchange(gather(sec_ids, xc, xu).reshape(devices, 6 * cap, nodes)).reshape(-1, nodes)
-
-    live = jnp.arange(quad, dtype=jnp.int32)[None, :] < qcount[:, None]
-    weights = jnp.where(live, qweights, jnp.zeros_like(qweights))
-    qx, qy, qz = qpoints[:, 0], qpoints[:, 1], qpoints[:, 2]
-    ones = jnp.ones_like(qx)
-    zeros = jnp.zeros_like(qx)
-    square = 1.0 + 2.0 * (qx * qx + qy * qy + qz * qz)
-    points = jnp.stack([qx, qy, qz, ones, square, weights, zeros, zeros], axis=1)
-
     scratch = [
         pltpu.VMEM((2 * HALF, 2 * nodes, quad), jnp.bfloat16),
         pltpu.VMEM((2 * HALF, 16, 2 * nodes), jnp.bfloat16),
     ]
+
+    limit = pltpu.CompilerParams(vmem_limit_bytes=16 * 1024 * 1024)
+
+    def near(value):
+        return pltpu.with_memory_space_constraint(value, pltpu.VMEM)
+
+    def gather(first, rows):
+        return pl.pallas_call(
+            functools.partial(gather_kernel, devices, cap, blocks, first),
+            out_shape=jax.ShapeDtypeStruct((devices * rows, nodes), f32),
+            in_specs=[smem, vmem, vmem],
+            out_specs=vmem,
+            compiler_params=limit,
+        )(ids, xc, xu).reshape(devices, rows // 2, 2, nodes)
+
+    out1 = gather(True, 6 * cap + 6)
+    out2 = gather(False, 6 * cap - 6)
+    in1 = near(exchange(out1).reshape(-1, nodes))
+    in2 = near(exchange(out2).reshape(-1, nodes))
+    points = pl.pallas_call(
+        pack_kernel,
+        out_shape=pltpu.VMEM((quad // 128, segs * 8, 128), f32),
+        in_specs=[vmem],
+        out_specs=vmem,
+        compiler_params=limit,
+    )(jnp.transpose(qpoints, (1, 0, 2)))
+    points = near(points)
     other = pl.pallas_call(
         functools.partial(pri_kernel, cap),
-        out_shape=jax.ShapeDtypeStruct((segs, 8, quad), f32),
+        out_shape=pltpu.VMEM((segs, 8, quad), f32),
         in_specs=[smem, vmem, vmem],
         out_specs=vmem,
+        compiler_params=limit,
         scratch_shapes=scratch,
-    )(pri_slots, pri_in, points)
-    parcels = pl.pallas_call(
-        functools.partial(sec_kernel, cap),
-        out_shape=jax.ShapeDtypeStruct((devices * 3 * cap, nodes), f32),
-        in_specs=[smem, vmem, vmem, vmem],
-        out_specs=vmem,
-        scratch_shapes=scratch + [pltpu.VMEM((2 * HALF, 16, quad), jnp.bfloat16)],
-    )(sec_slots, sec_in, points, other)
+    )(pri_slots, in1, points)
+
+    def secondary(early_part, *args):
+        return pl.pallas_call(
+            functools.partial(sec_kernel, early_part, cap),
+            out_shape=pltpu.VMEM((devices * 3 * cap, nodes), f32),
+            in_specs=[smem] * 4 + [vmem] * (len(args) - 4),
+            out_specs=vmem,
+            compiler_params=limit,
+            scratch_shapes=scratch + [pltpu.VMEM((2 * HALF, 16, quad), jnp.bfloat16)],
+        )(*args)
+
+    other = near(other)
+    parcels = near(secondary(True, sec_slots, qcount, order, early, in1, points, qweights, other))
+    parcels = secondary(
+        False, sec_slots, qcount, order, early, in2, points, qweights, other, parcels
+    )
     incoming = exchange(parcels.reshape(devices, 3, cap, nodes))
     select = (jnp.arange(blocks, dtype=jnp.int32)[:, None] == sec_ids[None, :]).astype(f32)
     incoming = jnp.transpose(incoming, (0, 2, 1, 3)).reshape(slots, 3, nodes)

time: 141 us -> 142 us (level)
  blocking collectives: 47.7 us -> 21.2 us
  waiting for transfers between devices: 19.7 us -> 41.2 us
  starting transfers between devices: 8.45 us -> 18.8 us
  Pallas kernels: 46 us -> 41.4 us
    all_to_all x2 -> x1, blocking collectives: 47.7 us -> 21.2 us  [exchange(): return lax.all_to_all(value, AXES, split_axis=0, concat_axis=0, tiled=True)]
    all_to_all x2 -> x3, waiting for transfers between devices: 19.7 us -> 41.2 us  [exchange(): return lax.all_to_all(value, AXES, split_axis=0, concat_axis=0, tiled=True)]
    all_to_all x2 -> x3, starting transfers between devices: 8.45 us -> 18.8 us  [exchange(): return lax.all_to_all(value, AXES, split_axis=0, concat_axis=0, tiled=True)]
    another operation x4 -> x0, local copies, waits for them, and re-layouts: 6.77 us -> none  [body(): jnp.stack([qx, qy, qz, ones, square, weights, zeros, zeros], axis=1)]
    unnamed x17 -> x32, local copies, waits for them, and re-layouts: 4.16 us -> 10.6 us
    pallas_call x4 -> x6, Pallas kernels: 46 us -> 41.4 us  [the longest x2 22.8 us: secondary(): pl.pallas_call(functools.partial(sec_kernel, early_part, cap), out_shape=...]
  transfers between devices with their start and end apart: 2 -> 3, of which waited for: 1 -> 2; matrix products, arithmetic and copies ran while one was open for 8% -> 1% of each run, Pallas kernels for 14% -> 19%
where the time goes in v3:
time: 142 us; the launch traced here: 141 us
  Pallas kernels  41.4 us (29%)
  waiting for transfers between devices  41.2 us (29%)
  blocking collectives  21.2 us (15%)
  starting transfers between devices  18.8 us (13%)
  local copies, waits for them, and re-layouts  12.6 us (9%)
  other arithmetic  4.43 us (3%)
  matrix products  1.67 us (1%)
    all_to_all x3, waiting for transfers between devices, exchange(): return lax.all_to_all(value, AXES, split_axis=0, concat_axis=0, tiled=True)  41.2 us
    pallas_call x2, Pallas kernels, secondary(): pl.pallas_call(functools.partial(sec_kernel, early_part, cap), out_shape=...  22.8 us
    all_to_all x1, blocking collectives, exchange(): return lax.all_to_all(value, AXES, split_axis=0, concat_axis=0, tiled=True)  21.2 us
    all_to_all x3, starting transfers between devices, exchange(): return lax.all_to_all(value, AXES, split_axis=0, concat_axis=0, tiled=True)  18.8 us
    pallas_call x1, Pallas kernels, body(): pl.pallas_call(functools.partial(pri_kernel, cap), out_shape=pltpu.VMEM((...  12.3 us
    unnamed x32, local copies, waits for them, and re-layouts  10.6 us
    pallas_call x2, Pallas kernels, gather(): pl.pallas_call(functools.partial(gather_kernel, devices, cap, blocks, fir...  5.93 us
  transfers between devices with their start and end apart: 3, of which 2 were waited for; matrix products, arithmetic and copies ran while one was open for 1% of the time, Pallas kernels for 19%

profile of v3, /device:TPU:1, one launch (start us, length us, event | category | flops | bytes accessed | tf_op | source)
XLA Modules:
  0.0 141.5 jit_solution(7646893013985629740)
XLA Ops:
  1.8 0.7 and_select_fusion.2
  3.0 21.2 %all_to_all.27 = s32[128,1,8]{2,1,0:T(1,128)S(1)} all-to-all(s32[128,1,8]{2,1,0:T(1,128)S(1)} %bitcast.37), channel_id=1, replica_groups=mesh['gx'=8,'gy'=16] {'gx','gy'}, dimensions={0} | all-to-all | bytes 8192 | tf_op jit(solution)/shard_map/all_to_all | solution.py:223
  24.7 0.8 reduce.3
  25.6 1.1 copy-done.8
  26.7 1.1 copy-done.10
  27.7 2.9 %shard_map.75 = f32[3840,128]{1,0:T(8,128)S(1)} custom-call(s32[1024]{0:T(1024)S(1)} %reshape.54.ids_ref, f32[1152,128]{1,0:T(8,128)S(1)} %bitcast.29, f32[1152,128]{1,0:T(8,128)S(1)} %bitcast.31), custom_call_target="tpu_custom_call" | custom-call | tf_op jit(solution)/shard_map/pallas_call | solution.py:255
  30.6 1.3 copy-done.4
  31.9 4.2 %all-to-all-start.2 = ((f32[128,15,2,128]{3,2,1,0:T(2,128)}), f32[128,15,2,128]{3,2,1,0:T(2,128)S(1)}, u32[]{:S(2)}, u32[]{:S(2)}) async-start(f32[128,15,2,128]{3,2,1,0:T(2,128)} %bitcast.26), calls=%async_computation.2 | async-start | bytes 3932160 | tf_op jit(solution)/shard_map/all_to_all | solution.py:223
  36.1 3.1 %shard_map.73 = f32[2304,128]{1,0:T(8,128)} custom-call(s32[1024]{0:T(1024)S(1)} %reshape.54.ids_ref, f32[1152,128]{1,0:T(8,128)S(1)} %bitcast.30, f32[1152,128]{1,0:T(8,128)S(1)} %bitcast.32), custom_call_target="tpu_custom_call" | custom-call | tf_op jit(solution)/shard_map/pallas_call | solution.py:255
  39.2 25.6 %all-to-all-done.2 = f32[128,15,2,128]{3,2,1,0:T(2,128)S(1)} async-done(((f32[128,15,2,128]{3,2,1,0:T(2,128)}), f32[128,15,2,128]{3,2,1,0:T(2,128)S(1)}, u32[]{:S(2)}, u32[]{:S(2)}) %all-to-all-start.2) | async-done | bytes 1966112 | tf_op jit(solution)/shard_map/all_to_all | solution.py:223
  64.8 4.7 %all-to-all-start.1 = ((f32[128,9,2,128]{3,2,1,0:T(2,128)}), f32[128,9,2,128]{3,2,1,0:T(2,128)S(1)}, u32[]{:S(2)}, u32[]{:S(2)}) async-start(f32[128,9,2,128]{3,2,1,0:T(2,128)} %bitcast.9), calls=%async_computation.1 | async-start | bytes 2359296 | tf_op jit(solution)/shard_map/all_to_all | solution.py:223
  69.6 1.1 copy-done.13
  72.2 12.3 %shard_map.76.refs_7_ = f32[256,8,256]{2,1,0:T(8,128)S(1)} custom-call(s32[256]{0:T(256)S(1)} %multiply_add_fusion.slots_ref, f32[3840,128]{1,0:T(8,128)S(1)} %bitcast.24, f32[2,2048,128]{2,1,0:T(8,128)S(1)} %shard_map.74.points_ref.refs_5_), custom_call_target="tpu_custom_call" | custom-call | tf_op jit(solution)/shard_map/pallas_call | solution.py:275
  84.5 10.8 %shard_map.77.refs_8_ = f32[1536,128]{1,0:T(8,128)S(1)} custom-call(s32[256]{0:T(256)S(1)} %get-tuple-element.7.refs_0_, s32[256]{0:T(256)S(1)} %copy-done.14, s32[256]{0:T(256)S(1)} %select_reduce_fusion.2.refs_2_, s32[1]{0:T(128)} %bitcast.4.refs_3_, f32[3840,128]{1,0:T(8,128)S(1)} %bitcast.25, f32[2,2048,128]{2,1,0:T(8,128)S(1)} %shard_map.74.points_ref.refs_5_, ...), custom_call_target="tpu_custom_call" | custom-call | tf_op jit(solution)/shard_map/pallas_call | solution.py:285
  95.4 1.3 copy-done
  96.7 0.9 copy-done.5
  97.6 1.6 %copy-done.1 = f32[256,8,256]{2,1,0:T(8,128)S(1)} copy-done((f32[256,8,256]{2,1,0:T(8,128)S(1)}, f32[256,8,256]{2,1,0:T(8,128)}, u32[]{:S(2)}) %copy-start.1) | copy-done | bytes 2097176
  99.2 1.1 copy-done.6
  100.3 12.0 %shard_map.78 = f32[1536,128]{1,0:T(8,128)S(1)} custom-call(s32[256]{0:T(256)S(1)} %get-tuple-element.7.refs_0_, s32[256]{0:T(256)S(1)} %copy-done.14, s32[256]{0:T(256)S(1)} %select_reduce_fusion.2.refs_2_, s32[1]{0:T(128)} %bitcast.4.refs_3_, f32[2304,128]{1,0:T(8,128)S(1)} %bitcast.27, f32[2,2048,128]{2,1,0:T(8,128)S(1)} %shard_map.74.points_ref.refs_5_, ...), custom_call_target="tpu_custom_call" | custom-call | tf_op jit(solution)/shard_map/pallas_call | solution.py:285
  112.3 0.9 copy-done.7
  113.2 9.9 %all-to-all-start.3 = ((f32[128,3,4,128]{3,2,1,0:T(4,128)}), f32[128,3,4,128]{3,2,1,0:T(4,128)S(1)}, u32[]{:S(2)}, u32[]{:S(2)}) async-start(f32[128,3,4,128]{3,2,1,0:T(4,128)} %bitcast.28), calls=%async_computation.3 | async-start | bytes 1572864 | tf_op jit(solution)/shard_map/all_to_all | solution.py:223
  123.1 0.9 eq.112
  124.0 15.7 %all-to-all-done.3 = f32[128,3,4,128]{3,2,1,0:T(4,128)S(1)} async-done(((f32[128,3,4,128]{3,2,1,0:T(4,128)}), f32[128,3,4,128]{3,2,1,0:T(4,128)S(1)}, u32[]{:S(2)}, u32[]{:S(2)}) %all-to-all-start.3) | async-done | bytes 786464 | tf_op jit(solution)/shard_map/all_to_all | solution.py:223
  139.8 1.7 %fusion.1 = f32[384,3,128]{2,0,1:T(8,128)} fusion(f32[512,3,128]{2,0,1:T(8,128)S(1)} %bitcast.35, s32[512]{0:T(512)S(1)} %eq.112), kind=kOutput, calls=%fused_computation.2 | convolution fusion | flops 906166272 | bytes 1378304 | tf_op jit(solution)/shard_map/bp,pcn->bcn/dot_general | solution.py:302
  (41 shorter events, 4.6 us)
Async XLA Ops:
  24.2 6.5 %copy-start.15 = (s32[128,1,8]{2,1,0:T(1,128)}, s32[128,1,8]{2,1,0:T(1,128)S(1)}, u32[]{:S(2)}) copy-start(s32[128,1,8]{2,1,0:T(1,128)S(1)} %all_to_all.27) | copy-start | bytes 12292
  25.6 1.1 copy-start.8
  26.7 1.1 copy-start.10
  30.6 1.3 copy-start.4
  31.9 4.2 %copy-start.9 = (f32[384,3,128]{2,0,1:T(8,128)S(1)}, f32[384,3,128]{2,0,1:T(8,128)}, u32[]{:S(2)}) copy-start(f32[384,3,128]{2,0,1:T(8,128)} %param.7) | copy-start | bytes 1769476
  31.9 4.2 %copy-start.11 = (f32[384,3,128]{2,0,1:T(8,128)S(1)}, f32[384,3,128]{2,0,1:T(8,128)}, u32[]{:S(2)}) copy-start(f32[384,3,128]{2,0,1:T(8,128)} %param.8) | copy-start | bytes 1769476
  31.9 32.9 %all-to-all-start.2 = ((f32[128,15,2,128]{3,2,1,0:T(2,128)}), f32[128,15,2,128]{3,2,1,0:T(2,128)S(1)}, u32[]{:S(2)}, u32[]{:S(2)}) async-start(f32[128,15,2,128]{3,2,1,0:T(2,128)} %bitcast.26), calls=%async_computation.2 | async-start | bytes 3932160 | tf_op jit(solution)/shard_map/all_to_all | solution.py:223
  64.8 4.8 %copy-start.2 = (f32[128,15,2,128]{3,2,1,0:T(2,128)}, f32[128,15,2,128]{3,2,1,0:T(2,128)S(1)}, u32[]{:S(2)}) copy-start(f32[128,15,2,128]{3,2,1,0:T(2,128)S(1)} %all-to-all-done.2) | copy-start | bytes 5898244
  64.8 32.8 %all-to-all-start.1 = ((f32[128,9,2,128]{3,2,1,0:T(2,128)}), f32[128,9,2,128]{3,2,1,0:T(2,128)S(1)}, u32[]{:S(2)}, u32[]{:S(2)}) async-start(f32[128,9,2,128]{3,2,1,0:T(2,128)} %bitcast.9), calls=%async_computation.1 | async-start | bytes 2359296 | tf_op jit(solution)/shard_map/all_to_all | solution.py:223
  69.5 1.1 copy-start.13
  70.7 1.5 %copy-start.3 = (f32[128,15,2,128]{3,2,1,0:T(2,128)S(1)}, f32[128,15,2,128]{3,2,1,0:T(2,128)}, u32[]{:S(2)}) copy-start(f32[128,15,2,128]{3,2,1,0:T(2,128)} %copy-done.2) | copy-start | bytes 5898244
  72.2 12.3 %copy-start.12 = (f32[256,256]{1,0:T(8,128)S(1)}, f32[256,256]{1,0:T(8,128)}, u32[]{:S(2)}) copy-start(f32[256,256]{1,0:T(8,128)} %refs_6_.3) | copy-start | bytes 786436
  72.2 12.3 %copy-start.14 = (s32[256]{0:T(256)S(1)}, s32[256]{0:T(256)}, u32[]{:S(2)}) copy-start(s32[256]{0:T(256)} %refs_1_.3) | copy-start | bytes 3076
  95.3 1.3 copy-start
  96.7 0.9 copy-start.5
  97.6 1.6 %copy-start.1 = (f32[256,8,256]{2,1,0:T(8,128)S(1)}, f32[256,8,256]{2,1,0:T(8,128)}, u32[]{:S(2)}) copy-start(f32[256,8,256]{2,1,0:T(8,128)} %copy-done) | copy-start | bytes 6291460
  99.2 1.1 copy-start.6
  112.3 0.9 copy-start.7
  113.2 26.5 %all-to-all-start.3 = ((f32[128,3,4,128]{3,2,1,0:T(4,128)}), f32[128,3,4,128]{3,2,1,0:T(4,128)S(1)}, u32[]{:S(2)}, u32[]{:S(2)}) async-start(f32[128,3,4,128]{3,2,1,0:T(4,128)} %bitcast.28), calls=%async_computation.3 | async-start | bytes 1572864 | tf_op jit(solution)/shard_map/all_to_all | solution.py:223

commit v4 on v3

--- a/solution.py
+++ b/solution.py
@@ -8,6 +8,7 @@
 
 AXES = ("gx", "gy")
 HALF = 8
+WIDE = 16
 
 
 def routing(block_ids, blocks_dev, capacity, slot_count):
@@ -22,7 +23,13 @@
     return (slot_ids, request)
 
 
-def gather_kernel(devices, capacity, blocks, first, ids_ref, xc_ref, xu_ref, out_ref):
+def table_kernel(xc_ref, xu_ref, out_ref):
+    half = xc_ref.shape[0]
+    out_ref[:half] = xc_ref[...]
+    out_ref[half:] = xu_ref[...]
+
+
+def gather_kernel(devices, capacity, blocks, first, ids_ref, table_ref, out_ref):
     if first:
         parts = [(1, rank, rank, capacity) for rank in range(capacity)]
         parts.append((0, 0, 6 * capacity, 1))
@@ -33,10 +40,8 @@
     def one_device(dev, carry):
         for side, rank, start, step in parts:
             local = ids_ref[dev * (2 * capacity) + side * capacity + rank]
-            base = dev * rows + start
-            out_ref[pl.ds(base, 3, stride=step), :] = xc_ref[pl.ds(local, 3, stride=blocks), :]
-            out_ref[pl.ds(base + 3 * step, 3, stride=step), :] = xu_ref[
-                pl.ds(local, 3, stride=blocks), :
+            out_ref[pl.ds(dev * rows + start, 6, stride=step), :] = table_ref[
+                pl.ds(local, 6, stride=blocks), :
             ]
         return carry
 
@@ -125,33 +130,37 @@
         sums = sums_of(both_ref, lhs_ref, i)
         out_ref[s] = sums * (1.0 / sums[6:7])
 
-    for i in range(HALF):
+    for i in range(WIDE):
         first(i, i)
 
     def one_group(g, carry):
-        base = g * (2 * HALF)
-        after = jnp.minimum(base + 2 * HALF, segs - HALF)
-        for i in range(HALF):
+        base = g * (2 * WIDE)
+        after = jnp.minimum(base + 2 * WIDE, segs - WIDE)
+        for i in range(WIDE):
             second(base + i, i)
-            first(base + HALF + i, HALF + i)
-        for i in range(HALF):
-            second(base + HALF + i, HALF + i)
+            first(base + WIDE + i, WIDE + i)
+        for i in range(WIDE):
+            second(base + WIDE + i, WIDE + i)
             first(after + i, i)
         return carry
 
-    lax.fori_loop(0, segs // (2 * HALF), one_group, 0)
+    lax.fori_loop(0, segs // (2 * WIDE), one_group, 0)
 
 
 def sec_kernel(early, capacity, *refs):
-    slots_ref, count_ref, order_ref, early_ref, fetched_ref, points_ref, weights_ref, other_ref = refs[:8]
+    slots_ref, count_ref, order_ref, early_ref, fetched_ref, points_ref, weights_ref = refs[:7]
     if early:
-        out_ref, both_ref, lhs_ref, left_ref = refs[8:]
+        far_ref, out_ref, both_ref, lhs_ref, left_ref, other_ref, sems = refs[7:]
         out_ref[...] = jnp.zeros_like(out_ref)
         low, high_end = 0, early_ref[0]
+        copies = []
     else:
-        before_ref, out_ref, both_ref, lhs_ref, left_ref = refs[8:]
-        out_ref[...] = before_ref[...]
+        far_ref, before_ref, out_ref, both_ref, lhs_ref, left_ref, other_ref, sems = refs[7:]
         low, high_end = early_ref[0], slots_ref.shape[0]
+        copies = [pltpu.make_async_copy(before_ref, out_ref, sems.at[1])]
+    copies.append(pltpu.make_async_copy(far_ref, other_ref, sems.at[0]))
+    for copy in copies:
+        copy.start()
 
     def segment(place):
         return order_ref[jnp.minimum(low + place, high_end - 1)]
@@ -179,17 +188,27 @@
 
     def third(place, i):
         slot = slots_ref[segment(place)]
-        result = lax.dot_general(
-            left_ref[i], both_ref[i], (((1,), (1,)), ((), ())), preferred_element_type=jnp.float32
-        )
-        half = result.shape[1] // 2
-        result = result[:8] + result[8:]
-        result = result[:, :half] + result[:, half:]
+        left, both = left_ref[i], both_ref[i]
+        half = both.shape[0] // 2
+        if i % 2 == 0:
+            result = lax.dot_general(
+                left, both, (((1,), (1,)), ((), ())), preferred_element_type=jnp.float32
+            )
+            result = result[:8] + result[8:]
+            result = result[:, :half] + result[:, half:]
+        else:
+            result = lax.dot_general(
+                both, left, (((1,), (1,)), ((), ())), preferred_element_type=jnp.float32
+            )
+            result = (result[:half] + result[half:]).T
+            result = result[:8] + result[8:]
         base = (slot // capacity) * (3 * capacity) + slot % capacity
         out_ref[pl.ds(base, 3, stride=capacity), :] = result[3:6]
 
     for i in range(HALF):
         first(i, i)
+    for copy in copies:
+        copy.wait()
 
     def one_group(g, carry):
         base = g * (2 * HALF)
@@ -219,11 +238,29 @@
     smem = pl.BlockSpec(memory_space=pltpu.SMEM)
     vmem = pl.BlockSpec(memory_space=pltpu.VMEM)
 
+    limit = pltpu.CompilerParams(vmem_limit_bytes=16 * 1024 * 1024)
+
+    def near(value):
+        return pltpu.with_memory_space_constraint(value, pltpu.VMEM)
+
+    def far(value):
+        return pltpu.with_memory_space_constraint(value, pltpu.HBM)
+
     def exchange(value):
         return lax.all_to_all(value, AXES, split_axis=0, concat_axis=0, tiled=True)
 
     sec_slots, sec_request = routing(sec_block, blocks, cap, slots)
     pri_slots, pri_request = routing(pri_block, blocks, cap, slots)
+    xc = jnp.transpose(node_coords, (1, 0, 2)).reshape(3 * blocks, nodes)
+    xu = jnp.transpose(node_disp, (1, 0, 2)).reshape(3 * blocks, nodes)
+    hbm = pl.BlockSpec(memory_space=pltpu.HBM)
+    table = pl.pallas_call(
+        table_kernel,
+        out_shape=pltpu.VMEM((6 * blocks, nodes), f32),
+        in_specs=[vmem, vmem],
+        out_specs=vmem,
+        compiler_params=limit,
+    )(far(xc), far(xu))
     requests = jnp.concatenate(
         [sec_request.reshape(devices, cap), pri_request.reshape(devices, cap)], axis=1
     )
@@ -239,26 +276,20 @@
     order = jnp.sum(jnp.where(place[:, None] == here[None, :], here[:, None], 0), axis=0)
     early = early.reshape(1)
 
-    xc = jnp.transpose(node_coords, (1, 0, 2)).reshape(3 * blocks, nodes)
-    xu = jnp.transpose(node_disp, (1, 0, 2)).reshape(3 * blocks, nodes)
-    scratch = [
-        pltpu.VMEM((2 * HALF, 2 * nodes, quad), jnp.bfloat16),
-        pltpu.VMEM((2 * HALF, 16, 2 * nodes), jnp.bfloat16),
-    ]
-
-    limit = pltpu.CompilerParams(vmem_limit_bytes=16 * 1024 * 1024)
-
-    def near(value):
-        return pltpu.with_memory_space_constraint(value, pltpu.VMEM)
+    def scratch(count):
+        return [
+            pltpu.VMEM((2 * count, 2 * nodes, quad), jnp.bfloat16),
+            pltpu.VMEM((2 * count, 16, 2 * nodes), jnp.bfloat16),
+        ]
 
     def gather(first, rows):
         return pl.pallas_call(
             functools.partial(gather_kernel, devices, cap, blocks, first),
-            out_shape=jax.ShapeDtypeStruct((devices * rows, nodes), f32),
-            in_specs=[smem, vmem, vmem],
+            out_shape=pltpu.HBM((devices * rows, nodes), f32),
+            in_specs=[smem, vmem],
             out_specs=vmem,
             compiler_params=limit,
-        )(ids, xc, xu).reshape(devices, rows // 2, 2, nodes)
+        )(ids, near(table)).reshape(devices, rows // 2, 2, nodes)
 
     out1 = gather(True, 6 * cap + 6)
     out2 = gather(False, 6 * cap - 6)
@@ -274,25 +305,31 @@
     points = near(points)
     other = pl.pallas_call(
         functools.partial(pri_kernel, cap),
-        out_shape=pltpu.VMEM((segs, 8, quad), f32),
+        out_shape=pltpu.HBM((segs, 8, quad), f32),
         in_specs=[smem, vmem, vmem],
         out_specs=vmem,
         compiler_params=limit,
-        scratch_shapes=scratch,
+        scratch_shapes=scratch(WIDE),
     )(pri_slots, in1, points)
 
     def secondary(early_part, *args):
         return pl.pallas_call(
             functools.partial(sec_kernel, early_part, cap),
-            out_shape=pltpu.VMEM((devices * 3 * cap, nodes), f32),
-            in_specs=[smem] * 4 + [vmem] * (len(args) - 4),
+            out_shape=pltpu.HBM((devices * 3 * cap, nodes), f32),
+            in_specs=[smem] * 4 + [vmem] * 3 + [hbm] * (len(args) - 7),
             out_specs=vmem,
             compiler_params=limit,
-            scratch_shapes=scratch + [pltpu.VMEM((2 * HALF, 16, quad), jnp.bfloat16)],
+            scratch_shapes=scratch(HALF)
+            + [
+                pltpu.VMEM((2 * HALF, 16, quad), jnp.bfloat16),
+                pltpu.VMEM((segs, 8, quad), f32),
+                pltpu.SemaphoreType.DMA((2,)),
+            ],
         )(*args)
 
-    other = near(other)
-    parcels = near(secondary(True, sec_slots, qcount, order, early, in1, points, qweights, other))
+    other = far(other)
+    parcels = secondary(True, sec_slots, qcount, order, early, in1, points, qweights, other)
+    parcels = far(parcels)
     parcels = secondary(
         False, sec_slots, qcount, order, early, in2, points, qweights, other, parcels
     )

time: 142 us -> 138 us (0.972)
  blocking collectives: 21.2 us -> 0 us
  starting transfers between devices: 18.8 us -> 30.3 us
  local copies, waits for them, and re-layouts: 12.6 us -> 3.32 us
  waiting for transfers between devices: 41.2 us -> 49.6 us
  Pallas kernels: 41.4 us -> 47 us
    all_to_all x1 -> x0, blocking collectives: 21.2 us -> none  [exchange(): return lax.all_to_all(value, AXES, split_axis=0, concat_axis=0, tiled=True)]
    all_to_all x3 -> x4, starting transfers between devices: 18.8 us -> 30.3 us  [exchange(): return lax.all_to_all(value, AXES, split_axis=0, concat_axis=0, tiled=True)]
    unnamed x32 -> x12, local copies, waits for them, and re-layouts: 10.6 us -> 1.32 us
    all_to_all x3 -> x4, waiting for transfers between devices: 41.2 us -> 49.6 us  [exchange(): return lax.all_to_all(value, AXES, split_axis=0, concat_axis=0, tiled=True)]
    pallas_call x2, Pallas kernels: 22.8 us -> 25.6 us  [secondary(): pl.pallas_call(functools.partial(sec_kernel, early_part, cap), out_shape=...]
    pallas_call x1 -> x2, Pallas kernels: 12.3 us -> 13.7 us  [the longest x1 12.4 us: body(): pl.pallas_call(functools.partial(pri_kernel, cap), out_shape=pltpu.HBM((s...]
  transfers between devices with their start and end apart: 3 -> 4, of which waited for: 2 -> 3; matrix products, arithmetic and copies ran while one was open for 1% -> 1% of each run, Pallas kernels for 19% -> 21%
where the time goes in v4:
time: 138 us; the launch traced here: 137 us
  waiting for transfers between devices  49.6 us (36%)
  Pallas kernels  47 us (34%)
  starting transfers between devices  30.3 us (22%)
  other arithmetic  5.3 us (4%)
  local copies, waits for them, and re-layouts  3.32 us (2%)
  matrix products  1.67 us (1%)
    all_to_all x4, waiting for transfers between devices, exchange(): return lax.all_to_all(value, AXES, split_axis=0, concat_axis=0, tiled=True)  49.6 us
    all_to_all x4, starting transfers between devices, exchange(): return lax.all_to_all(value, AXES, split_axis=0, concat_axis=0, tiled=True)  30.3 us
    pallas_call x2, Pallas kernels, secondary(): pl.pallas_call(functools.partial(sec_kernel, early_part, cap), out_shape=...  25.6 us
    pallas_call x1, Pallas kernels, body(): pl.pallas_call(functools.partial(pri_kernel, cap), out_shape=pltpu.HBM((s...  12.4 us
    pallas_call x2, Pallas kernels, gather(): pl.pallas_call(functools.partial(gather_kernel, devices, cap, blocks, fir...  7.28 us
  transfers between devices with their start and end apart: 4, of which 3 were waited for; matrix products, arithmetic and copies ran while one was open for 1% of the time, Pallas kernels for 21%

profile of v4, /device:TPU:1, one launch (start us, length us, event | category | flops | bytes accessed | tf_op | source)
XLA Modules:
  0.0 137.3 jit_solution(15903221996050254814)
XLA Ops:
  0.0 0.7 and_select_fusion.3
  0.9 0.7 convert_reduce_fusion.3
  1.6 0.7 and_select_fusion.2
  3.0 0.7 pad_add_fusion
  3.7 11.5 %all-to-all-start = ((s32[128,1,8]{2,1,0:T(1,128)}), s32[128,1,8]{2,1,0:T(1,128)S(1)}, u32[]{:S(2)}, u32[]{:S(2)}) async-start(s32[128,1,8]{2,1,0:T(1,128)} %bitcast.1), calls=%async_computation | async-start | bytes 131072 | tf_op jit(solution)/shard_map/all_to_all | solution.py:250
  15.2 1.3 shard_map.73.table_ref
  16.5 8.5 %all-to-all-done = s32[128,1,8]{2,1,0:T(1,128)S(1)} async-done(((s32[128,1,8]{2,1,0:T(1,128)}), s32[128,1,8]{2,1,0:T(1,128)S(1)}, u32[]{:S(2)}, u32[]{:S(2)}) %all-to-all-start) | async-done | bytes 4128 | tf_op jit(solution)/shard_map/all_to_all | solution.py:250
  25.0 0.6 broadcast.29
  25.6 0.8 reduce.3
  26.6 4.2 %shard_map.76 = f32[3840,128]{1,0:T(8,128)} custom-call(s32[1024]{0:T(1024)S(1)} %reshape.54.ids_ref, f32[2304,128]{1,0:T(8,128)S(1)} %shard_map.73.table_ref), custom_call_target="tpu_custom_call" | custom-call | tf_op jit(solution)/shard_map/pallas_call | solution.py:286
  30.7 4.1 %all-to-all-start.2 = ((f32[128,15,2,128]{3,2,1,0:T(2,128)}), f32[128,15,2,128]{3,2,1,0:T(2,128)S(1)}, u32[]{:S(2)}, u32[]{:S(2)}) async-start(f32[128,15,2,128]{3,2,1,0:T(2,128)} %bitcast.28), calls=%async_computation.2 | async-start | bytes 3932160 | tf_op jit(solution)/shard_map/all_to_all | solution.py:250
  34.9 3.1 %shard_map.74 = f32[2304,128]{1,0:T(8,128)} custom-call(s32[1024]{0:T(1024)S(1)} %reshape.54.ids_ref, f32[2304,128]{1,0:T(8,128)S(1)} %shard_map.73.table_ref), custom_call_target="tpu_custom_call" | custom-call | tf_op jit(solution)/shard_map/pallas_call | solution.py:286
  38.0 25.5 %all-to-all-done.2 = f32[128,15,2,128]{3,2,1,0:T(2,128)S(1)} async-done(((f32[128,15,2,128]{3,2,1,0:T(2,128)}), f32[128,15,2,128]{3,2,1,0:T(2,128)S(1)}, u32[]{:S(2)}, u32[]{:S(2)}) %all-to-all-start.2) | async-done | bytes 1966112 | tf_op jit(solution)/shard_map/all_to_all | solution.py:250
  63.5 4.7 %all-to-all-start.1 = ((f32[128,9,2,128]{3,2,1,0:T(2,128)}), f32[128,9,2,128]{3,2,1,0:T(2,128)S(1)}, u32[]{:S(2)}, u32[]{:S(2)}) async-start(f32[128,9,2,128]{3,2,1,0:T(2,128)} %bitcast.29), calls=%async_computation.1 | async-start | bytes 2359296 | tf_op jit(solution)/shard_map/all_to_all | solution.py:250
  68.2 1.1 copy-done.3
  69.4 0.4 shard_map.75.points_ref.refs_5_
  69.9 0.7 select_add_fusion
  70.9 12.4 %shard_map.77.refs_7_ = f32[256,8,256]{2,1,0:T(8,128)} custom-call(s32[256]{0:T(256)S(1)} %multiply_add_fusion.slots_ref, f32[3840,128]{1,0:T(8,128)S(1)} %bitcast.24, f32[2,2048,128]{2,1,0:T(8,128)S(1)} %shard_map.75.points_ref.refs_5_), custom_call_target="tpu_custom_call" | custom-call | tf_op jit(solution)/shard_map/pallas_call | solution.py:306
  83.3 12.2 %shard_map.78.refs_8_ = f32[1536,128]{1,0:T(8,128)} custom-call(s32[256]{0:T(256)S(1)} %get-tuple-element.7.refs_0_, s32[256]{0:T(256)S(1)} %copy-done.4, s32[256]{0:T(256)S(1)} %select_reduce_fusion.2.refs_2_, s32[1]{0:T(128)} %bitcast.4.refs_3_, f32[3840,128]{1,0:T(8,128)S(1)} %bitcast.25, f32[2,2048,128]{2,1,0:T(8,128)S(1)} %shard_map.75.points_ref.refs_5_, ...), custom_call_target="tpu_custom_call" | custom-call | tf_op jit(solution)/shard_map/pallas_call | solution.py:316
  95.5 13.5 %shard_map.79 = f32[1536,128]{1,0:T(8,128)} custom-call(s32[256]{0:T(256)S(1)} %get-tuple-element.7.refs_0_, s32[256]{0:T(256)S(1)} %copy-done.4, s32[256]{0:T(256)S(1)} %select_reduce_fusion.2.refs_2_, s32[1]{0:T(128)} %bitcast.4.refs_3_, f32[2304,128]{1,0:T(8,128)S(1)} %bitcast.26, f32[2,2048,128]{2,1,0:T(8,128)S(1)} %shard_map.75.points_ref.refs_5_, ...), custom_call_target="tpu_custom_call" | custom-call | tf_op jit(solution)/shard_map/pallas_call | solution.py:316
  109.0 9.9 %all-to-all-start.3 = ((f32[128,3,4,128]{3,2,1,0:T(4,128)}), f32[128,3,4,128]{3,2,1,0:T(4,128)S(1)}, u32[]{:S(2)}, u32[]{:S(2)}) async-start(f32[128,3,4,128]{3,2,1,0:T(4,128)} %bitcast.30), calls=%async_computation.3 | async-start | bytes 1572864 | tf_op jit(solution)/shard_map/all_to_all | solution.py:250
  118.9 0.9 eq.112
  119.8 15.7 %all-to-all-done.3 = f32[128,3,4,128]{3,2,1,0:T(4,128)S(1)} async-done(((f32[128,3,4,128]{3,2,1,0:T(4,128)}), f32[128,3,4,128]{3,2,1,0:T(4,128)S(1)}, u32[]{:S(2)}, u32[]{:S(2)}) %all-to-all-start.3) | async-done | bytes 786464 | tf_op jit(solution)/shard_map/all_to_all | solution.py:250
  135.6 1.7 %fusion.1 = f32[384,3,128]{2,0,1:T(8,128)} fusion(f32[512,3,128]{2,0,1:T(8,128)S(1)} %bitcast.32, s32[512]{0:T(512)S(1)} %eq.112), kind=kOutput, calls=%fused_computation.2 | convolution fusion | flops 906166272 | bytes 1378304 | tf_op jit(solution)/shard_map/bp,pcn->bcn/dot_general | solution.py:339
  (23 shorter events, 1.6 us)
Async XLA Ops:
  3.7 21.3 %all-to-all-start = ((s32[128,1,8]{2,1,0:T(1,128)}), s32[128,1,8]{2,1,0:T(1,128)S(1)}, u32[]{:S(2)}, u32[]{:S(2)}) async-start(s32[128,1,8]{2,1,0:T(1,128)} %bitcast.1), calls=%async_computation | async-start | bytes 131072 | tf_op jit(solution)/shard_map/all_to_all | solution.py:250
  25.0 5.7 %copy-start.5 = (s32[128,1,8]{2,1,0:T(1,128)}, s32[128,1,8]{2,1,0:T(1,128)S(1)}, u32[]{:S(2)}) copy-start(s32[128,1,8]{2,1,0:T(1,128)S(1)} %all-to-all-done) | copy-start | bytes 12292
  30.7 32.7 %all-to-all-start.2 = ((f32[128,15,2,128]{3,2,1,0:T(2,128)}), f32[128,15,2,128]{3,2,1,0:T(2,128)S(1)}, u32[]{:S(2)}, u32[]{:S(2)}) async-start(f32[128,15,2,128]{3,2,1,0:T(2,128)} %bitcast.28), calls=%async_computation.2 | async-start | bytes 3932160 | tf_op jit(solution)/shard_map/all_to_all | solution.py:250
  63.5 4.8 %copy-start = (f32[128,15,2,128]{3,2,1,0:T(2,128)}, f32[128,15,2,128]{3,2,1,0:T(2,128)S(1)}, u32[]{:S(2)}) copy-start(f32[128,15,2,128]{3,2,1,0:T(2,128)S(1)} %all-to-all-done.2) | copy-start | bytes 5898244
  63.5 32.0 %all-to-all-start.1 = ((f32[128,9,2,128]{3,2,1,0:T(2,128)}), f32[128,9,2,128]{3,2,1,0:T(2,128)S(1)}, u32[]{:S(2)}, u32[]{:S(2)}) async-start(f32[128,9,2,128]{3,2,1,0:T(2,128)} %bitcast.29), calls=%async_computation.1 | async-start | bytes 2359296 | tf_op jit(solution)/shard_map/all_to_all | solution.py:250
  68.2 1.1 copy-start.3
  69.4 1.5 %copy-start.1 = (f32[128,15,2,128]{3,2,1,0:T(2,128)S(1)}, f32[128,15,2,128]{3,2,1,0:T(2,128)}, u32[]{:S(2)}) copy-start(f32[128,15,2,128]{3,2,1,0:T(2,128)} %copy-done) | copy-start | bytes 5898244
  70.9 12.4 %copy-start.2 = (f32[256,256]{1,0:T(8,128)S(1)}, f32[256,256]{1,0:T(8,128)}, u32[]{:S(2)}) copy-start(f32[256,256]{1,0:T(8,128)} %refs_6_.3) | copy-start | bytes 786436
  70.9 12.4 %copy-start.4 = (s32[256]{0:T(256)S(1)}, s32[256]{0:T(256)}, u32[]{:S(2)}) copy-start(s32[256]{0:T(256)} %refs_1_.3) | copy-start | bytes 3076
  109.0 26.5 %all-to-all-start.3 = ((f32[128,3,4,128]{3,2,1,0:T(4,128)}), f32[128,3,4,128]{3,2,1,0:T(4,128)S(1)}, u32[]{:S(2)}, u32[]{:S(2)}) async-start(f32[128,3,4,128]{3,2,1,0:T(4,128)} %bitcast.30), calls=%async_computation.3 | async-start | bytes 1572864 | tf_op jit(solution)/shard_map/all_to_all | solution.py:250

commit v5 on v4

--- a/solution.py
+++ b/solution.py
@@ -11,25 +11,88 @@
 WIDE = 16
 
 
-def routing(block_ids, blocks_dev, capacity, slot_count):
-    owners = block_ids // blocks_dev
-    local_ids = block_ids % blocks_dev
-    positions = jnp.arange(block_ids.shape[0], dtype=jnp.int32)
-    same_owner = (owners[:, None] == owners[None, :]) & (positions[:, None] > positions[None, :])
-    ranks = jnp.sum(same_owner.astype(jnp.int32), axis=1)
-    slot_ids = owners * capacity + ranks
-    matches = slot_ids[:, None] == jnp.arange(slot_count, dtype=jnp.int32)[None, :]
-    request = jnp.sum(jnp.where(matches, local_ids[:, None], 0), axis=0)
-    return (slot_ids, request)
+def strict_upper(size):
+    row = lax.broadcasted_iota(jnp.int32, (size, size), 0)
+    column = lax.broadcasted_iota(jnp.int32, (size, size), 1)
+    return jnp.where(row < column, 1.0, 0.0).astype(jnp.bfloat16)
+
+
+def dot_last(left, right):
+    return lax.dot_general(
+        left, right, (((1,), (1,)), ((), ())), preferred_element_type=jnp.float32
+    )
+
+
+def plan_kernel(devices, capacity, blocks, sec_ref, pri_ref, plan_ref, request_ref):
+    segs = sec_ref.shape[1]
+    upper = strict_upper(segs)
+    device = lax.broadcasted_iota(jnp.int32, (devices, segs), 0).astype(jnp.float32)
+    column = lax.broadcasted_iota(jnp.int32, (request_ref.shape[1], segs), 0).astype(jnp.float32)
+    request = jnp.zeros(request_ref.shape, jnp.float32)
+    routes = []
+    for side, ref in enumerate((sec_ref, pri_ref)):
+        ids = ref[...].astype(jnp.float32)
+        owner = jnp.floor((ids + 0.5) * (1.0 / blocks))
+        local = ids - owner * blocks
+        mine = jnp.where(device == owner, 1.0, 0.0)
+        narrow = mine.astype(jnp.bfloat16)
+        before = jnp.dot(narrow, upper, preferred_element_type=jnp.float32)
+        rank = jnp.sum(mine * before, axis=0, keepdims=True)
+        coarse = jnp.floor(local * (1.0 / 16.0)) * 16.0
+        here = column == rank + side * capacity
+        for part in (coarse, local - coarse):
+            request += dot_last(narrow, jnp.where(here, part, 0.0).astype(jnp.bfloat16))
+        routes.append((owner, rank))
+    request_ref[...] = request
+
+    (sec_owner, sec_rank), (pri_owner, pri_rank) = routes
+    early = jnp.where(sec_rank == 0.0, 1.0, 0.0)
+    spread = jnp.broadcast_to(early, (16, segs)).astype(jnp.bfloat16)
+    ahead = jnp.dot(spread, upper, preferred_element_type=jnp.float32)[:1]
+    count = jnp.sum(early, axis=1, keepdims=True)
+    number = lax.broadcasted_iota(jnp.int32, (1, segs), 1).astype(jnp.float32)
+    place = jnp.where(sec_rank == 0.0, ahead, count + number - ahead)
+    target = lax.broadcasted_iota(jnp.int32, (segs, segs), 0).astype(jnp.float32)
+    moved = jnp.where(target == place, 1.0, 0.0).astype(jnp.bfloat16)
+    row = lax.broadcasted_iota(jnp.int32, (16, segs), 0)
+    values = jnp.where(row == 0, number, jnp.where(row == 1, sec_owner, sec_rank))
+    values = dot_last(values.astype(jnp.bfloat16), moved)
+    seg, dev, rank = values[0:1], values[1:2], values[2:3]
+    start = jnp.where(
+        rank == 0.0,
+        dev * (6 * capacity + 6) + 6 * capacity,
+        dev * (6 * capacity - 6) + (rank - 1.0),
+    )
+    rows = (
+        pri_owner * (6 * capacity + 6) + pri_rank,
+        seg,
+        start,
+        dev * (3 * capacity) + rank,
+        jnp.broadcast_to(count, (1, segs)),
+    )
+    plan_ref[...] = jnp.zeros_like(plan_ref)
+    for i, value in enumerate(rows):
+        plan_ref[i : i + 1, :] = value.astype(jnp.int32)
 
 
 def table_kernel(xc_ref, xu_ref, out_ref):
-    half = xc_ref.shape[0]
-    out_ref[:half] = xc_ref[...]
-    out_ref[half:] = xu_ref[...]
-
-
-def gather_kernel(devices, capacity, blocks, first, ids_ref, table_ref, out_ref):
+    blocks = xc_ref.shape[0] // 3
+
+    def one_block(b, carry):
+        for half, ref in enumerate((xc_ref, xu_ref)):
+            for c in range(3):
+                here = pl.ds(pl.multiple_of(c * blocks + b * 8, 8), 8)
+                out_ref[pl.ds(b * 64 + 3 * half + c, 8, stride=8), :] = ref[here, :]
+        return carry
+
+    lax.fori_loop(0, blocks // 8, one_block, 0, unroll=4)
+
+
+def gather_kernel(devices, capacity, first, ids_ref, table_ref, out_ref, turned, local_ref, sem):
+    turned[...] = ids_ref[...].T[: 2 * capacity].astype(jnp.int32)
+    copy = pltpu.make_async_copy(turned, local_ref, sem)
+    copy.start()
+    copy.wait()
     if first:
         parts = [(1, rank, rank, capacity) for rank in range(capacity)]
         parts.append((0, 0, 6 * capacity, 1))
@@ -39,10 +102,9 @@
 
     def one_device(dev, carry):
         for side, rank, start, step in parts:
-            local = ids_ref[dev * (2 * capacity) + side * capacity + rank]
-            out_ref[pl.ds(dev * rows + start, 6, stride=step), :] = table_ref[
-                pl.ds(local, 6, stride=blocks), :
-            ]
+            local = local_ref[side * capacity + rank, dev]
+            patch = table_ref[pl.ds(pl.multiple_of(local * 8, 8), 8), :]
+            out_ref[pl.ds(dev * rows + start, 6, stride=step), :] = patch[:6]
         return carry
 
     lax.fori_loop(0, devices, one_device, 0, unroll=4)
@@ -118,13 +180,11 @@
     return sums[:8] + sums[8:]
 
 
-def pri_kernel(capacity, slots_ref, fetched_ref, points_ref, out_ref, both_ref, lhs_ref):
-    segs = slots_ref.shape[0]
+def pri_kernel(capacity, plan_ref, fetched_ref, points_ref, out_ref, both_ref, lhs_ref):
+    segs = plan_ref.shape[1]
 
     def first(s, i):
-        slot = slots_ref[s]
-        start = (slot // capacity) * (6 * capacity + 6) + slot % capacity
-        stage_a(s, start, capacity, fetched_ref, points_ref, both_ref, lhs_ref, i)
+        stage_a(s, plan_ref[0, s], capacity, fetched_ref, points_ref, both_ref, lhs_ref, i)
 
     def second(s, i):
         sums = sums_of(both_ref, lhs_ref, i)
@@ -148,35 +208,30 @@
 
 
 def sec_kernel(early, capacity, *refs):
-    slots_ref, count_ref, order_ref, early_ref, fetched_ref, points_ref, weights_ref = refs[:7]
+    plan_ref, count_ref, fetched_ref, points_ref, weights_ref = refs[:5]
     if early:
-        far_ref, out_ref, both_ref, lhs_ref, left_ref, other_ref, sems = refs[7:]
+        far_ref, out_ref, both_ref, lhs_ref, left_ref, other_ref, sems = refs[5:]
         out_ref[...] = jnp.zeros_like(out_ref)
-        low, high_end = 0, early_ref[0]
+        low, high_end = 0, plan_ref[4, 0]
         copies = []
     else:
-        far_ref, before_ref, out_ref, both_ref, lhs_ref, left_ref, other_ref, sems = refs[7:]
-        low, high_end = early_ref[0], slots_ref.shape[0]
+        far_ref, before_ref, out_ref, both_ref, lhs_ref, left_ref, other_ref, sems = refs[5:]
+        low, high_end = plan_ref[4, 0], plan_ref.shape[1]
         copies = [pltpu.make_async_copy(before_ref, out_ref, sems.at[1])]
     copies.append(pltpu.make_async_copy(far_ref, other_ref, sems.at[0]))
     for copy in copies:
         copy.start()
 
-    def segment(place):
-        return order_ref[jnp.minimum(low + place, high_end - 1)]
+    def entry(row, place):
+        return plan_ref[row, jnp.minimum(low + place, high_end - 1)]
 
     def first(place, i):
-        s = segment(place)
-        slot = slots_ref[s]
-        dev, rank = slot // capacity, slot % capacity
-        if early:
-            start, step = dev * (6 * capacity + 6) + 6 * capacity, 1
-        else:
-            start, step = dev * (6 * capacity - 6) + (rank - 1), capacity - 1
+        step = 1 if early else capacity - 1
+        s, start = entry(1, place), entry(2, place)
         stage_a(s, start, step, fetched_ref, points_ref, both_ref, lhs_ref, i)
 
     def second(place, i):
-        s = segment(place)
+        s = entry(1, place)
         sums = sums_of(both_ref, lhs_ref, i)
         inverse = 1.0 / sums[6:7]
         weights = weights_ref[pl.ds(s, 1), :]
@@ -187,7 +242,6 @@
         left_ref[i] = jnp.concatenate([high, gap - high], axis=0).astype(jnp.bfloat16)
 
     def third(place, i):
-        slot = slots_ref[segment(place)]
         left, both = left_ref[i], both_ref[i]
         half = both.shape[0] // 2
         if i % 2 == 0:
@@ -202,8 +256,7 @@
             )
             result = (result[:half] + result[half:]).T
             result = result[:8] + result[8:]
-        base = (slot // capacity) * (3 * capacity) + slot % capacity
-        out_ref[pl.ds(base, 3, stride=capacity), :] = result[3:6]
+        out_ref[pl.ds(entry(3, place), 3, stride=capacity), :] = result[3:6]
 
     for i in range(HALF):
         first(i, i)
@@ -249,32 +302,28 @@
     def exchange(value):
         return lax.all_to_all(value, AXES, split_axis=0, concat_axis=0, tiled=True)
 
-    sec_slots, sec_request = routing(sec_block, blocks, cap, slots)
-    pri_slots, pri_request = routing(pri_block, blocks, cap, slots)
+    plan, request = pl.pallas_call(
+        functools.partial(plan_kernel, devices, cap, blocks),
+        out_shape=(
+            jax.ShapeDtypeStruct((8, segs), jnp.int32),
+            jax.ShapeDtypeStruct((devices, 128), f32),
+        ),
+        in_specs=[vmem, vmem],
+        out_specs=(vmem, vmem),
+        compiler_params=limit,
+    )(sec_block.reshape(1, segs), pri_block.reshape(1, segs))
     xc = jnp.transpose(node_coords, (1, 0, 2)).reshape(3 * blocks, nodes)
     xu = jnp.transpose(node_disp, (1, 0, 2)).reshape(3 * blocks, nodes)
     hbm = pl.BlockSpec(memory_space=pltpu.HBM)
     table = pl.pallas_call(
         table_kernel,
-        out_shape=pltpu.VMEM((6 * blocks, nodes), f32),
+        out_shape=pltpu.VMEM((8 * blocks, nodes), f32),
         in_specs=[vmem, vmem],
         out_specs=vmem,
         compiler_params=limit,
     )(far(xc), far(xu))
-    requests = jnp.concatenate(
-        [sec_request.reshape(devices, cap), pri_request.reshape(devices, cap)], axis=1
-    )
-    received = exchange(requests)
-    sec_ids = received[:, :cap].reshape(slots)
-    ids = received.reshape(2 * slots)
-
-    is_early = sec_slots % cap == 0
-    early = jnp.sum(is_early.astype(jnp.int32))
-    here = jnp.arange(segs, dtype=jnp.int32)
-    same = (is_early[:, None] == is_early[None, :]) & (here[:, None] > here[None, :])
-    place = jnp.sum(same.astype(jnp.int32), axis=1) + jnp.where(is_early, 0, early)
-    order = jnp.sum(jnp.where(place[:, None] == here[None, :], here[:, None], 0), axis=0)
-    early = early.reshape(1)
+    received = exchange(request.reshape(devices, 1, 128)).reshape(devices, 128)
+    sec_ids = received[:, :cap].reshape(slots).astype(jnp.int32)
 
     def scratch(count):
         return [
@@ -284,12 +333,17 @@
 
     def gather(first, rows):
         return pl.pallas_call(
-            functools.partial(gather_kernel, devices, cap, blocks, first),
+            functools.partial(gather_kernel, devices, cap, first),
             out_shape=pltpu.HBM((devices * rows, nodes), f32),
-            in_specs=[smem, vmem],
+            in_specs=[vmem, vmem],
             out_specs=vmem,
+            scratch_shapes=[
+                pltpu.VMEM((2 * cap, devices), jnp.int32),
+                pltpu.SMEM((2 * cap, devices), jnp.int32),
+                pltpu.SemaphoreType.DMA,
+            ],
             compiler_params=limit,
-        )(ids, near(table)).reshape(devices, rows // 2, 2, nodes)
+        )(received, near(table)).reshape(devices, rows // 2, 2, nodes)
 
     out1 = gather(True, 6 * cap + 6)
     out2 = gather(False, 6 * cap - 6)
@@ -310,13 +364,13 @@
         out_specs=vmem,
         compiler_params=limit,
         scratch_shapes=scratch(WIDE),
-    )(pri_slots, in1, points)
+    )(plan, in1, points)
 
     def secondary(early_part, *args):
         return pl.pallas_call(
             functools.partial(sec_kernel, early_part, cap),
             out_shape=pltpu.HBM((devices * 3 * cap, nodes), f32),
-            in_specs=[smem] * 4 + [vmem] * 3 + [hbm] * (len(args) - 7),
+            in_specs=[smem] * 2 + [vmem] * 3 + [hbm] * (len(args) - 5),
             out_specs=vmem,
             compiler_params=limit,
             scratch_shapes=scratch(HALF)
@@ -328,11 +382,9 @@
         )(*args)
 
     other = far(other)
-    parcels = secondary(True, sec_slots, qcount, order, early, in1, points, qweights, other)
+    parcels = secondary(True, plan, qcount, in1, points, qweights, other)
     parcels = far(parcels)
-    parcels = secondary(
-        False, sec_slots, qcount, order, early, in2, points, qweights, other, parcels
-    )
+    parcels = secondary(False, plan, qcount, in2, points, qweights, other, parcels)
     incoming = exchange(parcels.reshape(devices, 3, cap, nodes))
     select = (jnp.arange(blocks, dtype=jnp.int32)[:, None] == sec_ids[None, :]).astype(f32)
     incoming = jnp.transpose(incoming, (0, 2, 1, 3)).reshape(slots, 3, nodes)

time: 138 us -> 134 us (0.971)
  other arithmetic: 5.3 us -> 0.01 us
  local copies, waits for them, and re-layouts: 3.32 us -> 5.68 us
  Pallas kernels: 47 us -> 45.6 us
    unnamed x12 -> x22, local copies, waits for them, and re-layouts: 1.32 us -> 5.44 us
    reduce_sum x7 -> x0, other arithmetic: 1.67 us -> none  [the longest x1 0.71 us: body(): early = jnp.sum(is_early.astype(jnp.int32))]
    select_n x2 -> x0, other arithmetic: 1.38 us -> none  [the longest x1 0.69 us: routing(): owners = block_ids // blocks_dev]
    pallas_call x3 -> x4, Pallas kernels: 8.6 us -> 8.04 us  [the longest x2 5.48 us: gather(): pl.pallas_call(functools.partial(gather_kernel, devices, cap, first), out...]
  transfers between devices with their start and end apart: 4 -> 4, of which waited for: 3 -> 3; matrix products, arithmetic and copies ran while one was open for 1% -> 0% of each run, Pallas kernels for 21% -> 21%
where the time goes in v5:
time: 134 us; the launch traced here: 133 us
  waiting for transfers between devices  50 us (37%)
  Pallas kernels  45.6 us (34%)
  starting transfers between devices  30.3 us (23%)
  local copies, waits for them, and re-layouts  5.68 us (4%)
  matrix products  1.67 us (1%)
    all_to_all x4, waiting for transfers between devices, exchange(): return lax.all_to_all(value, AXES, split_axis=0, concat_axis=0, tiled=True)  50 us
    all_to_all x4, starting transfers between devices, exchange(): return lax.all_to_all(value, AXES, split_axis=0, concat_axis=0, tiled=True)  30.3 us
    pallas_call x2, Pallas kernels, secondary(): pl.pallas_call(functools.partial(sec_kernel, early_part, cap), out_shape=...  24.7 us
    pallas_call x1, Pallas kernels, body(): pl.pallas_call(functools.partial(pri_kernel, cap), out_shape=pltpu.HBM((s...  12.5 us
    pallas_call x2, Pallas kernels, gather(): pl.pallas_call(functools.partial(gather_kernel, devices, cap, first), out...  5.48 us
    unnamed x22, local copies, waits for them, and re-layouts  5.44 us
  transfers between devices with their start and end apart: 4, of which 3 were waited for; matrix products, arithmetic and copies ran while one was open for 0% of the time, Pallas kernels for 21%

profile of v5, /device:TPU:1, one launch (start us, length us, event | category | flops | bytes accessed | tf_op | source)
XLA Modules:
  0.0 133.5 jit_solution(13403506949197023441)
XLA Ops:
  0.0 0.7 copy-done.9
  0.7 0.7 copy-done.10
  1.4 1.1 shard_map.73
  2.5 11.5 %all-to-all-start = ((f32[128,1,128]{2,1,0:T(1,128)}), f32[128,1,128]{2,1,0:T(1,128)S(1)}, u32[]{:S(2)}, u32[]{:S(2)}) async-start(f32[128,1,128]{2,1,0:T(1,128)} %bitcast.3), calls=%async_computation | async-start | bytes 131072 | tf_op jit(solution)/shard_map/all_to_all | solution.py:303
  14.0 1.5 %shard_map.74.table_ref = f32[3072,128]{1,0:T(8,128)S(1)} custom-call(f32[1152,128]{1,0:T(8,128)} %bitcast.38, f32[1152,128]{1,0:T(8,128)} %bitcast.39), custom_call_target="tpu_custom_call" | custom-call | tf_op jit(solution)/shard_map/pallas_call | solution.py:318
  15.4 8.3 %all-to-all-done = f32[128,1,128]{2,1,0:T(1,128)S(1)} async-done(((f32[128,1,128]{2,1,0:T(1,128)}), f32[128,1,128]{2,1,0:T(1,128)S(1)}, u32[]{:S(2)}, u32[]{:S(2)}) %all-to-all-start) | async-done | bytes 65568 | tf_op jit(solution)/shard_map/all_to_all | solution.py:303
  23.7 3.0 %shard_map.77 = f32[3840,128]{1,0:T(8,128)} custom-call(f32[128,128]{1,0:T(8,128)S(1)} %bitcast.27, f32[3072,128]{1,0:T(8,128)S(1)} %shard_map.74.table_ref), custom_call_target="tpu_custom_call" | custom-call | tf_op jit(solution)/shard_map/pallas_call | solution.py:335
  26.7 4.2 %all-to-all-start.2 = ((f32[128,15,2,128]{3,2,1,0:T(2,128)}), f32[128,15,2,128]{3,2,1,0:T(2,128)S(1)}, u32[]{:S(2)}, u32[]{:S(2)}) async-start(f32[128,15,2,128]{3,2,1,0:T(2,128)} %bitcast.33), calls=%async_computation.2 | async-start | bytes 3932160 | tf_op jit(solution)/shard_map/all_to_all | solution.py:303
  30.9 0.8 copy-done.3
  31.7 2.5 %shard_map.75 = f32[2304,128]{1,0:T(8,128)} custom-call(f32[128,128]{1,0:T(8,128)S(1)} %bitcast.28, f32[3072,128]{1,0:T(8,128)S(1)} %shard_map.74.table_ref), custom_call_target="tpu_custom_call" | custom-call | tf_op jit(solution)/shard_map/pallas_call | solution.py:335
  34.3 25.2 %all-to-all-done.2 = f32[128,15,2,128]{3,2,1,0:T(2,128)S(1)} async-done(((f32[128,15,2,128]{3,2,1,0:T(2,128)}), f32[128,15,2,128]{3,2,1,0:T(2,128)S(1)}, u32[]{:S(2)}, u32[]{:S(2)}) %all-to-all-start.2) | async-done | bytes 1966112 | tf_op jit(solution)/shard_map/all_to_all | solution.py:303
  59.5 4.7 %all-to-all-start.1 = ((f32[128,9,2,128]{3,2,1,0:T(2,128)}), f32[128,9,2,128]{3,2,1,0:T(2,128)S(1)}, u32[]{:S(2)}, u32[]{:S(2)}) async-start(f32[128,9,2,128]{3,2,1,0:T(2,128)} %bitcast.34), calls=%async_computation.1 | async-start | bytes 2359296 | tf_op jit(solution)/shard_map/all_to_all | solution.py:303
  64.3 1.1 copy-done.7
  65.4 0.4 shard_map.76.points_ref.refs_3_
  65.8 1.2 copy-done.1
  66.9 12.5 %shard_map.78.refs_5_ = f32[256,8,256]{2,1,0:T(8,128)} custom-call(s32[8,256]{1,0:T(8,128)S(1)} %get-tuple-element.8.plan_ref.refs_0_, f32[3840,128]{1,0:T(8,128)S(1)} %bitcast.24, f32[2,2048,128]{2,1,0:T(8,128)S(1)} %shard_map.76.points_ref.refs_3_), custom_call_target="tpu_custom_call" | custom-call | tf_op jit(solution)/shard_map/pallas_call | solution.py:360
  79.4 11.7 %shard_map.79.refs_6_ = f32[1536,128]{1,0:T(8,128)} custom-call(s32[8,256]{1,0:T(8,128)S(1)} %get-tuple-element.8.plan_ref.refs_0_, s32[256]{0:T(256)S(1)} %copy-done.8, f32[3840,128]{1,0:T(8,128)S(1)} %bitcast.25, f32[2,2048,128]{2,1,0:T(8,128)S(1)} %shard_map.76.points_ref.refs_3_, f32[256,256]{1,0:T(8,128)S(1)} %copy-done.5, f32[256,8,256]{2,1,0:T(8,128)} %shard_map.78.refs_5_), custom_call_target="tpu_custom_call" | custom-call | tf_op jit(solution)/shard_map/pallas_call | solution.py:370
  91.2 0.9 copy-done.6
  92.1 13.0 %shard_map.80 = f32[1536,128]{1,0:T(8,128)} custom-call(s32[8,256]{1,0:T(8,128)S(1)} %get-tuple-element.8.plan_ref.refs_0_, s32[256]{0:T(256)S(1)} %copy-done.8, f32[2304,128]{1,0:T(8,128)S(1)} %bitcast.26, f32[2,2048,128]{2,1,0:T(8,128)S(1)} %shard_map.76.points_ref.refs_3_, f32[256,256]{1,0:T(8,128)S(1)} %copy-done.6, f32[256,8,256]{2,1,0:T(8,128)} %shard_map.78.refs_5_, ...), custom_call_target="tpu_custom_call" | custom-call | tf_op jit(solution)/shard_map/pallas_call | solution.py:370
  105.1 9.9 %all-to-all-start.3 = ((f32[128,3,4,128]{3,2,1,0:T(4,128)}), f32[128,3,4,128]{3,2,1,0:T(4,128)S(1)}, u32[]{:S(2)}, u32[]{:S(2)}) async-start(f32[128,3,4,128]{3,2,1,0:T(4,128)} %bitcast.35), calls=%async_computation.3 | async-start | bytes 1572864 | tf_op jit(solution)/shard_map/all_to_all | solution.py:303
  115.1 0.1 convert_element_type.12
  115.2 16.5 %all-to-all-done.3 = f32[128,3,4,128]{3,2,1,0:T(4,128)S(1)} async-done(((f32[128,3,4,128]{3,2,1,0:T(4,128)}), f32[128,3,4,128]{3,2,1,0:T(4,128)S(1)}, u32[]{:S(2)}, u32[]{:S(2)}) %all-to-all-start.3) | async-done | bytes 786464 | tf_op jit(solution)/shard_map/all_to_all | solution.py:303
  131.7 0.1 copy.11
  131.8 1.7 %fusion.1 = f32[384,3,128]{2,0,1:T(8,128)} fusion(f32[512,3,128]{2,0,1:T(8,128)S(1)} %bitcast.37, s32[512]{0:T(512)S(1)} %convert_element_type.12), kind=kOutput, calls=%fused_computation.2 | convolution fusion | flops 906166272 | bytes 1378304 | tf_op jit(solution)/shard_map/bp,pcn->bcn/dot_general | solution.py:391
  (18 shorter events, 0.0 us)
Async XLA Ops:
  0.0 0.7 copy-start.9
  0.7 0.7 copy-start.10
  2.5 21.3 %all-to-all-start = ((f32[128,1,128]{2,1,0:T(1,128)}), f32[128,1,128]{2,1,0:T(1,128)S(1)}, u32[]{:S(2)}, u32[]{:S(2)}) async-start(f32[128,1,128]{2,1,0:T(1,128)} %bitcast.3), calls=%async_computation | async-start | bytes 131072 | tf_op jit(solution)/shard_map/all_to_all | solution.py:303
  23.7 3.0 %copy-start.2 = (f32[128,1,128]{2,1,0:T(1,128)}, f32[128,1,128]{2,1,0:T(1,128)S(1)}, u32[]{:S(2)}) copy-start(f32[128,1,128]{2,1,0:T(1,128)S(1)} %all-to-all-done) | copy-start | bytes 196612
  26.7 32.7 %all-to-all-start.2 = ((f32[128,15,2,128]{3,2,1,0:T(2,128)}), f32[128,15,2,128]{3,2,1,0:T(2,128)S(1)}, u32[]{:S(2)}, u32[]{:S(2)}) async-start(f32[128,15,2,128]{3,2,1,0:T(2,128)} %bitcast.33), calls=%async_computation.2 | async-start | bytes 3932160 | tf_op jit(solution)/shard_map/all_to_all | solution.py:303
  30.9 0.8 copy-start.3
  59.5 4.8 %copy-start = (f32[128,15,2,128]{3,2,1,0:T(2,128)}, f32[128,15,2,128]{3,2,1,0:T(2,128)S(1)}, u32[]{:S(2)}) copy-start(f32[128,15,2,128]{3,2,1,0:T(2,128)S(1)} %all-to-all-done.2) | copy-start | bytes 5898244
  59.5 31.7 %all-to-all-start.1 = ((f32[128,9,2,128]{3,2,1,0:T(2,128)}), f32[128,9,2,128]{3,2,1,0:T(2,128)S(1)}, u32[]{:S(2)}, u32[]{:S(2)}) async-start(f32[128,9,2,128]{3,2,1,0:T(2,128)} %bitcast.34), calls=%async_computation.1 | async-start | bytes 2359296 | tf_op jit(solution)/shard_map/all_to_all | solution.py:303
  64.3 1.1 copy-start.7
  65.4 1.5 %copy-start.1 = (f32[128,15,2,128]{3,2,1,0:T(2,128)S(1)}, f32[128,15,2,128]{3,2,1,0:T(2,128)}, u32[]{:S(2)}) copy-start(f32[128,15,2,128]{3,2,1,0:T(2,128)} %copy-done) | copy-start | bytes 5898244
  66.9 12.5 %copy-start.5 = (f32[256,256]{1,0:T(8,128)S(1)}, f32[256,256]{1,0:T(8,128)}, u32[]{:S(2)}) copy-start(f32[256,256]{1,0:T(8,128)} %refs_4_.3) | copy-start | bytes 786436
  66.9 12.5 %copy-start.8 = (s32[256]{0:T(256)S(1)}, s32[256]{0:T(256)}, u32[]{:S(2)}) copy-start(s32[256]{0:T(256)} %refs_1_.3) | copy-start | bytes 3076
  91.2 1.0 copy-start.6
  92.1 22.9 %copy-start.4 = (f32[128,1,128]{2,1,0:T(1,128)S(1)}, f32[128,1,128]{2,1,0:T(1,128)}, u32[]{:S(2)}) copy-start(f32[128,1,128]{2,1,0:T(1,128)} %copy-done.2) | copy-start | bytes 196612
  105.1 26.5 %all-to-all-start.3 = ((f32[128,3,4,128]{3,2,1,0:T(4,128)}), f32[128,3,4,128]{3,2,1,0:T(4,128)S(1)}, u32[]{:S(2)}, u32[]{:S(2)}) async-start(f32[128,3,4,128]{3,2,1,0:T(4,128)} %bitcast.35), calls=%async_computation.3 | async-start | bytes 1572864 | tf_op jit(solution)/shard_map/all_to_all | solution.py:303

commit v6 on v5

--- a/solution.py
+++ b/solution.py
@@ -7,8 +7,8 @@
 from jax.sharding import PartitionSpec as P
 
 AXES = ("gx", "gy")
-HALF = 8
 WIDE = 16
+SETS = 8
 
 
 def strict_upper(size):
@@ -180,7 +180,7 @@
     return sums[:8] + sums[8:]
 
 
-def pri_kernel(capacity, plan_ref, fetched_ref, points_ref, out_ref, both_ref, lhs_ref):
+def primary_pass(capacity, plan_ref, fetched_ref, points_ref, other_ref, both_ref, lhs_ref):
     segs = plan_ref.shape[1]
 
     def first(s, i):
@@ -188,7 +188,7 @@
 
     def second(s, i):
         sums = sums_of(both_ref, lhs_ref, i)
-        out_ref[s] = sums * (1.0 / sums[6:7])
+        other_ref[s] = sums * (1.0 / sums[6:7])
 
     for i in range(WIDE):
         first(i, i)
@@ -207,26 +207,14 @@
     lax.fori_loop(0, segs // (2 * WIDE), one_group, 0)
 
 
-def sec_kernel(early, capacity, *refs):
-    plan_ref, count_ref, fetched_ref, points_ref, weights_ref = refs[:5]
-    if early:
-        far_ref, out_ref, both_ref, lhs_ref, left_ref, other_ref, sems = refs[5:]
-        out_ref[...] = jnp.zeros_like(out_ref)
-        low, high_end = 0, plan_ref[4, 0]
-        copies = []
-    else:
-        far_ref, before_ref, out_ref, both_ref, lhs_ref, left_ref, other_ref, sems = refs[5:]
-        low, high_end = plan_ref[4, 0], plan_ref.shape[1]
-        copies = [pltpu.make_async_copy(before_ref, out_ref, sems.at[1])]
-    copies.append(pltpu.make_async_copy(far_ref, other_ref, sems.at[0]))
-    for copy in copies:
-        copy.start()
+def secondary_pass(step, capacity, low, end, wait, refs):
+    plan_ref, count_ref, fetched_ref, points_ref, weights_ref, other_ref = refs[:6]
+    out_ref, both_ref, lhs_ref, left_ref = refs[6:]
 
     def entry(row, place):
-        return plan_ref[row, jnp.minimum(low + place, high_end - 1)]
+        return plan_ref[row, jnp.minimum(low + place, end - 1)]
 
     def first(place, i):
-        step = 1 if early else capacity - 1
         s, start = entry(1, place), entry(2, place)
         stage_a(s, start, step, fetched_ref, points_ref, both_ref, lhs_ref, i)
 
@@ -245,38 +233,79 @@
         left, both = left_ref[i], both_ref[i]
         half = both.shape[0] // 2
         if i % 2 == 0:
-            result = lax.dot_general(
-                left, both, (((1,), (1,)), ((), ())), preferred_element_type=jnp.float32
-            )
+            result = dot_last(left, both)
             result = result[:8] + result[8:]
             result = result[:, :half] + result[:, half:]
         else:
-            result = lax.dot_general(
-                both, left, (((1,), (1,)), ((), ())), preferred_element_type=jnp.float32
-            )
+            result = dot_last(both, left)
             result = (result[:half] + result[half:]).T
             result = result[:8] + result[8:]
         out_ref[pl.ds(entry(3, place), 3, stride=capacity), :] = result[3:6]
 
-    for i in range(HALF):
+    for i in range(SETS):
         first(i, i)
-    for copy in copies:
-        copy.wait()
+    wait()
+    for i in range(SETS):
+        second(i, i)
+        first(SETS + i, SETS + i)
 
     def one_group(g, carry):
-        base = g * (2 * HALF)
-        for i in range(HALF):
-            second(base + i, i)
-            first(base + HALF + i, HALF + i)
-        for i in range(HALF):
-            third(base + i, i)
-            second(base + HALF + i, HALF + i)
-        for i in range(HALF):
-            third(base + HALF + i, HALF + i)
-            first(base + 2 * HALF + i, i)
+        base = g * (3 * SETS)
+        for phase in range(3):
+            for i in range(SETS):
+                a, b, c = (phase * SETS + SETS * t + i for t in (2, 1, 0))
+                third(base + c, c)
+                second(base + b, b % (3 * SETS))
+                first(base + a, a % (3 * SETS))
         return carry
 
-    lax.fori_loop(0, (high_end - low + 2 * HALF - 1) // (2 * HALF), one_group, 0)
+    lax.fori_loop(0, (end - low + 3 * SETS - 1) // (3 * SETS), one_group, 0)
+
+
+def early_kernel(capacity, plan_ref, count_ref, fetched_ref, points_ref, far_weights_ref, *refs):
+    far_other_ref, out_ref, both_ref, lhs_ref, left_ref, other_ref, weights_ref, sems = refs
+    load = pltpu.make_async_copy(far_weights_ref, weights_ref, sems.at[0])
+    store = pltpu.make_async_copy(other_ref, far_other_ref, sems.at[1])
+    load.start()
+    out_ref[...] = jnp.zeros_like(out_ref)
+    primary_pass(capacity, plan_ref, fetched_ref, points_ref, other_ref, both_ref, lhs_ref)
+    store.start()
+    secondary_pass(
+        1,
+        capacity,
+        0,
+        plan_ref[4, 0],
+        load.wait,
+        (plan_ref, count_ref, fetched_ref, points_ref, weights_ref, other_ref)
+        + (out_ref, both_ref, lhs_ref, left_ref),
+    )
+    store.wait()
+
+
+def late_kernel(capacity, plan_ref, count_ref, fetched_ref, points_ref, *refs):
+    far_weights_ref, far_other_ref, before_ref, out_ref = refs[:4]
+    both_ref, lhs_ref, left_ref, other_ref, weights_ref, sems = refs[4:]
+    loads = [
+        pltpu.make_async_copy(far_other_ref, other_ref, sems.at[0]),
+        pltpu.make_async_copy(far_weights_ref, weights_ref, sems.at[1]),
+        pltpu.make_async_copy(before_ref, out_ref, sems.at[2]),
+    ]
+    for load in loads:
+        load.start()
+
+    def wait():
+        for load in loads:
+            load.wait()
+
+    secondary_pass(
+        capacity - 1,
+        capacity,
+        plan_ref[4, 0],
+        plan_ref.shape[1],
+        wait,
+        (plan_ref, count_ref, fetched_ref, points_ref, weights_ref, other_ref)
+        + (out_ref, both_ref, lhs_ref, left_ref),
+    )
 
 
 def body(node_coords, node_disp, qpoints, qweights, qcount, sec_block, pri_block):
@@ -311,7 +340,7 @@
         in_specs=[vmem, vmem],
         out_specs=(vmem, vmem),
         compiler_params=limit,
-    )(sec_block.reshape(1, segs), pri_block.reshape(1, segs))
+    )(far(sec_block.reshape(1, segs)), far(pri_block.reshape(1, segs)))
     xc = jnp.transpose(node_coords, (1, 0, 2)).reshape(3 * blocks, nodes)
     xu = jnp.transpose(node_disp, (1, 0, 2)).reshape(3 * blocks, nodes)
     hbm = pl.BlockSpec(memory_space=pltpu.HBM)
@@ -324,12 +353,6 @@
     )(far(xc), far(xu))
     received = exchange(request.reshape(devices, 1, 128)).reshape(devices, 128)
     sec_ids = received[:, :cap].reshape(slots).astype(jnp.int32)
-
-    def scratch(count):
-        return [
-            pltpu.VMEM((2 * count, 2 * nodes, quad), jnp.bfloat16),
-            pltpu.VMEM((2 * count, 16, 2 * nodes), jnp.bfloat16),
-        ]
 
     def gather(first, rows):
         return pl.pallas_call(
@@ -357,34 +380,35 @@
         compiler_params=limit,
     )(jnp.transpose(qpoints, (1, 0, 2)))
     points = near(points)
-    other = pl.pallas_call(
-        functools.partial(pri_kernel, cap),
-        out_shape=pltpu.HBM((segs, 8, quad), f32),
-        in_specs=[smem, vmem, vmem],
+
+    def scratch(count, sems):
+        return [
+            pltpu.VMEM((count, 2 * nodes, quad), jnp.bfloat16),
+            pltpu.VMEM((count, 16, 2 * nodes), jnp.bfloat16),
+            pltpu.VMEM((3 * SETS, 16, quad), jnp.bfloat16),
+            pltpu.VMEM((segs, 8, quad), f32),
+            pltpu.VMEM((segs, quad), f32),
+            pltpu.SemaphoreType.DMA((sems,)),
+        ]
+
+    parcel = pltpu.HBM((devices * 3 * cap, nodes), f32)
+    weights = far(qweights)
+    other, parcels = pl.pallas_call(
+        functools.partial(early_kernel, cap),
+        out_shape=(pltpu.HBM((segs, 8, quad), f32), parcel),
+        in_specs=[smem, smem, vmem, vmem, hbm],
+        out_specs=(hbm, vmem),
+        scratch_shapes=scratch(max(2 * WIDE, 3 * SETS), 2),
+        compiler_params=limit,
+    )(plan, qcount, in1, points, weights)
+    parcels = pl.pallas_call(
+        functools.partial(late_kernel, cap),
+        out_shape=parcel,
+        in_specs=[smem, smem, vmem, vmem, hbm, hbm, hbm],
         out_specs=vmem,
+        scratch_shapes=scratch(3 * SETS, 3),
         compiler_params=limit,
-        scratch_shapes=scratch(WIDE),
-    )(plan, in1, points)
-
-    def secondary(early_part, *args):
-        return pl.pallas_call(
-            functools.partial(sec_kernel, early_part, cap),
-            out_shape=pltpu.HBM((devices * 3 * cap, nodes), f32),
-            in_specs=[smem] * 2 + [vmem] * 3 + [hbm] * (len(args) - 5),
-            out_specs=vmem,
-            compiler_params=limit,
-            scratch_shapes=scratch(HALF)
-            + [
-                pltpu.VMEM((2 * HALF, 16, quad), jnp.bfloat16),
-                pltpu.VMEM((segs, 8, quad), f32),
-                pltpu.SemaphoreType.DMA((2,)),
-            ],
-        )(*args)
-
-    other = far(other)
-    parcels = secondary(True, plan, qcount, in1, points, qweights, other)
-    parcels = far(parcels)
-    parcels = secondary(False, plan, qcount, in2, points, qweights, other, parcels)
+    )(plan, qcount, in2, points, weights, far(other), far(parcels))
     incoming = exchange(parcels.reshape(devices, 3, cap, nodes))
     select = (jnp.arange(blocks, dtype=jnp.int32)[:, None] == sec_ids[None, :]).astype(f32)
     incoming = jnp.transpose(incoming, (0, 2, 1, 3)).reshape(slots, 3, nodes)

time: 134 us -> 129 us (0.963)
  Pallas kernels: 45.6 us -> 40.3 us
  local copies, waits for them, and re-layouts: 5.68 us -> 3.37 us
  starting transfers between devices: 30.3 us -> 32.5 us
    pallas_call x3 -> x2, Pallas kernels: 37.2 us -> 31.2 us  [the longest x1 19.2 us: body(): pl.pallas_call(functools.partial(early_kernel, cap), out_shape=(pltpu.HBM...]
    unnamed x22 -> x14, local copies, waits for them, and re-layouts: 5.44 us -> 3.13 us
    all_to_all x4, starting transfers between devices: 30.3 us -> 32.5 us  [exchange(): return lax.all_to_all(value, AXES, split_axis=0, concat_axis=0, tiled=True)]
  transfers between devices with their start and end apart: 4 -> 4, of which waited for: 3 -> 3; matrix products, arithmetic and copies ran while one was open for 0% -> 0% of each run, Pallas kernels for 21% -> 18%
where the time goes in v6:
time: 129 us; the launch traced here: 128 us
  waiting for transfers between devices  50.1 us (39%)
  Pallas kernels  40.3 us (31%)
  starting transfers between devices  32.5 us (25%)
  local copies, waits for them, and re-layouts  3.37 us (3%)
  matrix products  1.67 us (1%)
    all_to_all x4, waiting for transfers between devices, exchange(): return lax.all_to_all(value, AXES, split_axis=0, concat_axis=0, tiled=True)  50.1 us
    all_to_all x4, starting transfers between devices, exchange(): return lax.all_to_all(value, AXES, split_axis=0, concat_axis=0, tiled=True)  32.5 us
    pallas_call x1, Pallas kernels, body(): pl.pallas_call(functools.partial(early_kernel, cap), out_shape=(pltpu.HBM...  19.2 us
    pallas_call x1, Pallas kernels, body(): pl.pallas_call(functools.partial(late_kernel, cap), out_shape=parcel, in_...  12 us
    pallas_call x2, Pallas kernels, gather(): pl.pallas_call(functools.partial(gather_kernel, devices, cap, first), out...  5.49 us
    unnamed x14, local copies, waits for them, and re-layouts  3.13 us
  transfers between devices with their start and end apart: 4, of which 3 were waited for; matrix products, arithmetic and copies ran while one was open for 0% of the time, Pallas kernels for 18%

profile of v6, /device:TPU:1, one launch (start us, length us, event | category | flops | bytes accessed | tf_op | source)
XLA Modules:
  0.0 128.1 jit_solution(16735672749932833842)
XLA Ops:
  0.0 1.8 %shard_map.73 = (s32[8,256]{1,0:T(8,128)S(1)}, f32[128,128]{1,0:T(8,128)}) custom-call(s32[1,256]{1,0:T(1,128)} %bitcast.36, s32[1,256]{1,0:T(1,128)} %bitcast.37), custom_call_target="tpu_custom_call" | custom-call | tf_op jit(solution)/shard_map/pallas_call | solution.py:334
  1.8 11.5 %all-to-all-start = ((f32[128,1,128]{2,1,0:T(1,128)}), f32[128,1,128]{2,1,0:T(1,128)S(1)}, u32[]{:S(2)}, u32[]{:S(2)}) async-start(f32[128,1,128]{2,1,0:T(1,128)} %bitcast.3), calls=%async_computation | async-start | bytes 131072 | tf_op jit(solution)/shard_map/all_to_all | solution.py:332
  13.3 1.5 %shard_map.74.table_ref = f32[3072,128]{1,0:T(8,128)S(1)} custom-call(f32[1152,128]{1,0:T(8,128)} %bitcast.34, f32[1152,128]{1,0:T(8,128)} %bitcast.35), custom_call_target="tpu_custom_call" | custom-call | tf_op jit(solution)/shard_map/pallas_call | solution.py:347
  14.8 8.3 %all-to-all-done = f32[128,1,128]{2,1,0:T(1,128)S(1)} async-done(((f32[128,1,128]{2,1,0:T(1,128)}), f32[128,1,128]{2,1,0:T(1,128)S(1)}, u32[]{:S(2)}, u32[]{:S(2)}) %all-to-all-start) | async-done | bytes 65568 | tf_op jit(solution)/shard_map/all_to_all | solution.py:332
  23.1 3.0 %shard_map.77 = f32[3840,128]{1,0:T(8,128)} custom-call(f32[128,128]{1,0:T(8,128)S(1)} %bitcast.25, f32[3072,128]{1,0:T(8,128)S(1)} %shard_map.74.table_ref), custom_call_target="tpu_custom_call" | custom-call | tf_op jit(solution)/shard_map/pallas_call | solution.py:358
  26.1 4.2 %all-to-all-start.2 = ((f32[128,15,2,128]{3,2,1,0:T(2,128)}), f32[128,15,2,128]{3,2,1,0:T(2,128)S(1)}, u32[]{:S(2)}, u32[]{:S(2)}) async-start(f32[128,15,2,128]{3,2,1,0:T(2,128)} %bitcast.29), calls=%async_computation.2 | async-start | bytes 3932160 | tf_op jit(solution)/shard_map/all_to_all | solution.py:332
  30.3 0.0 copy-start.3
  30.3 0.8 copy-done.3
  31.1 2.5 %shard_map.75 = f32[2304,128]{1,0:T(8,128)} custom-call(f32[128,128]{1,0:T(8,128)S(1)} %bitcast.26, f32[3072,128]{1,0:T(8,128)S(1)} %shard_map.74.table_ref), custom_call_target="tpu_custom_call" | custom-call | tf_op jit(solution)/shard_map/pallas_call | solution.py:358
  33.6 25.2 %all-to-all-done.2 = f32[128,15,2,128]{3,2,1,0:T(2,128)S(1)} async-done(((f32[128,15,2,128]{3,2,1,0:T(2,128)}), f32[128,15,2,128]{3,2,1,0:T(2,128)S(1)}, u32[]{:S(2)}, u32[]{:S(2)}) %all-to-all-start.2) | async-done | bytes 1966112 | tf_op jit(solution)/shard_map/all_to_all | solution.py:332
  58.8 5.7 %all-to-all-start.1 = ((f32[128,9,2,128]{3,2,1,0:T(2,128)}), f32[128,9,2,128]{3,2,1,0:T(2,128)}, u32[]{:S(2)}, u32[]{:S(2)}) async-start(f32[128,9,2,128]{3,2,1,0:T(2,128)} %bitcast.30), calls=%async_computation.1 | async-start | bytes 2359296 | tf_op jit(solution)/shard_map/all_to_all | solution.py:332
  64.6 0.0 copy-start.6
  64.6 0.0 copy-start.5
  64.6 1.1 copy-done.5
  65.8 0.4 shard_map.76.points_ref
  66.2 1.1 copy-done.1
  67.3 19.2 %shard_map.78 = (f32[256,8,256]{2,1,0:T(8,128)}, f32[1536,128]{1,0:T(8,128)}) custom-call(s32[8,256]{1,0:T(8,128)S(1)} %get-tuple-element.10.plan_ref, s32[256]{0:T(256)S(1)} %copy-done.6, f32[3840,128]{1,0:T(8,128)S(1)} %bitcast.24, f32[2,2048,128]{2,1,0:T(8,128)S(1)} %shard_map.76.points_ref, f32[256,256]{1,0:T(8,128)} %refs_0_.1), custom_call_target="tpu_custom_call" | custom-call | tf_op jit(solution)/shard_map/pallas_call | solution.py:396
  86.5 0.0 copy-start.4
  86.5 12.0 %shard_map.79 = f32[1536,128]{1,0:T(8,128)} custom-call(s32[8,256]{1,0:T(8,128)S(1)} %get-tuple-element.10.plan_ref, s32[256]{0:T(256)S(1)} %copy-done.6, f32[2304,128]{1,0:T(8,128)} %bitcast.11.fetched_ref, f32[2,2048,128]{2,1,0:T(8,128)S(1)} %shard_map.76.points_ref, f32[256,256]{1,0:T(8,128)} %refs_0_.1, f32[256,8,256]{2,1,0:T(8,128)} %get-tuple-element.11.refs_1_, ...), custom_call_target="tpu_custom_call" | custom-call | tf_op jit(solution)/shard_map/pallas_call | solution.py:404
  98.5 11.1 %all-to-all-start.3 = ((f32[128,3,4,128]{3,2,1,0:T(4,128)}), f32[128,3,4,128]{3,2,1,0:T(4,128)S(1)}, u32[]{:S(2)}, u32[]{:S(2)}) async-start(f32[128,3,4,128]{3,2,1,0:T(4,128)} %bitcast.31), calls=%async_computation.3 | async-start | bytes 1572864 | tf_op jit(solution)/shard_map/all_to_all | solution.py:332
  109.7 0.1 convert_element_type.12
  109.8 16.5 %all-to-all-done.3 = f32[128,3,4,128]{3,2,1,0:T(4,128)S(1)} async-done(((f32[128,3,4,128]{3,2,1,0:T(4,128)}), f32[128,3,4,128]{3,2,1,0:T(4,128)S(1)}, u32[]{:S(2)}, u32[]{:S(2)}) %all-to-all-start.3) | async-done | bytes 786464 | tf_op jit(solution)/shard_map/all_to_all | solution.py:332
  126.2 0.1 copy.11
  126.4 1.7 %fusion.1 = f32[384,3,128]{2,0,1:T(8,128)} fusion(f32[512,3,128]{2,0,1:T(8,128)S(1)} %bitcast.33, s32[512]{0:T(512)S(1)} %convert_element_type.12), kind=kOutput, calls=%fused_computation.2 | convolution fusion | flops 906166272 | bytes 1378304 | tf_op jit(solution)/shard_map/bp,pcn->bcn/dot_general | solution.py:415
  (9 shorter events, 0.0 us)
Async XLA Ops:
  1.8 21.3 %all-to-all-start = ((f32[128,1,128]{2,1,0:T(1,128)}), f32[128,1,128]{2,1,0:T(1,128)S(1)}, u32[]{:S(2)}, u32[]{:S(2)}) async-start(f32[128,1,128]{2,1,0:T(1,128)} %bitcast.3), calls=%async_computation | async-start | bytes 131072 | tf_op jit(solution)/shard_map/all_to_all | solution.py:332
  23.1 3.0 %copy-start.2 = (f32[128,1,128]{2,1,0:T(1,128)}, f32[128,1,128]{2,1,0:T(1,128)S(1)}, u32[]{:S(2)}) copy-start(f32[128,1,128]{2,1,0:T(1,128)S(1)} %all-to-all-done) | copy-start | bytes 196612
  26.1 32.7 %all-to-all-start.2 = ((f32[128,15,2,128]{3,2,1,0:T(2,128)}), f32[128,15,2,128]{3,2,1,0:T(2,128)S(1)}, u32[]{:S(2)}, u32[]{:S(2)}) async-start(f32[128,15,2,128]{3,2,1,0:T(2,128)} %bitcast.29), calls=%async_computation.2 | async-start | bytes 3932160 | tf_op jit(solution)/shard_map/all_to_all | solution.py:332
  30.3 0.8 copy-start.3
  58.8 5.7 %copy-start = (f32[128,15,2,128]{3,2,1,0:T(2,128)}, f32[128,15,2,128]{3,2,1,0:T(2,128)S(1)}, u32[]{:S(2)}) copy-start(f32[128,15,2,128]{3,2,1,0:T(2,128)S(1)} %all-to-all-done.2) | copy-start | bytes 5898244
  58.8 27.6 %all-to-all-start.1 = ((f32[128,9,2,128]{3,2,1,0:T(2,128)}), f32[128,9,2,128]{3,2,1,0:T(2,128)}, u32[]{:S(2)}, u32[]{:S(2)}) async-start(f32[128,9,2,128]{3,2,1,0:T(2,128)} %bitcast.30), calls=%async_computation.1 | async-start | bytes 2359296 | tf_op jit(solution)/shard_map/all_to_all | solution.py:332
  64.6 1.5 %copy-start.6 = (s32[256]{0:T(256)S(1)}, s32[256]{0:T(256)}, u32[]{:S(2)}) copy-start(s32[256]{0:T(256)} %count_ref.3) | copy-start | bytes 3076
  64.6 1.1 copy-start.5
  65.7 1.5 %copy-start.1 = (f32[128,15,2,128]{3,2,1,0:T(2,128)S(1)}, f32[128,15,2,128]{3,2,1,0:T(2,128)}, u32[]{:S(2)}) copy-start(f32[128,15,2,128]{3,2,1,0:T(2,128)} %copy-done) | copy-start | bytes 5898244
  86.5 23.1 %copy-start.4 = (f32[128,1,128]{2,1,0:T(1,128)S(1)}, f32[128,1,128]{2,1,0:T(1,128)}, u32[]{:S(2)}) copy-start(f32[128,1,128]{2,1,0:T(1,128)} %copy-done.2) | copy-start | bytes 196612
  98.5 27.7 %all-to-all-start.3 = ((f32[128,3,4,128]{3,2,1,0:T(4,128)}), f32[128,3,4,128]{3,2,1,0:T(4,128)S(1)}, u32[]{:S(2)}, u32[]{:S(2)}) async-start(f32[128,3,4,128]{3,2,1,0:T(4,128)} %bitcast.31), calls=%async_computation.3 | async-start | bytes 1572864 | tf_op jit(solution)/shard_map/all_to_all | solution.py:332

commit v7 on v6

--- a/solution.py
+++ b/solution.py
@@ -9,6 +9,7 @@
 AXES = ("gx", "gy")
 WIDE = 16
 SETS = 8
+CHUNKS = 4
 
 
 def strict_upper(size):
@@ -69,6 +70,7 @@
         start,
         dev * (3 * capacity) + rank,
         jnp.broadcast_to(count, (1, segs)),
+        dev * 3.0,
     )
     plan_ref[...] = jnp.zeros_like(plan_ref)
     for i, value in enumerate(rows):
@@ -88,9 +90,10 @@
     lax.fori_loop(0, blocks // 8, one_block, 0, unroll=4)
 
 
-def gather_kernel(devices, capacity, first, ids_ref, table_ref, out_ref, turned, local_ref, sem):
-    turned[...] = ids_ref[...].T[: 2 * capacity].astype(jnp.int32)
-    copy = pltpu.make_async_copy(turned, local_ref, sem)
+def gather_kernel(devices, capacity, first, ids_ref, table_ref, *refs):
+    far_ref, turned_ref, near_ref, local_ref, sem, sems = refs
+    turned_ref[...] = ids_ref[...].T[: 2 * capacity].astype(jnp.int32)
+    copy = pltpu.make_async_copy(turned_ref, local_ref, sem)
     copy.start()
     copy.wait()
     if first:
@@ -104,10 +107,18 @@
         for side, rank, start, step in parts:
             local = local_ref[side * capacity + rank, dev]
             patch = table_ref[pl.ds(pl.multiple_of(local * 8, 8), 8), :]
-            out_ref[pl.ds(dev * rows + start, 6, stride=step), :] = patch[:6]
+            near_ref[pl.ds(dev * rows + start, 6, stride=step), :] = patch[:6]
         return carry
 
-    lax.fori_loop(0, devices, one_device, 0, unroll=4)
+    part = devices // CHUNKS
+    stores = []
+    for chunk in range(CHUNKS):
+        lax.fori_loop(chunk * part, (chunk + 1) * part, one_device, 0, unroll=4)
+        here = pl.ds(chunk * part * rows, part * rows)
+        stores.append(pltpu.make_async_copy(near_ref.at[here], far_ref.at[here], sems.at[chunk]))
+        stores[-1].start()
+    for store in stores:
+        store.wait()
 
 
 def pack_kernel(points_ref, out_ref):
@@ -148,7 +159,7 @@
     high = disp.astype(jnp.bfloat16).astype(jnp.float32)
     lhs = jnp.concatenate([high, disp - high], axis=0)
     lhs = jnp.concatenate([lhs, lhs], axis=1).astype(jnp.bfloat16)
-    return stacked.T.astype(jnp.bfloat16), lhs
+    return stacked.astype(jnp.bfloat16).T, lhs
 
 
 def points_of(points_ref, s):
@@ -207,7 +218,7 @@
     lax.fori_loop(0, segs // (2 * WIDE), one_group, 0)
 
 
-def secondary_pass(step, capacity, low, end, wait, refs):
+def secondary_pass(step, apart, base_row, low, end, wait, refs):
     plan_ref, count_ref, fetched_ref, points_ref, weights_ref, other_ref = refs[:6]
     out_ref, both_ref, lhs_ref, left_ref = refs[6:]
 
@@ -240,14 +251,13 @@
             result = dot_last(both, left)
             result = (result[:half] + result[half:]).T
             result = result[:8] + result[8:]
-        out_ref[pl.ds(entry(3, place), 3, stride=capacity), :] = result[3:6]
-
-    for i in range(SETS):
+        out_ref[pl.ds(entry(base_row, place), 3, stride=apart), :] = result[3:6]
+
+    for i in range(2 * SETS):
         first(i, i)
     wait()
     for i in range(SETS):
         second(i, i)
-        first(SETS + i, SETS + i)
 
     def one_group(g, carry):
         base = g * (3 * SETS)
@@ -272,7 +282,8 @@
     store.start()
     secondary_pass(
         1,
-        capacity,
+        1,
+        5,
         0,
         plan_ref[4, 0],
         load.wait,
@@ -288,10 +299,12 @@
     loads = [
         pltpu.make_async_copy(far_other_ref, other_ref, sems.at[0]),
         pltpu.make_async_copy(far_weights_ref, weights_ref, sems.at[1]),
-        pltpu.make_async_copy(before_ref, out_ref, sems.at[2]),
     ]
     for load in loads:
         load.start()
+    out_ref[...] = jnp.zeros_like(out_ref)
+    for row in range(0, before_ref.shape[0], 8):
+        out_ref[pl.ds(row * capacity, 8, stride=capacity), :] = before_ref[row : row + 8, :]
 
     def wait():
         for load in loads:
@@ -300,12 +313,32 @@
     secondary_pass(
         capacity - 1,
         capacity,
+        3,
         plan_ref[4, 0],
         plan_ref.shape[1],
         wait,
         (plan_ref, count_ref, fetched_ref, points_ref, weights_ref, other_ref)
         + (out_ref, both_ref, lhs_ref, left_ref),
     )
+
+
+def assemble_kernel(capacity, blocks, ids_ref, in_ref, out_ref):
+    devices = ids_ref.shape[1]
+    block = lax.broadcasted_iota(jnp.int32, (blocks, devices), 0)
+    select, rows = [], []
+    for rank in range(capacity):
+        select.append(jnp.where(block == ids_ref[rank : rank + 1, :], 1.0, 0.0))
+        step = 3 * capacity
+        parts = [in_ref[pl.ds(c * capacity + rank, devices, stride=step), :] for c in range(3)]
+        rows.append(jnp.concatenate(parts, axis=1))
+    select = jnp.concatenate(select, axis=1).astype(jnp.bfloat16)
+    total = None
+    for piece in pieces(jnp.concatenate(rows, axis=0)):
+        term = jnp.dot(select, piece.astype(jnp.bfloat16), preferred_element_type=jnp.float32)
+        total = term if total is None else total + term
+    nodes = in_ref.shape[1]
+    for c in range(3):
+        out_ref[c * blocks : (c + 1) * blocks, :] = total[:, c * nodes : (c + 1) * nodes]
 
 
 def body(node_coords, node_disp, qpoints, qweights, qcount, sec_block, pri_block):
@@ -352,24 +385,28 @@
         compiler_params=limit,
     )(far(xc), far(xu))
     received = exchange(request.reshape(devices, 1, 128)).reshape(devices, 128)
-    sec_ids = received[:, :cap].reshape(slots).astype(jnp.int32)
 
     def gather(first, rows):
-        return pl.pallas_call(
+        out, turned = pl.pallas_call(
             functools.partial(gather_kernel, devices, cap, first),
-            out_shape=pltpu.HBM((devices * rows, nodes), f32),
+            out_shape=(
+                pltpu.HBM((devices * rows, nodes), f32),
+                jax.ShapeDtypeStruct((2 * cap, devices), jnp.int32),
+            ),
             in_specs=[vmem, vmem],
-            out_specs=vmem,
+            out_specs=(hbm, vmem),
             scratch_shapes=[
-                pltpu.VMEM((2 * cap, devices), jnp.int32),
+                pltpu.VMEM((devices * rows, nodes), f32),
                 pltpu.SMEM((2 * cap, devices), jnp.int32),
                 pltpu.SemaphoreType.DMA,
+                pltpu.SemaphoreType.DMA((CHUNKS,)),
             ],
             compiler_params=limit,
-        )(received, near(table)).reshape(devices, rows // 2, 2, nodes)
-
-    out1 = gather(True, 6 * cap + 6)
-    out2 = gather(False, 6 * cap - 6)
+        )(received, near(table))
+        return out.reshape(devices, rows // 2, 2, nodes), turned
+
+    out1, turned = gather(True, 6 * cap + 6)
+    out2, _ = gather(False, 6 * cap - 6)
     in1 = near(exchange(out1).reshape(-1, nodes))
     in2 = near(exchange(out2).reshape(-1, nodes))
     points = pl.pallas_call(
@@ -391,11 +428,13 @@
             pltpu.SemaphoreType.DMA((sems,)),
         ]
 
-    parcel = pltpu.HBM((devices * 3 * cap, nodes), f32)
     weights = far(qweights)
     other, parcels = pl.pallas_call(
         functools.partial(early_kernel, cap),
-        out_shape=(pltpu.HBM((segs, 8, quad), f32), parcel),
+        out_shape=(
+            pltpu.HBM((segs, 8, quad), f32),
+            jax.ShapeDtypeStruct((devices * 3, nodes), f32),
+        ),
         in_specs=[smem, smem, vmem, vmem, hbm],
         out_specs=(hbm, vmem),
         scratch_shapes=scratch(max(2 * WIDE, 3 * SETS), 2),
@@ -403,16 +442,21 @@
     )(plan, qcount, in1, points, weights)
     parcels = pl.pallas_call(
         functools.partial(late_kernel, cap),
-        out_shape=parcel,
-        in_specs=[smem, smem, vmem, vmem, hbm, hbm, hbm],
+        out_shape=pltpu.VMEM((devices * 3 * cap, nodes), f32),
+        in_specs=[smem, smem, vmem, vmem, hbm, hbm, vmem],
         out_specs=vmem,
-        scratch_shapes=scratch(3 * SETS, 3),
-        compiler_params=limit,
-    )(plan, qcount, in2, points, weights, far(other), far(parcels))
-    incoming = exchange(parcels.reshape(devices, 3, cap, nodes))
-    select = (jnp.arange(blocks, dtype=jnp.int32)[:, None] == sec_ids[None, :]).astype(f32)
-    incoming = jnp.transpose(incoming, (0, 2, 1, 3)).reshape(slots, 3, nodes)
-    return jnp.einsum("bp,pcn->bcn", select, incoming, precision=lax.Precision.HIGHEST)
+        scratch_shapes=scratch(3 * SETS, 2),
+        compiler_params=limit,
+    )(plan, qcount, in2, points, weights, far(other), parcels)
+    incoming = exchange(parcels.reshape(devices, 3, cap, nodes)).reshape(-1, nodes)
+    gap = pl.pallas_call(
+        functools.partial(assemble_kernel, cap, blocks),
+        out_shape=jax.ShapeDtypeStruct((3 * blocks, nodes), f32),
+        in_specs=[vmem, vmem],
+        out_specs=vmem,
+        compiler_params=limit,
+    )(turned, near(incoming))
+    return jnp.transpose(gap.reshape(3, blocks, nodes), (1, 0, 2))
 
 
 def solution(mesh):

time: 129 us -> 124 us (0.961)
  blocking collectives: 0 us -> 26.7 us
  waiting for transfers between devices: 50.1 us -> 34 us
  starting transfers between devices: 32.5 us -> 21.4 us
  Pallas kernels: 40.3 us -> 38.2 us
  matrix products: 1.67 us -> 0 us
    all_to_all x0 -> x1, blocking collectives: none -> 26.7 us  [exchange(): return lax.all_to_all(value, AXES, split_axis=0, concat_axis=0, tiled=True)]
    all_to_all x4 -> x3, waiting for transfers between devices: 50.1 us -> 34 us  [exchange(): return lax.all_to_all(value, AXES, split_axis=0, concat_axis=0, tiled=True)]
    all_to_all x4 -> x3, starting transfers between devices: 32.5 us -> 21.4 us  [exchange(): return lax.all_to_all(value, AXES, split_axis=0, concat_axis=0, tiled=True)]
    pallas_call x1, Pallas kernels: 19.2 us -> 17 us  [body(): pl.pallas_call(functools.partial(early_kernel, cap), out_shape=(pltpu.HBM...]
    dot_general x1 -> x0, matrix products: 1.67 us -> none  [body(): jnp.einsum('bp,pcn->bcn', select, incoming, precision=lax.Precision.HIGHEST)]
    pallas_call x1 -> x2, Pallas kernels: 12 us -> 12.2 us  [the longest x1 10.6 us: body(): pl.pallas_call(functools.partial(late_kernel, cap), out_shape=pltpu.VMEM(...]
    unnamed x14 -> x12, local copies, waits for them, and re-layouts: 3.13 us -> 3.12 us
  transfers between devices with their start and end apart: 4 -> 3, of which waited for: 3 -> 3; matrix products, arithmetic and copies ran while one was open for 0% -> 0% of each run, Pallas kernels for 18% -> 18%
where the time goes in v7:
time: 124 us
  Pallas kernels  38.2 us (31%)
  waiting for transfers between devices  34 us (27%)
  blocking collectives  26.7 us (22%)
  starting transfers between devices  21.4 us (17%)
  local copies, waits for them, and re-layouts  3.12 us (3%)
    all_to_all x3, waiting for transfers between devices, exchange(): return lax.all_to_all(value, AXES, split_axis=0, concat_axis=0, tiled=True)  34 us
    all_to_all x1, blocking collectives, exchange(): return lax.all_to_all(value, AXES, split_axis=0, concat_axis=0, tiled=True)  26.7 us
    all_to_all x3, starting transfers between devices, exchange(): return lax.all_to_all(value, AXES, split_axis=0, concat_axis=0, tiled=True)  21.4 us
    pallas_call x1, Pallas kernels, body(): pl.pallas_call(functools.partial(early_kernel, cap), out_shape=(pltpu.HBM...  17 us
    pallas_call x1, Pallas kernels, body(): pl.pallas_call(functools.partial(late_kernel, cap), out_shape=pltpu.VMEM(...  10.6 us
    pallas_call x2, Pallas kernels, gather(): pl.pallas_call(functools.partial(gather_kernel, devices, cap, first), out...  5.32 us
    unnamed x12, local copies, waits for them, and re-layouts  3.12 us
  transfers between devices with their start and end apart: 3, of which 3 were waited for; matrix products, arithmetic and copies ran while one was open for 0% of the time, Pallas kernels for 18%

profile of v7, /device:TPU:1, one launch (start us, length us, event | category | flops | bytes accessed | tf_op | source)
XLA Modules:
  0.0 123.6 jit_solution(5755010129680837555)
XLA Ops:
  0.0 1.8 %shard_map.73 = (s32[8,256]{1,0:T(8,128)S(1)}, f32[128,128]{1,0:T(8,128)}) custom-call(s32[1,256]{1,0:T(1,128)} %bitcast.32, s32[1,256]{1,0:T(1,128)} %bitcast.33), custom_call_target="tpu_custom_call" | custom-call | tf_op jit(solution)/shard_map/pallas_call | solution.py:367
  1.8 11.5 %all-to-all-start = ((f32[128,1,128]{2,1,0:T(1,128)}), f32[128,1,128]{2,1,0:T(1,128)S(1)}, u32[]{:S(2)}, u32[]{:S(2)}) async-start(f32[128,1,128]{2,1,0:T(1,128)} %bitcast.3), calls=%async_computation | async-start | bytes 131072 | tf_op jit(solution)/shard_map/all_to_all | solution.py:365
  13.3 1.5 %shard_map.74.table_ref = f32[3072,128]{1,0:T(8,128)S(1)} custom-call(f32[1152,128]{1,0:T(8,128)} %bitcast.30, f32[1152,128]{1,0:T(8,128)} %bitcast.31), custom_call_target="tpu_custom_call" | custom-call | tf_op jit(solution)/shard_map/pallas_call | solution.py:380
  14.8 8.3 %all-to-all-done = f32[128,1,128]{2,1,0:T(1,128)S(1)} async-done(((f32[128,1,128]{2,1,0:T(1,128)}), f32[128,1,128]{2,1,0:T(1,128)S(1)}, u32[]{:S(2)}, u32[]{:S(2)}) %all-to-all-start) | async-done | bytes 65568 | tf_op jit(solution)/shard_map/all_to_all | solution.py:365
  23.1 2.5 %shard_map.75 = (f32[3840,128]{1,0:T(8,128)}, s32[8,128]{1,0:T(8,128)S(1)}) custom-call(f32[128,128]{1,0:T(8,128)S(1)} %bitcast.26, f32[3072,128]{1,0:T(8,128)S(1)} %shard_map.74.table_ref), custom_call_target="tpu_custom_call" | custom-call | tf_op jit(solution)/shard_map/pallas_call | solution.py:390
  25.6 0.0 copy-done.3
  25.6 4.2 %all-to-all-start.2 = ((f32[128,15,2,128]{3,2,1,0:T(2,128)}), f32[128,15,2,128]{3,2,1,0:T(2,128)S(1)}, u32[]{:S(2)}, u32[]{:S(2)}) async-start(f32[128,15,2,128]{3,2,1,0:T(2,128)} %bitcast.28), calls=%async_computation.2 | async-start | bytes 3932160 | tf_op jit(solution)/shard_map/all_to_all | solution.py:365
  29.8 0.0 copy-start.4
  29.8 0.8 copy-done.4
  30.6 2.8 %shard_map.76 = (f32[2304,128]{1,0:T(8,128)}, s32[8,128]{1,0:T(8,128)}) custom-call(f32[128,128]{1,0:T(8,128)S(1)} %bitcast.27, f32[3072,128]{1,0:T(8,128)S(1)} %shard_map.74.table_ref), custom_call_target="tpu_custom_call" | custom-call | tf_op jit(solution)/shard_map/pallas_call | solution.py:390
  33.4 24.9 %all-to-all-done.2 = f32[128,15,2,128]{3,2,1,0:T(2,128)S(1)} async-done(((f32[128,15,2,128]{3,2,1,0:T(2,128)}), f32[128,15,2,128]{3,2,1,0:T(2,128)S(1)}, u32[]{:S(2)}, u32[]{:S(2)}) %all-to-all-start.2) | async-done | bytes 1966112 | tf_op jit(solution)/shard_map/all_to_all | solution.py:365
  58.4 5.7 %all-to-all-start.1 = ((f32[128,9,2,128]{3,2,1,0:T(2,128)}), f32[128,9,2,128]{3,2,1,0:T(2,128)}, u32[]{:S(2)}, u32[]{:S(2)}) async-start(f32[128,9,2,128]{3,2,1,0:T(2,128)} %bitcast.29), calls=%async_computation.1 | async-start | bytes 2359296 | tf_op jit(solution)/shard_map/all_to_all | solution.py:365
  64.1 0.0 copy-done
  64.1 0.0 copy-start.5
  64.1 0.0 copy-start.2
  64.1 1.1 copy-done.2
  65.3 0.4 shard_map.77.points_ref
  65.7 0.0 copy-done.5
  65.7 1.1 copy-done.1
  66.8 17.0 %shard_map.78 = (f32[256,8,256]{2,1,0:T(8,128)}, f32[384,128]{1,0:T(8,128)S(1)}) custom-call(s32[8,256]{1,0:T(8,128)S(1)} %get-tuple-element.14.plan_ref, s32[256]{0:T(256)S(1)} %copy-done.5, f32[3840,128]{1,0:T(8,128)S(1)} %bitcast.22, f32[2,2048,128]{2,1,0:T(8,128)S(1)} %shard_map.77.points_ref, f32[256,256]{1,0:T(8,128)} %refs_0_.1), custom_call_target="tpu_custom_call" | custom-call | tf_op jit(solution)/shard_map/pallas_call | solution.py:432
  83.9 0.8 all-to-all-done.1
  84.6 10.6 %shard_map.79 = f32[1536,128]{1,0:T(8,128)S(1)} custom-call(s32[8,256]{1,0:T(8,128)S(1)} %get-tuple-element.14.plan_ref, s32[256]{0:T(256)S(1)} %copy-done.5, f32[2304,128]{1,0:T(8,128)} %bitcast.10.fetched_ref, f32[2,2048,128]{2,1,0:T(8,128)S(1)} %shard_map.77.points_ref, f32[256,256]{1,0:T(8,128)} %refs_0_.1, f32[256,8,256]{2,1,0:T(8,128)} %get-tuple-element.17.refs_1_, ...), custom_call_target="tpu_custom_call" | custom-call | tf_op jit(solution)/shard_map/pallas_call | solution.py:443
  95.2 26.7 %all_to_all.20 = f32[128,3,4,128]{3,2,1,0:T(4,128)S(1)} all-to-all(f32[128,3,4,128]{3,2,1,0:T(4,128)S(1)} %bitcast.24), channel_id=1, replica_groups=mesh['gx'=8,'gy'=16] {'gx','gy'}, dimensions={0} | all-to-all | bytes 1572864 | tf_op jit(solution)/shard_map/all_to_all | solution.py:365
  122.0 1.6 %shard_map.80 = f32[1152,128]{1,0:T(8,128)} custom-call(s32[8,128]{1,0:T(8,128)S(1)} %get-tuple-element.13.ids_ref, f32[1536,128]{1,0:T(8,128)S(1)} %bitcast.23), custom_call_target="tpu_custom_call" | custom-call | tf_op jit(solution)/shard_map/pallas_call | solution.py:452
  (3 shorter events, 0.0 us)
Async XLA Ops:
  1.8 21.3 %all-to-all-start = ((f32[128,1,128]{2,1,0:T(1,128)}), f32[128,1,128]{2,1,0:T(1,128)S(1)}, u32[]{:S(2)}, u32[]{:S(2)}) async-start(f32[128,1,128]{2,1,0:T(1,128)} %bitcast.3), calls=%async_computation | async-start | bytes 131072 | tf_op jit(solution)/shard_map/all_to_all | solution.py:365
  23.1 2.5 %copy-start.3 = (f32[128,1,128]{2,1,0:T(1,128)}, f32[128,1,128]{2,1,0:T(1,128)S(1)}, u32[]{:S(2)}) copy-start(f32[128,1,128]{2,1,0:T(1,128)S(1)} %all-to-all-done) | copy-start | bytes 196612
  25.6 32.7 %all-to-all-start.2 = ((f32[128,15,2,128]{3,2,1,0:T(2,128)}), f32[128,15,2,128]{3,2,1,0:T(2,128)S(1)}, u32[]{:S(2)}, u32[]{:S(2)}) async-start(f32[128,15,2,128]{3,2,1,0:T(2,128)} %bitcast.28), calls=%async_computation.2 | async-start | bytes 3932160 | tf_op jit(solution)/shard_map/all_to_all | solution.py:365
  29.8 0.8 copy-start.4
  58.4 5.7 %copy-start = (f32[128,15,2,128]{3,2,1,0:T(2,128)}, f32[128,15,2,128]{3,2,1,0:T(2,128)S(1)}, u32[]{:S(2)}) copy-start(f32[128,15,2,128]{3,2,1,0:T(2,128)S(1)} %all-to-all-done.2) | copy-start | bytes 5898244
  58.4 26.3 %all-to-all-start.1 = ((f32[128,9,2,128]{3,2,1,0:T(2,128)}), f32[128,9,2,128]{3,2,1,0:T(2,128)}, u32[]{:S(2)}, u32[]{:S(2)}) async-start(f32[128,9,2,128]{3,2,1,0:T(2,128)} %bitcast.29), calls=%async_computation.1 | async-start | bytes 2359296 | tf_op jit(solution)/shard_map/all_to_all | solution.py:365
  64.1 1.5 %copy-start.5 = (s32[256]{0:T(256)S(1)}, s32[256]{0:T(256)}, u32[]{:S(2)}) copy-start(s32[256]{0:T(256)} %count_ref.3) | copy-start | bytes 3076
  64.1 1.1 copy-start.2
  65.3 1.5 %copy-start.1 = (f32[128,15,2,128]{3,2,1,0:T(2,128)S(1)}, f32[128,15,2,128]{3,2,1,0:T(2,128)}, u32[]{:S(2)}) copy-start(f32[128,15,2,128]{3,2,1,0:T(2,128)} %copy-done) | copy-start | bytes 5898244

commit v8 on v7

--- a/solution.py
+++ b/solution.py
@@ -8,7 +8,8 @@
 
 AXES = ("gx", "gy")
 WIDE = 16
-SETS = 8
+EARLY_SETS = 7
+LATE_SETS = 8
 CHUNKS = 4
 
 
@@ -191,7 +192,8 @@
     return sums[:8] + sums[8:]
 
 
-def primary_pass(capacity, plan_ref, fetched_ref, points_ref, other_ref, both_ref, lhs_ref):
+def primary_pass(capacity, follow, refs):
+    plan_ref, fetched_ref, points_ref, other_ref, both_ref, lhs_ref = refs
     segs = plan_ref.shape[1]
 
     def first(s, i):
@@ -204,21 +206,29 @@
     for i in range(WIDE):
         first(i, i)
 
-    def one_group(g, carry):
+    def one_group(g, last):
         base = g * (2 * WIDE)
-        after = jnp.minimum(base + 2 * WIDE, segs - WIDE)
         for i in range(WIDE):
             second(base + i, i)
             first(base + WIDE + i, WIDE + i)
         for i in range(WIDE):
             second(base + WIDE + i, WIDE + i)
-            first(after + i, i)
+            if last:
+                follow(i)
+            else:
+                first(base + 2 * WIDE + i, i)
+
+    groups = segs // (2 * WIDE)
+
+    def full_group(g, carry):
+        one_group(g, False)
         return carry
 
-    lax.fori_loop(0, segs // (2 * WIDE), one_group, 0)
-
-
-def secondary_pass(step, apart, base_row, low, end, wait, refs):
+    lax.fori_loop(0, groups - 1, full_group, 0)
+    one_group(groups - 1, True)
+
+
+def secondary_pass(step, apart, base_row, low, end, sets, refs):
     plan_ref, count_ref, fetched_ref, points_ref, weights_ref, other_ref = refs[:6]
     out_ref, both_ref, lhs_ref, left_ref = refs[6:]
 
@@ -253,23 +263,34 @@
             result = result[:8] + result[8:]
         out_ref[pl.ds(entry(base_row, place), 3, stride=apart), :] = result[3:6]
 
-    for i in range(2 * SETS):
-        first(i, i)
-    wait()
-    for i in range(SETS):
-        second(i, i)
-
-    def one_group(g, carry):
-        base = g * (3 * SETS)
+    def begin(i):
+        if i < 2 * sets:
+            first(i, i)
+
+    def one_group(g, last):
+        base = g * (3 * sets)
         for phase in range(3):
-            for i in range(SETS):
-                a, b, c = (phase * SETS + SETS * t + i for t in (2, 1, 0))
+            for i in range(sets):
+                a, b, c = (phase * sets + sets * t + i for t in (2, 1, 0))
                 third(base + c, c)
-                second(base + b, b % (3 * SETS))
-                first(base + a, a % (3 * SETS))
-        return carry
-
-    lax.fori_loop(0, (end - low + 3 * SETS - 1) // (3 * SETS), one_group, 0)
+                if not last or b < 3 * sets:
+                    second(base + b, b % (3 * sets))
+                if not last or a < 3 * sets:
+                    first(base + a, a % (3 * sets))
+
+    def finish():
+        for i in range(sets):
+            second(i, i)
+        groups = (end - low + 3 * sets - 1) // (3 * sets)
+
+        def full_group(g, carry):
+            one_group(g, False)
+            return carry
+
+        lax.fori_loop(0, groups - 1, full_group, 0)
+        one_group(groups - 1, True)
+
+    return begin, finish
 
 
 def early_kernel(capacity, plan_ref, count_ref, fetched_ref, points_ref, far_weights_ref, *refs):
@@ -278,18 +299,22 @@
     store = pltpu.make_async_copy(other_ref, far_other_ref, sems.at[1])
     load.start()
     out_ref[...] = jnp.zeros_like(out_ref)
-    primary_pass(capacity, plan_ref, fetched_ref, points_ref, other_ref, both_ref, lhs_ref)
-    store.start()
-    secondary_pass(
+    begin, finish = secondary_pass(
         1,
         1,
         5,
         0,
         plan_ref[4, 0],
-        load.wait,
+        EARLY_SETS,
         (plan_ref, count_ref, fetched_ref, points_ref, weights_ref, other_ref)
         + (out_ref, both_ref, lhs_ref, left_ref),
     )
+    primary_pass(
+        capacity, begin, (plan_ref, fetched_ref, points_ref, other_ref, both_ref, lhs_ref)
+    )
+    store.start()
+    load.wait()
+    finish()
     store.wait()
 
 
@@ -306,20 +331,21 @@
     for row in range(0, before_ref.shape[0], 8):
         out_ref[pl.ds(row * capacity, 8, stride=capacity), :] = before_ref[row : row + 8, :]
 
-    def wait():
-        for load in loads:
-            load.wait()
-
-    secondary_pass(
+    begin, finish = secondary_pass(
         capacity - 1,
         capacity,
         3,
         plan_ref[4, 0],
         plan_ref.shape[1],
-        wait,
+        LATE_SETS,
         (plan_ref, count_ref, fetched_ref, points_ref, weights_ref, other_ref)
         + (out_ref, both_ref, lhs_ref, left_ref),
     )
+    for i in range(2 * LATE_SETS):
+        begin(i)
+    for load in loads:
+        load.wait()
+    finish()
 
 
 def assemble_kernel(capacity, blocks, ids_ref, in_ref, out_ref):
@@ -422,7 +448,7 @@
         return [
             pltpu.VMEM((count, 2 * nodes, quad), jnp.bfloat16),
             pltpu.VMEM((count, 16, 2 * nodes), jnp.bfloat16),
-            pltpu.VMEM((3 * SETS, 16, quad), jnp.bfloat16),
+            pltpu.VMEM((count, 16, quad), jnp.bfloat16),
             pltpu.VMEM((segs, 8, quad), f32),
             pltpu.VMEM((segs, quad), f32),
             pltpu.SemaphoreType.DMA((sems,)),
@@ -437,7 +463,7 @@
         ),
         in_specs=[smem, smem, vmem, vmem, hbm],
         out_specs=(hbm, vmem),
-        scratch_shapes=scratch(max(2 * WIDE, 3 * SETS), 2),
+        scratch_shapes=scratch(max(2 * WIDE, 3 * EARLY_SETS), 2),
         compiler_params=limit,
     )(plan, qcount, in1, points, weights)
     parcels = pl.pallas_call(
@@ -445,7 +471,7 @@
         out_shape=pltpu.VMEM((devices * 3 * cap, nodes), f32),
         in_specs=[smem, smem, vmem, vmem, hbm, hbm, vmem],
         out_specs=vmem,
-        scratch_shapes=scratch(3 * SETS, 2),
+        scratch_shapes=scratch(3 * LATE_SETS, 2),
         compiler_params=limit,
     )(plan, qcount, in2, points, weights, far(other), parcels)
     incoming = exchange(parcels.reshape(devices, 3, cap, nodes)).reshape(-1, nodes)

time: 124 us -> 122 us (0.984)
  blocking collectives: 26.7 us -> 25.2 us
    all_to_all x1, blocking collectives: 26.7 us -> 25.2 us  [exchange(): return lax.all_to_all(value, AXES, split_axis=0, concat_axis=0, tiled=True)]
  transfers between devices with their start and end apart: 3 -> 3, of which waited for: 3 -> 3; matrix products, arithmetic and copies ran while one was open for 0% -> 0% of each run, Pallas kernels for 18% -> 17%
where the time goes in v8:
time: 122 us
  Pallas kernels  37.7 us (31%)
  waiting for transfers between devices  34.4 us (28%)
  blocking collectives  25.2 us (21%)
  starting transfers between devices  21.4 us (18%)
  local copies, waits for them, and re-layouts  3.12 us (3%)
    all_to_all x3, waiting for transfers between devices, exchange(): return lax.all_to_all(value, AXES, split_axis=0, concat_axis=0, tiled=True)  34.4 us
    all_to_all x1, blocking collectives, exchange(): return lax.all_to_all(value, AXES, split_axis=0, concat_axis=0, tiled=True)  25.2 us
    all_to_all x3, starting transfers between devices, exchange(): return lax.all_to_all(value, AXES, split_axis=0, concat_axis=0, tiled=True)  21.4 us
    pallas_call x1, Pallas kernels, body(): pl.pallas_call(functools.partial(early_kernel, cap), out_shape=(pltpu.HBM...  16.7 us
    pallas_call x1, Pallas kernels, body(): pl.pallas_call(functools.partial(late_kernel, cap), out_shape=pltpu.VMEM(...  10.4 us
    pallas_call x2, Pallas kernels, gather(): pl.pallas_call(functools.partial(gather_kernel, devices, cap, first), out...  5.32 us
    unnamed x12, local copies, waits for them, and re-layouts  3.12 us
  transfers between devices with their start and end apart: 3, of which 3 were waited for; matrix products, arithmetic and copies ran while one was open for 0% of the time, Pallas kernels for 17%

profile of v8, /device:TPU:1, one launch (start us, length us, event | category | flops | bytes accessed | tf_op | source)
XLA Modules:
  0.0 121.9 jit_solution(7133787196040662487)
XLA Ops:
  0.0 1.8 %shard_map.73 = (s32[8,256]{1,0:T(8,128)S(1)}, f32[128,128]{1,0:T(8,128)}) custom-call(s32[1,256]{1,0:T(1,128)} %bitcast.32, s32[1,256]{1,0:T(1,128)} %bitcast.33), custom_call_target="tpu_custom_call" | custom-call | tf_op jit(solution)/shard_map/pallas_call | solution.py:393
  1.8 11.5 %all-to-all-start = ((f32[128,1,128]{2,1,0:T(1,128)}), f32[128,1,128]{2,1,0:T(1,128)S(1)}, u32[]{:S(2)}, u32[]{:S(2)}) async-start(f32[128,1,128]{2,1,0:T(1,128)} %bitcast.3), calls=%async_computation | async-start | bytes 131072 | tf_op jit(solution)/shard_map/all_to_all | solution.py:391
  13.3 1.5 %shard_map.74.table_ref = f32[3072,128]{1,0:T(8,128)S(1)} custom-call(f32[1152,128]{1,0:T(8,128)} %bitcast.30, f32[1152,128]{1,0:T(8,128)} %bitcast.31), custom_call_target="tpu_custom_call" | custom-call | tf_op jit(solution)/shard_map/pallas_call | solution.py:406
  14.8 8.3 %all-to-all-done = f32[128,1,128]{2,1,0:T(1,128)S(1)} async-done(((f32[128,1,128]{2,1,0:T(1,128)}), f32[128,1,128]{2,1,0:T(1,128)S(1)}, u32[]{:S(2)}, u32[]{:S(2)}) %all-to-all-start) | async-done | bytes 65568 | tf_op jit(solution)/shard_map/all_to_all | solution.py:391
  23.1 2.5 %shard_map.75 = (f32[3840,128]{1,0:T(8,128)}, s32[8,128]{1,0:T(8,128)S(1)}) custom-call(f32[128,128]{1,0:T(8,128)S(1)} %bitcast.26, f32[3072,128]{1,0:T(8,128)S(1)} %shard_map.74.table_ref), custom_call_target="tpu_custom_call" | custom-call | tf_op jit(solution)/shard_map/pallas_call | solution.py:416
  25.6 0.0 copy-done.3
  25.6 4.2 %all-to-all-start.2 = ((f32[128,15,2,128]{3,2,1,0:T(2,128)}), f32[128,15,2,128]{3,2,1,0:T(2,128)S(1)}, u32[]{:S(2)}, u32[]{:S(2)}) async-start(f32[128,15,2,128]{3,2,1,0:T(2,128)} %bitcast.28), calls=%async_computation.2 | async-start | bytes 3932160 | tf_op jit(solution)/shard_map/all_to_all | solution.py:391
  29.8 0.0 copy-start.4
  29.8 0.8 copy-done.4
  30.6 2.8 %shard_map.76 = (f32[2304,128]{1,0:T(8,128)}, s32[8,128]{1,0:T(8,128)}) custom-call(f32[128,128]{1,0:T(8,128)S(1)} %bitcast.27, f32[3072,128]{1,0:T(8,128)S(1)} %shard_map.74.table_ref), custom_call_target="tpu_custom_call" | custom-call | tf_op jit(solution)/shard_map/pallas_call | solution.py:416
  33.4 24.9 %all-to-all-done.2 = f32[128,15,2,128]{3,2,1,0:T(2,128)S(1)} async-done(((f32[128,15,2,128]{3,2,1,0:T(2,128)}), f32[128,15,2,128]{3,2,1,0:T(2,128)S(1)}, u32[]{:S(2)}, u32[]{:S(2)}) %all-to-all-start.2) | async-done | bytes 1966112 | tf_op jit(solution)/shard_map/all_to_all | solution.py:391
  58.4 5.7 %all-to-all-start.1 = ((f32[128,9,2,128]{3,2,1,0:T(2,128)}), f32[128,9,2,128]{3,2,1,0:T(2,128)}, u32[]{:S(2)}, u32[]{:S(2)}) async-start(f32[128,9,2,128]{3,2,1,0:T(2,128)} %bitcast.29), calls=%async_computation.1 | async-start | bytes 2359296 | tf_op jit(solution)/shard_map/all_to_all | solution.py:391
  64.1 0.0 copy-done
  64.1 0.0 copy-start.5
  64.1 0.0 copy-start.2
  64.1 1.1 copy-done.2
  65.3 0.4 shard_map.77.points_ref
  65.7 0.0 copy-done.5
  65.7 1.1 copy-done.1
  66.8 16.7 %shard_map.78 = (f32[256,8,256]{2,1,0:T(8,128)}, f32[384,128]{1,0:T(8,128)S(1)}) custom-call(s32[8,256]{1,0:T(8,128)S(1)} %get-tuple-element.14.plan_ref, s32[256]{0:T(256)S(1)} %copy-done.5, f32[3840,128]{1,0:T(8,128)S(1)} %bitcast.22, f32[2,2048,128]{2,1,0:T(8,128)S(1)} %shard_map.77.points_ref, f32[256,256]{1,0:T(8,128)} %refs_0_.1), custom_call_target="tpu_custom_call" | custom-call | tf_op jit(solution)/shard_map/pallas_call | solution.py:458
  83.5 1.1 all-to-all-done.1
  84.6 10.4 %shard_map.79 = f32[1536,128]{1,0:T(8,128)S(1)} custom-call(s32[8,256]{1,0:T(8,128)S(1)} %get-tuple-element.14.plan_ref, s32[256]{0:T(256)S(1)} %copy-done.5, f32[2304,128]{1,0:T(8,128)} %bitcast.10.fetched_ref, f32[2,2048,128]{2,1,0:T(8,128)S(1)} %shard_map.77.points_ref, f32[256,256]{1,0:T(8,128)} %refs_0_.1, f32[256,8,256]{2,1,0:T(8,128)} %get-tuple-element.17.refs_1_, ...), custom_call_target="tpu_custom_call" | custom-call | tf_op jit(solution)/shard_map/pallas_call | solution.py:469
  95.1 25.2 %all_to_all.20 = f32[128,3,4,128]{3,2,1,0:T(4,128)S(1)} all-to-all(f32[128,3,4,128]{3,2,1,0:T(4,128)S(1)} %bitcast.24), channel_id=1, replica_groups=mesh['gx'=8,'gy'=16] {'gx','gy'}, dimensions={0} | all-to-all | bytes 1572864 | tf_op jit(solution)/shard_map/all_to_all | solution.py:391
  120.3 1.6 %shard_map.80 = f32[1152,128]{1,0:T(8,128)} custom-call(s32[8,128]{1,0:T(8,128)S(1)} %get-tuple-element.13.ids_ref, f32[1536,128]{1,0:T(8,128)S(1)} %bitcast.23), custom_call_target="tpu_custom_call" | custom-call | tf_op jit(solution)/shard_map/pallas_call | solution.py:478
  (3 shorter events, 0.0 us)
Async XLA Ops:
  1.8 21.3 %all-to-all-start = ((f32[128,1,128]{2,1,0:T(1,128)}), f32[128,1,128]{2,1,0:T(1,128)S(1)}, u32[]{:S(2)}, u32[]{:S(2)}) async-start(f32[128,1,128]{2,1,0:T(1,128)} %bitcast.3), calls=%async_computation | async-start | bytes 131072 | tf_op jit(solution)/shard_map/all_to_all | solution.py:391
  23.1 2.5 %copy-start.3 = (f32[128,1,128]{2,1,0:T(1,128)}, f32[128,1,128]{2,1,0:T(1,128)S(1)}, u32[]{:S(2)}) copy-start(f32[128,1,128]{2,1,0:T(1,128)S(1)} %all-to-all-done) | copy-start | bytes 196612
  25.6 32.7 %all-to-all-start.2 = ((f32[128,15,2,128]{3,2,1,0:T(2,128)}), f32[128,15,2,128]{3,2,1,0:T(2,128)S(1)}, u32[]{:S(2)}, u32[]{:S(2)}) async-start(f32[128,15,2,128]{3,2,1,0:T(2,128)} %bitcast.28), calls=%async_computation.2 | async-start | bytes 3932160 | tf_op jit(solution)/shard_map/all_to_all | solution.py:391
  29.8 0.8 copy-start.4
  58.4 5.7 %copy-start = (f32[128,15,2,128]{3,2,1,0:T(2,128)}, f32[128,15,2,128]{3,2,1,0:T(2,128)S(1)}, u32[]{:S(2)}) copy-start(f32[128,15,2,128]{3,2,1,0:T(2,128)S(1)} %all-to-all-done.2) | copy-start | bytes 5898244
  58.4 26.3 %all-to-all-start.1 = ((f32[128,9,2,128]{3,2,1,0:T(2,128)}), f32[128,9,2,128]{3,2,1,0:T(2,128)}, u32[]{:S(2)}, u32[]{:S(2)}) async-start(f32[128,9,2,128]{3,2,1,0:T(2,128)} %bitcast.29), calls=%async_computation.1 | async-start | bytes 2359296 | tf_op jit(solution)/shard_map/all_to_all | solution.py:391
  64.1 1.5 %copy-start.5 = (s32[256]{0:T(256)S(1)}, s32[256]{0:T(256)}, u32[]{:S(2)}) copy-start(s32[256]{0:T(256)} %count_ref.3) | copy-start | bytes 3076
  64.1 1.1 copy-start.2
  65.3 1.5 %copy-start.1 = (f32[128,15,2,128]{3,2,1,0:T(2,128)S(1)}, f32[128,15,2,128]{3,2,1,0:T(2,128)}, u32[]{:S(2)}) copy-start(f32[128,15,2,128]{3,2,1,0:T(2,128)} %copy-done) | copy-start | bytes 5898244

commit v9 on v8

--- a/solution.py
+++ b/solution.py
@@ -25,13 +25,12 @@
     )
 
 
-def plan_kernel(devices, capacity, blocks, sec_ref, pri_ref, plan_ref, request_ref):
+def route_kernel(devices, capacity, blocks, sec_ref, pri_ref, request_ref, route_ref):
     segs = sec_ref.shape[1]
     upper = strict_upper(segs)
     device = lax.broadcasted_iota(jnp.int32, (devices, segs), 0).astype(jnp.float32)
     column = lax.broadcasted_iota(jnp.int32, (request_ref.shape[1], segs), 0).astype(jnp.float32)
     request = jnp.zeros(request_ref.shape, jnp.float32)
-    routes = []
     for side, ref in enumerate((sec_ref, pri_ref)):
         ids = ref[...].astype(jnp.float32)
         owner = jnp.floor((ids + 0.5) * (1.0 / blocks))
@@ -43,11 +42,17 @@
         coarse = jnp.floor(local * (1.0 / 16.0)) * 16.0
         here = column == rank + side * capacity
         for part in (coarse, local - coarse):
-            request += dot_last(narrow, jnp.where(here, part, 0.0).astype(jnp.bfloat16))
-        routes.append((owner, rank))
+            request += dot_last(narrow, jnp.where(here, 8.0 * part, 0.0).astype(jnp.bfloat16))
+        route_ref[2 * side : 2 * side + 1, :] = owner
+        route_ref[2 * side + 1 : 2 * side + 2, :] = rank
     request_ref[...] = request
 
-    (sec_owner, sec_rank), (pri_owner, pri_rank) = routes
+
+def order_kernel(capacity, route_ref, plan_ref):
+    segs = route_ref.shape[1]
+    upper = strict_upper(segs)
+    sec_owner, sec_rank = route_ref[0:1, :], route_ref[1:2, :]
+    pri_owner, pri_rank = route_ref[2:3, :], route_ref[3:4, :]
     early = jnp.where(sec_rank == 0.0, 1.0, 0.0)
     spread = jnp.broadcast_to(early, (16, segs)).astype(jnp.bfloat16)
     ahead = jnp.dot(spread, upper, preferred_element_type=jnp.float32)[:1]
@@ -106,8 +111,8 @@
 
     def one_device(dev, carry):
         for side, rank, start, step in parts:
-            local = local_ref[side * capacity + rank, dev]
-            patch = table_ref[pl.ds(pl.multiple_of(local * 8, 8), 8), :]
+            row = pl.multiple_of(local_ref[side * capacity + rank, dev], 8)
+            patch = table_ref[pl.ds(row, 8), :]
             near_ref[pl.ds(dev * rows + start, 6, stride=step), :] = patch[:6]
         return carry
 
@@ -348,23 +353,36 @@
     finish()
 
 
-def assemble_kernel(capacity, blocks, ids_ref, in_ref, out_ref):
+def assemble_kernel(capacity, blocks, ids_ref, in_ref, out_ref, near_ref, sems):
     devices = ids_ref.shape[1]
-    block = lax.broadcasted_iota(jnp.int32, (blocks, devices), 0)
-    select, rows = [], []
-    for rank in range(capacity):
-        select.append(jnp.where(block == ids_ref[rank : rank + 1, :], 1.0, 0.0))
-        step = 3 * capacity
-        parts = [in_ref[pl.ds(c * capacity + rank, devices, stride=step), :] for c in range(3)]
-        rows.append(jnp.concatenate(parts, axis=1))
+    block = 8 * lax.broadcasted_iota(jnp.int32, (blocks, devices), 0)
+    nodes = in_ref.shape[1]
+    select = [
+        jnp.where(block == ids_ref[rank : rank + 1, :], 1.0, 0.0) for rank in range(capacity)
+    ]
     select = jnp.concatenate(select, axis=1).astype(jnp.bfloat16)
-    total = None
-    for piece in pieces(jnp.concatenate(rows, axis=0)):
-        term = jnp.dot(select, piece.astype(jnp.bfloat16), preferred_element_type=jnp.float32)
-        total = term if total is None else total + term
-    nodes = in_ref.shape[1]
-    for c in range(3):
-        out_ref[c * blocks : (c + 1) * blocks, :] = total[:, c * nodes : (c + 1) * nodes]
+    step = 3 * capacity
+    stores = []
+    for components in ((0, 1), (2,)):
+        rows = []
+        for rank in range(capacity):
+            parts = [
+                in_ref[pl.ds(c * capacity + rank, devices, stride=step), :] for c in components
+            ]
+            rows.append(jnp.concatenate(parts, axis=1))
+        total = None
+        for piece in pieces(jnp.concatenate(rows, axis=0)):
+            term = jnp.dot(select, piece.astype(jnp.bfloat16), preferred_element_type=jnp.float32)
+            total = term if total is None else total + term
+        for i, c in enumerate(components):
+            near_ref[c * blocks : (c + 1) * blocks, :] = total[:, i * nodes : (i + 1) * nodes]
+        here = pl.ds(components[0] * blocks, len(components) * blocks)
+        stores.append(
+            pltpu.make_async_copy(near_ref.at[here], out_ref.at[here], sems.at[len(stores)])
+        )
+        stores[-1].start()
+    for store in stores:
+        store.wait()
 
 
 def body(node_coords, node_disp, qpoints, qweights, qcount, sec_block, pri_block):
@@ -390,16 +408,20 @@
     def exchange(value):
         return lax.all_to_all(value, AXES, split_axis=0, concat_axis=0, tiled=True)
 
-    plan, request = pl.pallas_call(
-        functools.partial(plan_kernel, devices, cap, blocks),
-        out_shape=(
-            jax.ShapeDtypeStruct((8, segs), jnp.int32),
-            jax.ShapeDtypeStruct((devices, 128), f32),
-        ),
+    request, route = pl.pallas_call(
+        functools.partial(route_kernel, devices, cap, blocks),
+        out_shape=(jax.ShapeDtypeStruct((devices, 128), f32), jax.ShapeDtypeStruct((4, segs), f32)),
         in_specs=[vmem, vmem],
         out_specs=(vmem, vmem),
         compiler_params=limit,
     )(far(sec_block.reshape(1, segs)), far(pri_block.reshape(1, segs)))
+    plan = pl.pallas_call(
+        functools.partial(order_kernel, cap),
+        out_shape=jax.ShapeDtypeStruct((8, segs), jnp.int32),
+        in_specs=[vmem],
+        out_specs=vmem,
+        compiler_params=limit,
+    )(route)
     xc = jnp.transpose(node_coords, (1, 0, 2)).reshape(3 * blocks, nodes)
     xu = jnp.transpose(node_disp, (1, 0, 2)).reshape(3 * blocks, nodes)
     hbm = pl.BlockSpec(memory_space=pltpu.HBM)
@@ -479,7 +501,11 @@
         functools.partial(assemble_kernel, cap, blocks),
         out_shape=jax.ShapeDtypeStruct((3 * blocks, nodes), f32),
         in_specs=[vmem, vmem],
-        out_specs=vmem,
+        out_specs=hbm,
+        scratch_shapes=[
+            pltpu.VMEM((3 * blocks, nodes), f32),
+            pltpu.SemaphoreType.DMA((2,)),
+        ],
         compiler_params=limit,
     )(turned, near(incoming))
     return jnp.transpose(gap.reshape(3, blocks, nodes), (1, 0, 2))

time: 122 us -> 123 us (level)
    unnamed x12 -> x14, local copies, waits for them, and re-layouts: 3.12 us -> 3.12 us
  transfers between devices with their start and end apart: 3 -> 3, of which waited for: 3 -> 3; matrix products, arithmetic and copies ran while one was open for 0% -> 0% of each run, Pallas kernels for 17% -> 18%
where the time goes in v9:
time: 123 us; the launch traced here: 122 us
  Pallas kernels  38 us (31%)
  waiting for transfers between devices  34.1 us (28%)
  blocking collectives  25.6 us (21%)
  starting transfers between devices  21.4 us (17%)
  local copies, waits for them, and re-layouts  3.12 us (3%)
    all_to_all x3, waiting for transfers between devices, exchange(): return lax.all_to_all(value, AXES, split_axis=0, concat_axis=0, tiled=True)  34.1 us
    all_to_all x1, blocking collectives, exchange(): return lax.all_to_all(value, AXES, split_axis=0, concat_axis=0, tiled=True)  25.6 us
    all_to_all x3, starting transfers between devices, exchange(): return lax.all_to_all(value, AXES, split_axis=0, concat_axis=0, tiled=True)  21.4 us
    pallas_call x1, Pallas kernels, body(): pl.pallas_call(functools.partial(early_kernel, cap), out_shape=(pltpu.HBM...  16.7 us
    pallas_call x1, Pallas kernels, body(): pl.pallas_call(functools.partial(late_kernel, cap), out_shape=pltpu.VMEM(...  10.4 us
    pallas_call x2, Pallas kernels, gather(): pl.pallas_call(functools.partial(gather_kernel, devices, cap, first), out...  5.1 us
    unnamed x14, local copies, waits for them, and re-layouts  3.12 us
  transfers between devices with their start and end apart: 3, of which 3 were waited for; matrix products, arithmetic and copies ran while one was open for 0% of the time, Pallas kernels for 18%

profile of v9, /device:TPU:1, one launch (start us, length us, event | category | flops | bytes accessed | tf_op | source)
XLA Modules:
  0.0 122.4 jit_solution(1284928779837073936)
XLA Ops:
  0.0 2.0 %shard_map.73 = (f32[128,128]{1,0:T(8,128)}, f32[4,256]{1,0:T(4,128)S(1)}) custom-call(s32[1,256]{1,0:T(1,128)} %bitcast.32, s32[1,256]{1,0:T(1,128)} %bitcast.33), custom_call_target="tpu_custom_call" | custom-call | tf_op jit(solution)/shard_map/pallas_call | solution.py:411
  2.0 11.5 %all-to-all-start = ((f32[128,1,128]{2,1,0:T(1,128)}), f32[128,1,128]{2,1,0:T(1,128)S(1)}, u32[]{:S(2)}, u32[]{:S(2)}) async-start(f32[128,1,128]{2,1,0:T(1,128)} %bitcast.3), calls=%async_computation | async-start | bytes 131072 | tf_op jit(solution)/shard_map/all_to_all | solution.py:409
  13.5 1.5 %shard_map.74.table_ref = f32[3072,128]{1,0:T(8,128)S(1)} custom-call(f32[1152,128]{1,0:T(8,128)} %bitcast.30, f32[1152,128]{1,0:T(8,128)} %bitcast.31), custom_call_target="tpu_custom_call" | custom-call | tf_op jit(solution)/shard_map/pallas_call | solution.py:428
  14.9 8.3 %all-to-all-done = f32[128,1,128]{2,1,0:T(1,128)S(1)} async-done(((f32[128,1,128]{2,1,0:T(1,128)}), f32[128,1,128]{2,1,0:T(1,128)S(1)}, u32[]{:S(2)}, u32[]{:S(2)}) %all-to-all-start) | async-done | bytes 65568 | tf_op jit(solution)/shard_map/all_to_all | solution.py:409
  23.3 2.4 %shard_map.75 = (f32[3840,128]{1,0:T(8,128)}, s32[8,128]{1,0:T(8,128)S(1)}) custom-call(f32[128,128]{1,0:T(8,128)S(1)} %bitcast.26, f32[3072,128]{1,0:T(8,128)S(1)} %shard_map.74.table_ref), custom_call_target="tpu_custom_call" | custom-call | tf_op jit(solution)/shard_map/pallas_call | solution.py:438
  25.7 0.0 copy-done.3
  25.7 4.2 %all-to-all-start.2 = ((f32[128,15,2,128]{3,2,1,0:T(2,128)}), f32[128,15,2,128]{3,2,1,0:T(2,128)S(1)}, u32[]{:S(2)}, u32[]{:S(2)}) async-start(f32[128,15,2,128]{3,2,1,0:T(2,128)} %bitcast.28), calls=%async_computation.2 | async-start | bytes 3932160 | tf_op jit(solution)/shard_map/all_to_all | solution.py:409
  29.8 0.0 copy-start.4
  29.8 0.8 copy-done.4
  30.7 2.7 %shard_map.77 = (f32[2304,128]{1,0:T(8,128)}, s32[8,128]{1,0:T(8,128)}) custom-call(f32[128,128]{1,0:T(8,128)S(1)} %bitcast.27, f32[3072,128]{1,0:T(8,128)S(1)} %shard_map.74.table_ref), custom_call_target="tpu_custom_call" | custom-call | tf_op jit(solution)/shard_map/pallas_call | solution.py:438
  33.4 25.0 %all-to-all-done.2 = f32[128,15,2,128]{3,2,1,0:T(2,128)S(1)} async-done(((f32[128,15,2,128]{3,2,1,0:T(2,128)}), f32[128,15,2,128]{3,2,1,0:T(2,128)S(1)}, u32[]{:S(2)}, u32[]{:S(2)}) %all-to-all-start.2) | async-done | bytes 1966112 | tf_op jit(solution)/shard_map/all_to_all | solution.py:409
  58.4 5.7 %all-to-all-start.1 = ((f32[128,9,2,128]{3,2,1,0:T(2,128)}), f32[128,9,2,128]{3,2,1,0:T(2,128)}, u32[]{:S(2)}, u32[]{:S(2)}) async-start(f32[128,9,2,128]{3,2,1,0:T(2,128)} %bitcast.29), calls=%async_computation.1 | async-start | bytes 2359296 | tf_op jit(solution)/shard_map/all_to_all | solution.py:409
  64.2 0.0 copy-start.5
  64.2 0.3 shard_map.76.plan_ref
  64.5 0.0 copy-done
  64.5 0.0 copy-start.2
  64.5 1.1 copy-done.2
  65.7 0.4 shard_map.78.points_ref
  66.1 1.1 copy-done.1
  67.2 16.7 %shard_map.79 = (f32[256,8,256]{2,1,0:T(8,128)}, f32[384,128]{1,0:T(8,128)S(1)}) custom-call(s32[8,256]{1,0:T(8,128)S(1)} %shard_map.76.plan_ref, s32[256]{0:T(256)S(1)} %copy-done.5, f32[3840,128]{1,0:T(8,128)S(1)} %bitcast.22, f32[2,2048,128]{2,1,0:T(8,128)S(1)} %shard_map.78.points_ref, f32[256,256]{1,0:T(8,128)} %refs_0_.1), custom_call_target="tpu_custom_call" | custom-call | tf_op jit(solution)/shard_map/pallas_call | solution.py:480
  83.9 0.7 all-to-all-done.1
  84.7 10.4 %shard_map.80 = f32[1536,128]{1,0:T(8,128)S(1)} custom-call(s32[8,256]{1,0:T(8,128)S(1)} %shard_map.76.plan_ref, s32[256]{0:T(256)S(1)} %copy-done.6, f32[2304,128]{1,0:T(8,128)} %bitcast.10.fetched_ref, f32[2,2048,128]{2,1,0:T(8,128)S(1)} %shard_map.78.points_ref, f32[256,256]{1,0:T(8,128)} %refs_0_.1, f32[256,8,256]{2,1,0:T(8,128)} %get-tuple-element.17.refs_1_, ...), custom_call_target="tpu_custom_call" | custom-call | tf_op jit(solution)/shard_map/pallas_call | solution.py:491
  95.1 25.6 %all_to_all.20 = f32[128,3,4,128]{3,2,1,0:T(4,128)S(1)} all-to-all(f32[128,3,4,128]{3,2,1,0:T(4,128)S(1)} %bitcast.24), channel_id=1, replica_groups=mesh['gx'=8,'gy'=16] {'gx','gy'}, dimensions={0} | all-to-all | bytes 1572864 | tf_op jit(solution)/shard_map/all_to_all | solution.py:409
  120.7 1.6 %shard_map.81 = f32[1152,128]{1,0:T(8,128)} custom-call(s32[8,128]{1,0:T(8,128)S(1)} %get-tuple-element.13.ids_ref, f32[1536,128]{1,0:T(8,128)S(1)} %bitcast.23), custom_call_target="tpu_custom_call" | custom-call | tf_op jit(solution)/shard_map/pallas_call | solution.py:500
  (6 shorter events, 0.0 us)
Async XLA Ops:
  2.0 21.3 %all-to-all-start = ((f32[128,1,128]{2,1,0:T(1,128)}), f32[128,1,128]{2,1,0:T(1,128)S(1)}, u32[]{:S(2)}, u32[]{:S(2)}) async-start(f32[128,1,128]{2,1,0:T(1,128)} %bitcast.3), calls=%async_computation | async-start | bytes 131072 | tf_op jit(solution)/shard_map/all_to_all | solution.py:409
  23.3 2.4 %copy-start.3 = (f32[128,1,128]{2,1,0:T(1,128)}, f32[128,1,128]{2,1,0:T(1,128)S(1)}, u32[]{:S(2)}) copy-start(f32[128,1,128]{2,1,0:T(1,128)S(1)} %all-to-all-done) | copy-start | bytes 196612
  25.7 32.7 %all-to-all-start.2 = ((f32[128,15,2,128]{3,2,1,0:T(2,128)}), f32[128,15,2,128]{3,2,1,0:T(2,128)S(1)}, u32[]{:S(2)}, u32[]{:S(2)}) async-start(f32[128,15,2,128]{3,2,1,0:T(2,128)} %bitcast.28), calls=%async_computation.2 | async-start | bytes 3932160 | tf_op jit(solution)/shard_map/all_to_all | solution.py:409
  29.8 0.8 copy-start.4
  58.4 6.1 %copy-start = (f32[128,15,2,128]{3,2,1,0:T(2,128)}, f32[128,15,2,128]{3,2,1,0:T(2,128)S(1)}, u32[]{:S(2)}) copy-start(f32[128,15,2,128]{3,2,1,0:T(2,128)S(1)} %all-to-all-done.2) | copy-start | bytes 5898244
  58.4 26.3 %all-to-all-start.1 = ((f32[128,9,2,128]{3,2,1,0:T(2,128)}), f32[128,9,2,128]{3,2,1,0:T(2,128)}, u32[]{:S(2)}, u32[]{:S(2)}) async-start(f32[128,9,2,128]{3,2,1,0:T(2,128)} %bitcast.29), calls=%async_computation.1 | async-start | bytes 2359296 | tf_op jit(solution)/shard_map/all_to_all | solution.py:409
  64.2 1.9 %copy-start.5 = (s32[256]{0:T(256)S(1)}, s32[256]{0:T(256)}, u32[]{:S(2)}) copy-start(s32[256]{0:T(256)} %count_ref.3) | copy-start | bytes 3076
  64.5 1.1 copy-start.2
  65.7 1.5 %copy-start.1 = (f32[128,15,2,128]{3,2,1,0:T(2,128)S(1)}, f32[128,15,2,128]{3,2,1,0:T(2,128)}, u32[]{:S(2)}) copy-start(f32[128,15,2,128]{3,2,1,0:T(2,128)} %copy-done) | copy-start | bytes 5898244
  67.2 17.5 %copy-start.6 = (s32[256]{0:T(256)S(1)}, s32[256]{0:T(256)}, u32[]{:S(2)}) copy-start(s32[256]{0:T(256)} %count_ref.3) | copy-start | bytes 3076

commit v10 on v9

--- a/solution.py
+++ b/solution.py
@@ -161,7 +161,7 @@
     extended = jnp.where(row == 3, square, jnp.where(row == 4, 1.0, -4.0 * coord))
     a, b, c = pieces(extended)
     stacked = jnp.concatenate([a, a, b, b, a, c], axis=0)
-    disp = jnp.where(row < 3, 0.0, jnp.where(row == 6, 1.0, raw))
+    disp = jnp.where(row == 0, 1.0, jnp.where(row < 5, 0.0, pltpu.roll(raw, 2, 0)))
     high = disp.astype(jnp.bfloat16).astype(jnp.float32)
     lhs = jnp.concatenate([high, disp - high], axis=0)
     lhs = jnp.concatenate([lhs, lhs], axis=1).astype(jnp.bfloat16)
@@ -198,7 +198,7 @@
 
 
 def primary_pass(capacity, follow, refs):
-    plan_ref, fetched_ref, points_ref, other_ref, both_ref, lhs_ref = refs
+    plan_ref, fetched_ref, points_ref, filled_ref, both_ref, lhs_ref = refs
     segs = plan_ref.shape[1]
 
     def first(s, i):
@@ -206,7 +206,9 @@
 
     def second(s, i):
         sums = sums_of(both_ref, lhs_ref, i)
-        other_ref[s] = sums * (1.0 / sums[6:7])
+        value = sums * (1.0 / sums[0:1])
+        for h in range(filled_ref.shape[0]):
+            filled_ref[h, pl.ds(s * 8 + 5, 3), :] = value[5:8, h * 128 : (h + 1) * 128]
 
     for i in range(WIDE):
         first(i, i)
@@ -234,7 +236,7 @@
 
 
 def secondary_pass(step, apart, base_row, low, end, sets, refs):
-    plan_ref, count_ref, fetched_ref, points_ref, weights_ref, other_ref = refs[:6]
+    plan_ref, count_ref, fetched_ref, points_ref, weights_ref, filled_ref = refs[:6]
     out_ref, both_ref, lhs_ref, left_ref = refs[6:]
 
     def entry(row, place):
@@ -247,11 +249,11 @@
     def second(place, i):
         s = entry(1, place)
         sums = sums_of(both_ref, lhs_ref, i)
-        inverse = 1.0 / sums[6:7]
+        inverse = 1.0 / sums[0:1]
         weights = weights_ref[pl.ds(s, 1), :]
         position = lax.broadcasted_iota(jnp.int32, weights.shape, 1)
         weights = jnp.where(position < count_ref[s], weights, 0.0)
-        gap = (weights * inverse) * (sums * inverse - other_ref[s])
+        gap = (weights * inverse) * (sums * inverse - points_of(filled_ref, s))
         high = gap.astype(jnp.bfloat16).astype(jnp.float32)
         left_ref[i] = jnp.concatenate([high, gap - high], axis=0).astype(jnp.bfloat16)
 
@@ -266,7 +268,7 @@
             result = dot_last(both, left)
             result = (result[:half] + result[half:]).T
             result = result[:8] + result[8:]
-        out_ref[pl.ds(entry(base_row, place), 3, stride=apart), :] = result[3:6]
+        out_ref[pl.ds(entry(base_row, place), 3, stride=apart), :] = result[5:8]
 
     def begin(i):
         if i < 2 * sets:
@@ -298,12 +300,10 @@
     return begin, finish
 
 
-def early_kernel(capacity, plan_ref, count_ref, fetched_ref, points_ref, far_weights_ref, *refs):
-    far_other_ref, out_ref, both_ref, lhs_ref, left_ref, other_ref, weights_ref, sems = refs
-    load = pltpu.make_async_copy(far_weights_ref, weights_ref, sems.at[0])
-    store = pltpu.make_async_copy(other_ref, far_other_ref, sems.at[1])
-    load.start()
+def early_kernel(capacity, plan_ref, count_ref, fetched_ref, points_ref, weights_ref, *refs):
+    filled_ref, out_ref, both_ref, lhs_ref, left_ref = refs
     out_ref[...] = jnp.zeros_like(out_ref)
+    filled_ref[...] = points_ref[...]
     begin, finish = secondary_pass(
         1,
         1,
@@ -311,31 +311,22 @@
         0,
         plan_ref[4, 0],
         EARLY_SETS,
-        (plan_ref, count_ref, fetched_ref, points_ref, weights_ref, other_ref)
+        (plan_ref, count_ref, fetched_ref, points_ref, weights_ref, filled_ref)
         + (out_ref, both_ref, lhs_ref, left_ref),
     )
     primary_pass(
-        capacity, begin, (plan_ref, fetched_ref, points_ref, other_ref, both_ref, lhs_ref)
+        capacity, begin, (plan_ref, fetched_ref, points_ref, filled_ref, both_ref, lhs_ref)
     )
-    store.start()
-    load.wait()
     finish()
-    store.wait()
 
 
 def late_kernel(capacity, plan_ref, count_ref, fetched_ref, points_ref, *refs):
-    far_weights_ref, far_other_ref, before_ref, out_ref = refs[:4]
-    both_ref, lhs_ref, left_ref, other_ref, weights_ref, sems = refs[4:]
-    loads = [
-        pltpu.make_async_copy(far_other_ref, other_ref, sems.at[0]),
-        pltpu.make_async_copy(far_weights_ref, weights_ref, sems.at[1]),
-    ]
-    for load in loads:
-        load.start()
+    far_weights_ref, before_ref, out_ref, both_ref, lhs_ref, left_ref, weights_ref, sem = refs
+    load = pltpu.make_async_copy(far_weights_ref, weights_ref, sem)
+    load.start()
     out_ref[...] = jnp.zeros_like(out_ref)
     for row in range(0, before_ref.shape[0], 8):
         out_ref[pl.ds(row * capacity, 8, stride=capacity), :] = before_ref[row : row + 8, :]
-
     begin, finish = secondary_pass(
         capacity - 1,
         capacity,
@@ -343,13 +334,12 @@
         plan_ref[4, 0],
         plan_ref.shape[1],
         LATE_SETS,
-        (plan_ref, count_ref, fetched_ref, points_ref, weights_ref, other_ref)
+        (plan_ref, count_ref, fetched_ref, points_ref, weights_ref, points_ref)
         + (out_ref, both_ref, lhs_ref, left_ref),
     )
     for i in range(2 * LATE_SETS):
         begin(i)
-    for load in loads:
-        load.wait()
+    load.wait()
     finish()
 
 
@@ -466,36 +456,34 @@
     )(jnp.transpose(qpoints, (1, 0, 2)))
     points = near(points)
 
-    def scratch(count, sems):
+    def scratch(count):
         return [
             pltpu.VMEM((count, 2 * nodes, quad), jnp.bfloat16),
             pltpu.VMEM((count, 16, 2 * nodes), jnp.bfloat16),
             pltpu.VMEM((count, 16, quad), jnp.bfloat16),
-            pltpu.VMEM((segs, 8, quad), f32),
-            pltpu.VMEM((segs, quad), f32),
-            pltpu.SemaphoreType.DMA((sems,)),
         ]
 
-    weights = far(qweights)
-    other, parcels = pl.pallas_call(
+    filled, parcels = pl.pallas_call(
         functools.partial(early_kernel, cap),
         out_shape=(
-            pltpu.HBM((segs, 8, quad), f32),
-            jax.ShapeDtypeStruct((devices * 3, nodes), f32),
+            pltpu.VMEM((quad // 128, segs * 8, 128), f32),
+            pltpu.HBM((devices * 3, nodes), f32),
         ),
-        in_specs=[smem, smem, vmem, vmem, hbm],
-        out_specs=(hbm, vmem),
-        scratch_shapes=scratch(max(2 * WIDE, 3 * EARLY_SETS), 2),
-        compiler_params=limit,
-    )(plan, qcount, in1, points, weights)
+        in_specs=[smem, smem, vmem, vmem, vmem],
+        out_specs=(vmem, vmem),
+        scratch_shapes=scratch(max(2 * WIDE, 3 * EARLY_SETS)),
+        input_output_aliases={3: 0},
+        compiler_params=limit,
+    )(plan, qcount, in1, points, far(qweights))
     parcels = pl.pallas_call(
         functools.partial(late_kernel, cap),
         out_shape=pltpu.VMEM((devices * 3 * cap, nodes), f32),
-        in_specs=[smem, smem, vmem, vmem, hbm, hbm, vmem],
+        in_specs=[smem, smem, vmem, vmem, hbm, vmem],
         out_specs=vmem,
-        scratch_shapes=scratch(3 * LATE_SETS, 2),
-        compiler_params=limit,
-    )(plan, qcount, in2, points, weights, far(other), parcels)
+        scratch_shapes=scratch(3 * LATE_SETS)
+        + [pltpu.VMEM((segs, quad), f32), pltpu.SemaphoreType.DMA],
+        compiler_params=limit,
+    )(plan, qcount, in2, near(filled), far(qweights), far(parcels))
     incoming = exchange(parcels.reshape(devices, 3, cap, nodes)).reshape(-1, nodes)
     gap = pl.pallas_call(
         functools.partial(assemble_kernel, cap, blocks),

time: 123 us -> 159 us (1.29)
  Pallas kernels: 38 us -> 73.1 us
    pallas_call x1, Pallas kernels: 16.7 us -> 52.3 us  [body(): pl.pallas_call(functools.partial(early_kernel, cap), out_shape=(pltpu.VME...]
    unnamed x14 -> x16, local copies, waits for them, and re-layouts: 3.12 us -> 3.72 us
  transfers between devices with their start and end apart: 3 -> 3, of which waited for: 3 -> 2; matrix products, arithmetic and copies ran while one was open for 0% -> 0% of each run, Pallas kernels for 18% -> 36%
where the time goes in v10:
time: 159 us; the launch traced here: 158 us
  Pallas kernels  73.1 us (46%)
  waiting for transfers between devices  33.3 us (21%)
  blocking collectives  26.3 us (17%)
  starting transfers between devices  21.4 us (13%)
  local copies, waits for them, and re-layouts  3.72 us (2%)
    pallas_call x1, Pallas kernels, body(): pl.pallas_call(functools.partial(early_kernel, cap), out_shape=(pltpu.VME...  52.3 us
    all_to_all x3, waiting for transfers between devices, exchange(): return lax.all_to_all(value, AXES, split_axis=0, concat_axis=0, tiled=True)  33.3 us
    all_to_all x1, blocking collectives, exchange(): return lax.all_to_all(value, AXES, split_axis=0, concat_axis=0, tiled=True)  26.3 us
    all_to_all x3, starting transfers between devices, exchange(): return lax.all_to_all(value, AXES, split_axis=0, concat_axis=0, tiled=True)  21.4 us
    pallas_call x1, Pallas kernels, body(): pl.pallas_call(functools.partial(late_kernel, cap), out_shape=pltpu.VMEM(...  9.96 us
    pallas_call x2, Pallas kernels, gather(): pl.pallas_call(functools.partial(gather_kernel, devices, cap, first), out...  5.09 us
    unnamed x16, local copies, waits for them, and re-layouts  3.72 us
  transfers between devices with their start and end apart: 3, of which 2 were waited for; matrix products, arithmetic and copies ran while one was open for 0% of the time, Pallas kernels for 36%

profile of v10, /device:TPU:1, one launch (start us, length us, event | category | flops | bytes accessed | tf_op | source)
XLA Modules:
  0.0 158.2 jit_solution(18049332894326851614)
XLA Ops:
  0.0 2.0 %shard_map.73 = (f32[128,128]{1,0:T(8,128)}, f32[4,256]{1,0:T(4,128)S(1)}) custom-call(s32[1,256]{1,0:T(1,128)} %bitcast.32, s32[1,256]{1,0:T(1,128)} %bitcast.33), custom_call_target="tpu_custom_call" | custom-call | tf_op jit(solution)/shard_map/pallas_call | solution.py:401
  2.0 0.6 copy-done.6
  2.6 11.5 %all-to-all-start = ((f32[128,1,128]{2,1,0:T(1,128)}), f32[128,1,128]{2,1,0:T(1,128)S(1)}, u32[]{:S(2)}, u32[]{:S(2)}) async-start(f32[128,1,128]{2,1,0:T(1,128)} %bitcast.3), calls=%async_computation | async-start | bytes 131072 | tf_op jit(solution)/shard_map/all_to_all | solution.py:399
  14.1 1.5 shard_map.74.table_ref
  15.5 8.3 %all-to-all-done = f32[128,1,128]{2,1,0:T(1,128)S(1)} async-done(((f32[128,1,128]{2,1,0:T(1,128)}), f32[128,1,128]{2,1,0:T(1,128)S(1)}, u32[]{:S(2)}, u32[]{:S(2)}) %all-to-all-start) | async-done | bytes 65568 | tf_op jit(solution)/shard_map/all_to_all | solution.py:399
  23.9 2.4 %shard_map.75 = (f32[3840,128]{1,0:T(8,128)}, s32[8,128]{1,0:T(8,128)S(1)}) custom-call(f32[128,128]{1,0:T(8,128)S(1)} %bitcast.26, f32[3072,128]{1,0:T(8,128)S(1)} %shard_map.74.table_ref), custom_call_target="tpu_custom_call" | custom-call | tf_op jit(solution)/shard_map/pallas_call | solution.py:428
  26.2 0.0 copy-done.3
  26.3 4.2 %all-to-all-start.2 = ((f32[128,15,2,128]{3,2,1,0:T(2,128)}), f32[128,15,2,128]{3,2,1,0:T(2,128)S(1)}, u32[]{:S(2)}, u32[]{:S(2)}) async-start(f32[128,15,2,128]{3,2,1,0:T(2,128)} %bitcast.28), calls=%async_computation.2 | async-start | bytes 3932160 | tf_op jit(solution)/shard_map/all_to_all | solution.py:399
  30.4 0.0 copy-start.4
  30.4 0.8 copy-done.4
  31.3 2.7 %shard_map.77 = (f32[2304,128]{1,0:T(8,128)}, s32[8,128]{1,0:T(8,128)}) custom-call(f32[128,128]{1,0:T(8,128)S(1)} %bitcast.27, f32[3072,128]{1,0:T(8,128)S(1)} %shard_map.74.table_ref), custom_call_target="tpu_custom_call" | custom-call | tf_op jit(solution)/shard_map/pallas_call | solution.py:428
  34.0 25.0 %all-to-all-done.2 = f32[128,15,2,128]{3,2,1,0:T(2,128)S(1)} async-done(((f32[128,15,2,128]{3,2,1,0:T(2,128)}), f32[128,15,2,128]{3,2,1,0:T(2,128)S(1)}, u32[]{:S(2)}, u32[]{:S(2)}) %all-to-all-start.2) | async-done | bytes 1966112 | tf_op jit(solution)/shard_map/all_to_all | solution.py:399
  59.0 5.7 %all-to-all-start.1 = ((f32[128,9,2,128]{3,2,1,0:T(2,128)}), f32[128,9,2,128]{3,2,1,0:T(2,128)}, u32[]{:S(2)}, u32[]{:S(2)}) async-start(f32[128,9,2,128]{3,2,1,0:T(2,128)} %bitcast.29), calls=%async_computation.1 | async-start | bytes 2359296 | tf_op jit(solution)/shard_map/all_to_all | solution.py:399
  64.8 0.0 copy-start.5
  64.8 0.3 shard_map.76.plan_ref
  65.1 0.0 copy-start.2
  65.2 1.1 copy-done.2
  66.3 0.4 shard_map.78.points_ref
  66.7 1.1 copy-done.1
  67.8 52.3 %shard_map.79 = (f32[2,2048,128]{2,1,0:T(8,128)S(1)}, f32[384,128]{1,0:T(8,128)}) custom-call(s32[8,256]{1,0:T(8,128)S(1)} %shard_map.76.plan_ref, s32[256]{0:T(256)S(1)} %copy-done.5, f32[3840,128]{1,0:T(8,128)S(1)} %bitcast.22, f32[2,2048,128]{2,1,0:T(8,128)S(1)} %shard_map.78.points_ref, f32[256,256]{1,0:T(8,128)} %refs_0_.1), custom_call_target="tpu_custom_call", output_to_operand_aliasing={{0}: (3, {})} | custom-call | tf_op jit(solution)/shard_map/pallas_call | solution.py:466
  120.1 0.0 all-to-all-done.1
  120.1 10.0 %shard_map.80 = f32[1536,128]{1,0:T(8,128)S(1)} custom-call(s32[8,256]{1,0:T(8,128)S(1)} %shard_map.76.plan_ref, s32[256]{0:T(256)S(1)} %copy-done.5, f32[2304,128]{1,0:T(8,128)} %bitcast.10.fetched_ref, f32[2,2048,128]{2,1,0:T(8,128)S(1)} %get-tuple-element.17.points_ref, f32[256,256]{1,0:T(8,128)} %refs_0_.1, f32[384,128]{1,0:T(8,128)} %get-tuple-element.18.refs_1_), custom_call_target="tpu_custom_call" | custom-call | tf_op jit(solution)/shard_map/pallas_call | solution.py:478
  130.1 26.3 %all_to_all.20 = f32[128,3,4,128]{3,2,1,0:T(4,128)S(1)} all-to-all(f32[128,3,4,128]{3,2,1,0:T(4,128)S(1)} %bitcast.23), channel_id=1, replica_groups=mesh['gx'=8,'gy'=16] {'gx','gy'}, dimensions={0} | all-to-all | bytes 1572864 | tf_op jit(solution)/shard_map/all_to_all | solution.py:399
  156.4 1.6 %shard_map.81 = f32[1152,128]{1,0:T(8,128)} custom-call(s32[8,128]{1,0:T(8,128)S(1)} %get-tuple-element.13.ids_ref, f32[1536,128]{1,0:T(8,128)S(1)} %bitcast.24), custom_call_target="tpu_custom_call" | custom-call | tf_op jit(solution)/shard_map/pallas_call | solution.py:488
  (8 shorter events, 0.0 us)
Async XLA Ops:
  2.0 0.6 copy-start.6
  2.6 21.3 %all-to-all-start = ((f32[128,1,128]{2,1,0:T(1,128)}), f32[128,1,128]{2,1,0:T(1,128)S(1)}, u32[]{:S(2)}, u32[]{:S(2)}) async-start(f32[128,1,128]{2,1,0:T(1,128)} %bitcast.3), calls=%async_computation | async-start | bytes 131072 | tf_op jit(solution)/shard_map/all_to_all | solution.py:399
  23.9 2.4 %copy-start.3 = (f32[128,1,128]{2,1,0:T(1,128)}, f32[128,1,128]{2,1,0:T(1,128)S(1)}, u32[]{:S(2)}) copy-start(f32[128,1,128]{2,1,0:T(1,128)S(1)} %all-to-all-done) | copy-start | bytes 196612
  26.3 32.7 %all-to-all-start.2 = ((f32[128,15,2,128]{3,2,1,0:T(2,128)}), f32[128,15,2,128]{3,2,1,0:T(2,128)S(1)}, u32[]{:S(2)}, u32[]{:S(2)}) async-start(f32[128,15,2,128]{3,2,1,0:T(2,128)} %bitcast.28), calls=%async_computation.2 | async-start | bytes 3932160 | tf_op jit(solution)/shard_map/all_to_all | solution.py:399
  30.4 0.8 copy-start.4
  34.0 30.8 %copy-start.7 = (f32[4,256]{1,0:T(4,128)S(1)}, f32[4,256]{1,0:T(4,128)}, u32[]{:S(2)}) copy-start(f32[4,256]{1,0:T(4,128)} %copy-done.6) | copy-start | bytes 12292
  59.0 6.1 %copy-start = (f32[128,15,2,128]{3,2,1,0:T(2,128)}, f32[128,15,2,128]{3,2,1,0:T(2,128)S(1)}, u32[]{:S(2)}) copy-start(f32[128,15,2,128]{3,2,1,0:T(2,128)S(1)} %all-to-all-done.2) | copy-start | bytes 5898244
  59.0 61.1 %all-to-all-start.1 = ((f32[128,9,2,128]{3,2,1,0:T(2,128)}), f32[128,9,2,128]{3,2,1,0:T(2,128)}, u32[]{:S(2)}, u32[]{:S(2)}) async-start(f32[128,9,2,128]{3,2,1,0:T(2,128)} %bitcast.29), calls=%async_computation.1 | async-start | bytes 2359296 | tf_op jit(solution)/shard_map/all_to_all | solution.py:399
  64.8 1.9 %copy-start.5 = (s32[256]{0:T(256)S(1)}, s32[256]{0:T(256)}, u32[]{:S(2)}) copy-start(s32[256]{0:T(256)} %count_ref.3) | copy-start | bytes 3076
  65.1 1.1 copy-start.2
  66.3 1.5 copy-start.1

commit v11 on v9

--- a/solution.py
+++ b/solution.py
@@ -25,12 +25,13 @@
     )
 
 
-def route_kernel(devices, capacity, blocks, sec_ref, pri_ref, request_ref, route_ref):
+def plan_kernel(devices, capacity, blocks, sec_ref, pri_ref, plan_ref, request_ref):
     segs = sec_ref.shape[1]
     upper = strict_upper(segs)
     device = lax.broadcasted_iota(jnp.int32, (devices, segs), 0).astype(jnp.float32)
     column = lax.broadcasted_iota(jnp.int32, (request_ref.shape[1], segs), 0).astype(jnp.float32)
     request = jnp.zeros(request_ref.shape, jnp.float32)
+    routes = []
     for side, ref in enumerate((sec_ref, pri_ref)):
         ids = ref[...].astype(jnp.float32)
         owner = jnp.floor((ids + 0.5) * (1.0 / blocks))
@@ -43,16 +44,10 @@
         here = column == rank + side * capacity
         for part in (coarse, local - coarse):
             request += dot_last(narrow, jnp.where(here, 8.0 * part, 0.0).astype(jnp.bfloat16))
-        route_ref[2 * side : 2 * side + 1, :] = owner
-        route_ref[2 * side + 1 : 2 * side + 2, :] = rank
+        routes.append((owner, rank))
     request_ref[...] = request
 
-
-def order_kernel(capacity, route_ref, plan_ref):
-    segs = route_ref.shape[1]
-    upper = strict_upper(segs)
-    sec_owner, sec_rank = route_ref[0:1, :], route_ref[1:2, :]
-    pri_owner, pri_rank = route_ref[2:3, :], route_ref[3:4, :]
+    (sec_owner, sec_rank), (pri_owner, pri_rank) = routes
     early = jnp.where(sec_rank == 0.0, 1.0, 0.0)
     spread = jnp.broadcast_to(early, (16, segs)).astype(jnp.bfloat16)
     ahead = jnp.dot(spread, upper, preferred_element_type=jnp.float32)[:1]
@@ -119,7 +114,7 @@
     part = devices // CHUNKS
     stores = []
     for chunk in range(CHUNKS):
-        lax.fori_loop(chunk * part, (chunk + 1) * part, one_device, 0, unroll=4)
+        lax.fori_loop(chunk * part, (chunk + 1) * part, one_device, 0, unroll=8)
         here = pl.ds(chunk * part * rows, part * rows)
         stores.append(pltpu.make_async_copy(near_ref.at[here], far_ref.at[here], sems.at[chunk]))
         stores[-1].start()
@@ -327,9 +322,14 @@
     far_weights_ref, far_other_ref, before_ref, out_ref = refs[:4]
     both_ref, lhs_ref, left_ref, other_ref, weights_ref, sems = refs[4:]
     loads = [
-        pltpu.make_async_copy(far_other_ref, other_ref, sems.at[0]),
-        pltpu.make_async_copy(far_weights_ref, weights_ref, sems.at[1]),
+        pltpu.make_async_copy(far_weights_ref, weights_ref, sems.at[CHUNKS]),
     ]
+    part = other_ref.shape[0] // CHUNKS
+    for chunk in range(CHUNKS):
+        here = pl.ds(chunk * part, part)
+        loads.append(
+            pltpu.make_async_copy(far_other_ref.at[here], other_ref.at[here], sems.at[chunk])
+        )
     for load in loads:
         load.start()
     out_ref[...] = jnp.zeros_like(out_ref)
@@ -408,20 +408,16 @@
     def exchange(value):
         return lax.all_to_all(value, AXES, split_axis=0, concat_axis=0, tiled=True)
 
-    request, route = pl.pallas_call(
-        functools.partial(route_kernel, devices, cap, blocks),
-        out_shape=(jax.ShapeDtypeStruct((devices, 128), f32), jax.ShapeDtypeStruct((4, segs), f32)),
+    plan, request = pl.pallas_call(
+        functools.partial(plan_kernel, devices, cap, blocks),
+        out_shape=(
+            jax.ShapeDtypeStruct((8, segs), jnp.int32),
+            jax.ShapeDtypeStruct((devices, 128), f32),
+        ),
         in_specs=[vmem, vmem],
         out_specs=(vmem, vmem),
         compiler_params=limit,
     )(far(sec_block.reshape(1, segs)), far(pri_block.reshape(1, segs)))
-    plan = pl.pallas_call(
-        functools.partial(order_kernel, cap),
-        out_shape=jax.ShapeDtypeStruct((8, segs), jnp.int32),
-        in_specs=[vmem],
-        out_specs=vmem,
-        compiler_params=limit,
-    )(route)
     xc = jnp.transpose(node_coords, (1, 0, 2)).reshape(3 * blocks, nodes)
     xu = jnp.transpose(node_disp, (1, 0, 2)).reshape(3 * blocks, nodes)
     hbm = pl.BlockSpec(memory_space=pltpu.HBM)
@@ -493,7 +489,7 @@
         out_shape=pltpu.VMEM((devices * 3 * cap, nodes), f32),
         in_specs=[smem, smem, vmem, vmem, hbm, hbm, vmem],
         out_specs=vmem,
-        scratch_shapes=scratch(3 * LATE_SETS, 2),
+        scratch_shapes=scratch(3 * LATE_SETS, CHUNKS + 1),
         compiler_params=limit,
     )(plan, qcount, in2, points, weights, far(other), parcels)
     incoming = exchange(parcels.reshape(devices, 3, cap, nodes)).reshape(-1, nodes)

time: 123 us -> 122 us (level)
    unnamed x14 -> x12, local copies, waits for them, and re-layouts: 3.12 us -> 3.12 us
  transfers between devices with their start and end apart: 3 -> 3, of which waited for: 3 -> 3; matrix products, arithmetic and copies ran while one was open for 0% -> 0% of each run, Pallas kernels for 18% -> 17%
where the time goes in v11:
time: 122 us
  Pallas kernels  37.4 us (31%)
  waiting for transfers between devices  34.5 us (28%)
  blocking collectives  25.2 us (21%)
  starting transfers between devices  21.4 us (18%)
  local copies, waits for them, and re-layouts  3.12 us (3%)
    all_to_all x3, waiting for transfers between devices, exchange(): return lax.all_to_all(value, AXES, split_axis=0, concat_axis=0, tiled=True)  34.5 us
    all_to_all x1, blocking collectives, exchange(): return lax.all_to_all(value, AXES, split_axis=0, concat_axis=0, tiled=True)  25.2 us
    all_to_all x3, starting transfers between devices, exchange(): return lax.all_to_all(value, AXES, split_axis=0, concat_axis=0, tiled=True)  21.4 us
    pallas_call x1, Pallas kernels, body(): pl.pallas_call(functools.partial(early_kernel, cap), out_shape=(pltpu.HBM...  16.7 us
    pallas_call x1, Pallas kernels, body(): pl.pallas_call(functools.partial(late_kernel, cap), out_shape=pltpu.VMEM(...  10.5 us
    pallas_call x2, Pallas kernels, gather(): pl.pallas_call(functools.partial(gather_kernel, devices, cap, first), out...  4.96 us
    unnamed x12, local copies, waits for them, and re-layouts  3.12 us
  transfers between devices with their start and end apart: 3, of which 3 were waited for; matrix products, arithmetic and copies ran while one was open for 0% of the time, Pallas kernels for 17%

profile of v11, /device:TPU:1, one launch (start us, length us, event | category | flops | bytes accessed | tf_op | source)
XLA Modules:
  0.0 121.8 jit_solution(3186293070838131613)
XLA Ops:
  0.0 1.8 %shard_map.73 = (s32[8,256]{1,0:T(8,128)S(1)}, f32[128,128]{1,0:T(8,128)}) custom-call(s32[1,256]{1,0:T(1,128)} %bitcast.32, s32[1,256]{1,0:T(1,128)} %bitcast.33), custom_call_target="tpu_custom_call" | custom-call | tf_op jit(solution)/shard_map/pallas_call | solution.py:411
  1.8 11.5 %all-to-all-start = ((f32[128,1,128]{2,1,0:T(1,128)}), f32[128,1,128]{2,1,0:T(1,128)S(1)}, u32[]{:S(2)}, u32[]{:S(2)}) async-start(f32[128,1,128]{2,1,0:T(1,128)} %bitcast.3), calls=%async_computation | async-start | bytes 131072 | tf_op jit(solution)/shard_map/all_to_all | solution.py:409
  13.3 1.5 %shard_map.74.table_ref = f32[3072,128]{1,0:T(8,128)S(1)} custom-call(f32[1152,128]{1,0:T(8,128)} %bitcast.30, f32[1152,128]{1,0:T(8,128)} %bitcast.31), custom_call_target="tpu_custom_call" | custom-call | tf_op jit(solution)/shard_map/pallas_call | solution.py:424
  14.8 8.3 %all-to-all-done = f32[128,1,128]{2,1,0:T(1,128)S(1)} async-done(((f32[128,1,128]{2,1,0:T(1,128)}), f32[128,1,128]{2,1,0:T(1,128)S(1)}, u32[]{:S(2)}, u32[]{:S(2)}) %all-to-all-start) | async-done | bytes 65568 | tf_op jit(solution)/shard_map/all_to_all | solution.py:409
  23.1 2.3 %shard_map.75 = (f32[3840,128]{1,0:T(8,128)}, s32[8,128]{1,0:T(8,128)S(1)}) custom-call(f32[128,128]{1,0:T(8,128)S(1)} %bitcast.26, f32[3072,128]{1,0:T(8,128)S(1)} %shard_map.74.table_ref), custom_call_target="tpu_custom_call" | custom-call | tf_op jit(solution)/shard_map/pallas_call | solution.py:434
  25.4 0.0 copy-done.3
  25.4 4.2 %all-to-all-start.2 = ((f32[128,15,2,128]{3,2,1,0:T(2,128)}), f32[128,15,2,128]{3,2,1,0:T(2,128)S(1)}, u32[]{:S(2)}, u32[]{:S(2)}) async-start(f32[128,15,2,128]{3,2,1,0:T(2,128)} %bitcast.28), calls=%async_computation.2 | async-start | bytes 3932160 | tf_op jit(solution)/shard_map/all_to_all | solution.py:409
  29.6 0.0 copy-start.4
  29.6 0.8 copy-done.4
  30.4 2.6 %shard_map.76 = (f32[2304,128]{1,0:T(8,128)}, s32[8,128]{1,0:T(8,128)}) custom-call(f32[128,128]{1,0:T(8,128)S(1)} %bitcast.27, f32[3072,128]{1,0:T(8,128)S(1)} %shard_map.74.table_ref), custom_call_target="tpu_custom_call" | custom-call | tf_op jit(solution)/shard_map/pallas_call | solution.py:434
  33.1 25.1 %all-to-all-done.2 = f32[128,15,2,128]{3,2,1,0:T(2,128)S(1)} async-done(((f32[128,15,2,128]{3,2,1,0:T(2,128)}), f32[128,15,2,128]{3,2,1,0:T(2,128)S(1)}, u32[]{:S(2)}, u32[]{:S(2)}) %all-to-all-start.2) | async-done | bytes 1966112 | tf_op jit(solution)/shard_map/all_to_all | solution.py:409
  58.2 5.7 %all-to-all-start.1 = ((f32[128,9,2,128]{3,2,1,0:T(2,128)}), f32[128,9,2,128]{3,2,1,0:T(2,128)}, u32[]{:S(2)}, u32[]{:S(2)}) async-start(f32[128,9,2,128]{3,2,1,0:T(2,128)} %bitcast.29), calls=%async_computation.1 | async-start | bytes 2359296 | tf_op jit(solution)/shard_map/all_to_all | solution.py:409
  63.9 0.0 copy-done
  63.9 0.0 copy-start.5
  63.9 0.0 copy-start.2
  64.0 1.1 copy-done.2
  65.1 0.4 shard_map.77.points_ref
  65.5 0.0 copy-done.5
  65.5 1.1 copy-done.1
  66.6 16.7 %shard_map.78 = (f32[256,8,256]{2,1,0:T(8,128)}, f32[384,128]{1,0:T(8,128)S(1)}) custom-call(s32[8,256]{1,0:T(8,128)S(1)} %get-tuple-element.14.plan_ref, s32[256]{0:T(256)S(1)} %copy-done.5, f32[3840,128]{1,0:T(8,128)S(1)} %bitcast.22, f32[2,2048,128]{2,1,0:T(8,128)S(1)} %shard_map.77.points_ref, f32[256,256]{1,0:T(8,128)} %refs_0_.1), custom_call_target="tpu_custom_call" | custom-call | tf_op jit(solution)/shard_map/pallas_call | solution.py:476
  83.3 1.1 all-to-all-done.1
  84.4 10.5 %shard_map.79 = f32[1536,128]{1,0:T(8,128)S(1)} custom-call(s32[8,256]{1,0:T(8,128)S(1)} %get-tuple-element.14.plan_ref, s32[256]{0:T(256)S(1)} %copy-done.5, f32[2304,128]{1,0:T(8,128)} %bitcast.10.fetched_ref, f32[2,2048,128]{2,1,0:T(8,128)S(1)} %shard_map.77.points_ref, f32[256,256]{1,0:T(8,128)} %refs_0_.1, f32[256,8,256]{2,1,0:T(8,128)} %get-tuple-element.17.refs_1_, ...), custom_call_target="tpu_custom_call" | custom-call | tf_op jit(solution)/shard_map/pallas_call | solution.py:487
  94.9 25.2 %all_to_all.20 = f32[128,3,4,128]{3,2,1,0:T(4,128)S(1)} all-to-all(f32[128,3,4,128]{3,2,1,0:T(4,128)S(1)} %bitcast.24), channel_id=1, replica_groups=mesh['gx'=8,'gy'=16] {'gx','gy'}, dimensions={0} | all-to-all | bytes 1572864 | tf_op jit(solution)/shard_map/all_to_all | solution.py:409
  120.2 1.6 %shard_map.80 = f32[1152,128]{1,0:T(8,128)} custom-call(s32[8,128]{1,0:T(8,128)S(1)} %get-tuple-element.13.ids_ref, f32[1536,128]{1,0:T(8,128)S(1)} %bitcast.23), custom_call_target="tpu_custom_call" | custom-call | tf_op jit(solution)/shard_map/pallas_call | solution.py:496
  (3 shorter events, 0.0 us)
Async XLA Ops:
  1.8 21.3 %all-to-all-start = ((f32[128,1,128]{2,1,0:T(1,128)}), f32[128,1,128]{2,1,0:T(1,128)S(1)}, u32[]{:S(2)}, u32[]{:S(2)}) async-start(f32[128,1,128]{2,1,0:T(1,128)} %bitcast.3), calls=%async_computation | async-start | bytes 131072 | tf_op jit(solution)/shard_map/all_to_all | solution.py:409
  23.1 2.3 %copy-start.3 = (f32[128,1,128]{2,1,0:T(1,128)}, f32[128,1,128]{2,1,0:T(1,128)S(1)}, u32[]{:S(2)}) copy-start(f32[128,1,128]{2,1,0:T(1,128)S(1)} %all-to-all-done) | copy-start | bytes 196612
  25.4 32.7 %all-to-all-start.2 = ((f32[128,15,2,128]{3,2,1,0:T(2,128)}), f32[128,15,2,128]{3,2,1,0:T(2,128)S(1)}, u32[]{:S(2)}, u32[]{:S(2)}) async-start(f32[128,15,2,128]{3,2,1,0:T(2,128)} %bitcast.28), calls=%async_computation.2 | async-start | bytes 3932160 | tf_op jit(solution)/shard_map/all_to_all | solution.py:409
  29.6 0.8 copy-start.4
  58.2 5.7 %copy-start = (f32[128,15,2,128]{3,2,1,0:T(2,128)}, f32[128,15,2,128]{3,2,1,0:T(2,128)S(1)}, u32[]{:S(2)}) copy-start(f32[128,15,2,128]{3,2,1,0:T(2,128)S(1)} %all-to-all-done.2) | copy-start | bytes 5898244
  58.2 26.3 %all-to-all-start.1 = ((f32[128,9,2,128]{3,2,1,0:T(2,128)}), f32[128,9,2,128]{3,2,1,0:T(2,128)}, u32[]{:S(2)}, u32[]{:S(2)}) async-start(f32[128,9,2,128]{3,2,1,0:T(2,128)} %bitcast.29), calls=%async_computation.1 | async-start | bytes 2359296 | tf_op jit(solution)/shard_map/all_to_all | solution.py:409
  63.9 1.5 %copy-start.5 = (s32[256]{0:T(256)S(1)}, s32[256]{0:T(256)}, u32[]{:S(2)}) copy-start(s32[256]{0:T(256)} %count_ref.3) | copy-start | bytes 3076
  63.9 1.1 copy-start.2
  65.1 1.5 %copy-start.1 = (f32[128,15,2,128]{3,2,1,0:T(2,128)S(1)}, f32[128,15,2,128]{3,2,1,0:T(2,128)}, u32[]{:S(2)}) copy-start(f32[128,15,2,128]{3,2,1,0:T(2,128)} %copy-done) | copy-start | bytes 5898244
